TPU v7x, 32 devices: a whole 2x2x4 slice. The times are simulated.
32 devices in a mesh: fsdp: 16 (over z, x, core), rep: 2 (over y).
Axes of the slice: x: 2, y: 2, z: 4, core: 2. Of those that a mesh axis runs over, the one named last changes fastest.
Arguments:
- tokens: bfloat16 [37632, 256], P(('fsdp', 'rep')), may hold values from -6 to 6
- heights: int32 [32], P(('fsdp', 'rep')), may hold values from 7 to 28, as said below
- widths: int32 [32], P(('fsdp', 'rep')), may hold values from 7 to 42, as said below
- w_qkv: bfloat16 [2, 256, 768], P(None, 'fsdp'), may hold values from -0.375 to 0.375
- w_proj: bfloat16 [2, 256, 256], P(None, 'fsdp'), may hold values from -0.75 to 0.75
- w_fc1: bfloat16 [2, 256, 1024], P(None, 'fsdp'), may hold values from -0.375 to 0.375
- w_fc2: bfloat16 [2, 1024, 256], P(None, 'fsdp'), may hold values from -0.1875 to 0.1875
- vectors: bfloat16 [2, 22, 256], P(None, None, 'fsdp'), may hold values from -0.9 to 1.3
- cotangent: bfloat16 [37632, 256], P(('fsdp', 'rep')), may hold values from -6 to 6, as said below
Outputs:
- outputs: float32 [37632, 256], P(('fsdp', 'rep'))
- grad_tokens: float32 [37632, 256], P(('fsdp', 'rep'))
- grad_w_qkv: float32 [2, 256, 768], P(None, 'fsdp')
- grad_w_proj: float32 [2, 256, 256], P(None, 'fsdp')
- grad_w_fc1: float32 [2, 256, 1024], P(None, 'fsdp')
- grad_w_fc2: float32 [2, 1024, 256], P(None, 'fsdp')
- grad_vectors: float32 [2, 22, 256], P(None, None, 'fsdp')
Inputs may be any that keep to these rules, and one draw needn't show every extreme that they name: `heights`: multiples of 7; the first image's height is 28. `widths`: multiples of 7; the first image's width is 42. `cotangent`: zero on cells that are not live.
All inputs are finite; a program needn't handle non-finite values.
Results may differ from a plain program's by a relative error of at most 0.018.
Values may be sent and summed in bfloat16 or wider, within the bound.
A program may use at most 192 MiB of HBM per device.

v0:
```python
from functools import partial

import jax
import jax.numpy as jnp
from jax import lax
from jax.sharding import PartitionSpec as P

HEAD = 32
STRIPE = 7
HP = 28
WP = 42


eps_norm = 1e-05
masked_score = -1000000000.0


def layer_norm(values, gain, shift):
    centre = jnp.mean(values, axis=-1, keepdims=True)
    centred = values - centre
    spread = jnp.mean(centred * centred, axis=-1, keepdims=True)
    return centred * lax.rsqrt(spread + eps_norm) * gain + shift


def position_term(values, taps, shift):
    image_count, height, breadth, channels = values.shape
    half_dim = channels // 2
    rows_part = values[..., :half_dim].reshape(
        image_count, height // STRIPE, STRIPE, breadth, half_dim
    )
    padded = jnp.pad(rows_part, ((0, 0), (0, 0), (1, 1), (1, 1), (0, 0)))
    total_rows = jnp.zeros_like(rows_part)
    for tap_index in range(9):
        offset_row, offset_col = (tap_index // 3, tap_index % 3)
        total_rows = (
            total_rows
            + padded[:, :, offset_row : offset_row + STRIPE, offset_col : offset_col + breadth, :]
            * taps[tap_index, :half_dim]
        )
    cols_part = values[..., half_dim:].reshape(
        image_count, height, breadth // STRIPE, STRIPE, half_dim
    )
    padded = jnp.pad(cols_part, ((0, 0), (1, 1), (0, 0), (1, 1), (0, 0)))
    total_cols = jnp.zeros_like(cols_part)
    for tap_index in range(9):
        offset_row, offset_col = (tap_index // 3, tap_index % 3)
        total_cols = (
            total_cols
            + padded[:, offset_row : offset_row + height, :, offset_col : offset_col + STRIPE, :]
            * taps[tap_index, half_dim:]
        )
    joined = jnp.concatenate(
        [
            total_rows.reshape(image_count, height, breadth, half_dim),
            total_cols.reshape(image_count, height, breadth, half_dim),
        ],
        axis=-1,
    )
    return joined + shift


def to_rows(tensor):
    image_count, height, breadth, channels = tensor.shape
    return tensor.reshape(image_count, height // STRIPE, STRIPE * breadth, channels)


def from_rows(tensor, height, breadth):
    return tensor.reshape(tensor.shape[0], height, breadth, tensor.shape[-1])


def to_columns(tensor):
    image_count, height, breadth, channels = tensor.shape
    split = tensor.reshape(image_count, height, breadth // STRIPE, STRIPE, channels)
    return split.transpose(0, 2, 1, 3, 4).reshape(
        image_count, breadth // STRIPE, height * STRIPE, channels
    )


def from_columns(tensor, height, breadth):
    image_count, stripes, length, channels = tensor.shape
    split = tensor.reshape(image_count, stripes, height, STRIPE, channels)
    return split.transpose(0, 2, 1, 3, 4).reshape(image_count, height, breadth, channels)


def stripe_scores(queries, keys_in, live):
    stripes, length, channels = queries.shape
    shape_four = (stripes, length, channels // HEAD, HEAD)
    query_heads = queries.reshape(shape_four)
    key_heads = keys_in.reshape(shape_four)
    scores = jnp.einsum(
        "sqhd,skhd->shqk", query_heads, key_heads, preferred_element_type=jnp.float32
    ) * HEAD ** (-0.5)
    return (scores + jnp.where(live[:, None, None, :], 0.0, masked_score), query_heads, key_heads)


def attend_one(image_parts):
    queries, keys_in, values, live = image_parts
    stripes, length, channels = queries.shape
    scores, query_heads, key_heads = stripe_scores(queries, keys_in, live)
    row_max = jnp.max(scores, axis=-1, keepdims=True)
    expo = jnp.exp(scores - row_max)
    row_total = jnp.sum(expo, axis=-1, keepdims=True)
    probs_low = (expo / row_total).astype(jnp.bfloat16)
    value_heads = values.reshape(stripes, length, channels // HEAD, HEAD)
    mixed = jnp.einsum(
        "shqk,skhd->sqhd", probs_low, value_heads, preferred_element_type=jnp.float32
    )
    return (mixed.reshape(stripes, length, channels), (row_max + jnp.log(row_total))[..., 0])


def attend_back_one(image_parts):
    queries, keys_in, values, live, log_total, grad_out = image_parts
    stripes, length, channels = queries.shape
    shape_four = (stripes, length, channels // HEAD, HEAD)
    scores, query_heads, key_heads = stripe_scores(queries, keys_in, live)
    probs = jnp.exp(scores - log_total[..., None])
    probs_low = probs.astype(jnp.bfloat16)
    value_heads = values.reshape(shape_four)
    grad_heads = grad_out.reshape(shape_four)
    grad_values = jnp.einsum(
        "shqk,sqhd->skhd", probs_low, grad_heads, preferred_element_type=jnp.float32
    )
    grad_probs = jnp.einsum(
        "sqhd,skhd->shqk", grad_heads, value_heads, preferred_element_type=jnp.float32
    )
    inner = jnp.sum(probs * grad_probs, axis=-1, keepdims=True)
    grad_scores = (probs * (grad_probs - inner)).astype(jnp.bfloat16)
    grad_queries = jnp.einsum(
        "shqk,skhd->sqhd", grad_scores, key_heads, preferred_element_type=jnp.float32
    ) * HEAD ** (-0.5)
    grad_keys = jnp.einsum(
        "shqk,sqhd->skhd", grad_scores, query_heads, preferred_element_type=jnp.float32
    ) * HEAD ** (-0.5)
    return (
        grad_queries.reshape(stripes, length, channels),
        grad_keys.reshape(stripes, length, channels),
        grad_values.reshape(stripes, length, channels),
    )


def attention_forward(queries, keys_all, values_all, live):
    half_dim = queries.shape[-1] // 2
    height, breadth = (queries.shape[1], queries.shape[2])
    live_rows = to_rows(live[..., None])[..., 0]
    live_cols = to_columns(live[..., None])[..., 0]
    out_rows, log_rows = lax.map(
        attend_one,
        (
            to_rows(queries[..., :half_dim]),
            to_rows(keys_all[..., :half_dim]),
            to_rows(values_all[..., :half_dim]),
            live_rows,
        ),
    )
    out_cols, log_cols = lax.map(
        attend_one,
        (
            to_columns(queries[..., half_dim:]),
            to_columns(keys_all[..., half_dim:]),
            to_columns(values_all[..., half_dim:]),
            live_cols,
        ),
    )
    joined = jnp.concatenate(
        [from_rows(out_rows, height, breadth), from_columns(out_cols, height, breadth)], axis=-1
    )
    return (joined, log_rows, log_cols)


def attention_back(queries, keys_all, values_all, live, log_rows, log_cols, grad_attn):
    half_dim = queries.shape[-1] // 2
    height, breadth = (queries.shape[1], queries.shape[2])
    live_rows = to_rows(live[..., None])[..., 0]
    live_cols = to_columns(live[..., None])[..., 0]
    rows_grads = lax.map(
        attend_back_one,
        (
            to_rows(queries[..., :half_dim]),
            to_rows(keys_all[..., :half_dim]),
            to_rows(values_all[..., :half_dim]),
            live_rows,
            log_rows,
            to_rows(grad_attn[..., :half_dim]),
        ),
    )
    cols_grads = lax.map(
        attend_back_one,
        (
            to_columns(queries[..., half_dim:]),
            to_columns(keys_all[..., half_dim:]),
            to_columns(values_all[..., half_dim:]),
            live_cols,
            log_cols,
            to_columns(grad_attn[..., half_dim:]),
        ),
    )
    return tuple(
        (
            jnp.concatenate(
                [
                    from_rows(rows_grads[member], height, breadth),
                    from_columns(cols_grads[member], height, breadth),
                ],
                axis=-1,
            )
            for member in range(3)
        )
    )


def run_layer(hidden_in, live, weights):
    w_mix, w_out, w_up, w_down, vec_low = weights
    vec = vec_low.astype(jnp.float32)
    image_count, height, breadth, width_d = hidden_in.shape
    flat_in = hidden_in.reshape(-1, width_d)
    normed_low = layer_norm(flat_in, vec[0], vec[1]).astype(jnp.bfloat16)
    bias_mix = jnp.concatenate([vec[2], jnp.zeros_like(vec[2]), vec[3]])
    mixed_low = (jnp.dot(normed_low, w_mix, preferred_element_type=jnp.float32) + bias_mix).astype(
        jnp.bfloat16
    )
    mixed_low = mixed_low.reshape(image_count, height, breadth, 3 * width_d)
    queries = mixed_low[..., :width_d]
    keys_all = mixed_low[..., width_d : 2 * width_d]
    values_all = mixed_low[..., 2 * width_d :] * live[..., None].astype(jnp.bfloat16)
    attended, log_rows, log_cols = attention_forward(queries, keys_all, values_all, live)
    position = position_term(values_all.astype(jnp.float32), vec[9:18], vec[8])
    attn_low = (attended + position).astype(jnp.bfloat16).reshape(-1, width_d)
    after = flat_in + (jnp.dot(attn_low, w_out, preferred_element_type=jnp.float32) + vec[4])
    normed_two_low = layer_norm(after, vec[5], vec[6]).astype(jnp.bfloat16)
    hidden = jnp.dot(normed_two_low, w_up, preferred_element_type=jnp.float32) + vec[18:].reshape(
        -1
    )
    act_low = jax.nn.gelu(hidden, approximate=False).astype(jnp.bfloat16)
    result = after + (jnp.dot(act_low, w_down, preferred_element_type=jnp.float32) + vec[7])
    saved = (
        flat_in,
        normed_low,
        queries,
        keys_all,
        values_all,
        log_rows,
        log_cols,
        attn_low,
        after,
        normed_two_low,
        hidden,
        act_low,
    )
    return (result, saved)


def layer_back(grad_out, saved, live, weights):
    w_mix, w_out, w_up, w_down, vec_low = weights
    vec = vec_low.astype(jnp.float32)
    (
        flat_in,
        normed_low,
        queries,
        keys_all,
        values_all,
        log_rows,
        log_cols,
        attn_low,
        after,
        normed_two_low,
        hidden,
        act_low,
    ) = saved
    image_count, height, breadth, width_d = queries.shape
    grad_out_bias = jnp.sum(grad_out, axis=0)
    grad_out_low = grad_out.astype(jnp.bfloat16)
    grad_down = jnp.einsum("tf,td->fd", act_low, grad_out_low, preferred_element_type=jnp.float32)
    grad_act = jnp.einsum("td,fd->tf", grad_out_low, w_down, preferred_element_type=jnp.float32)
    grad_hidden = jax.vjp(partial(jax.nn.gelu, approximate=False), hidden)[1](grad_act)[0]
    grad_hidden_bias = jnp.sum(grad_hidden, axis=0)
    grad_hidden_low = grad_hidden.astype(jnp.bfloat16)
    grad_up = jnp.einsum(
        "tc,tf->cf", normed_two_low, grad_hidden_low, preferred_element_type=jnp.float32
    )
    grad_normed_two = jnp.einsum(
        "tf,cf->tc", grad_hidden_low, w_up, preferred_element_type=jnp.float32
    )
    grad_after_norm, grad_gain_two, grad_shift_two = jax.vjp(layer_norm, after, vec[5], vec[6])[1](
        grad_normed_two
    )
    grad_after = grad_out + grad_after_norm
    grad_proj_bias = jnp.sum(grad_after, axis=0)
    grad_after_low = grad_after.astype(jnp.bfloat16)
    grad_outw = jnp.einsum(
        "tc,td->cd", attn_low, grad_after_low, preferred_element_type=jnp.float32
    )
    grad_attn_low = jnp.einsum(
        "td,cd->tc", grad_after_low, w_out, preferred_element_type=jnp.float32
    ).astype(jnp.bfloat16)
    grad_attn_low = grad_attn_low.reshape(image_count, height, breadth, width_d)
    position_pull = jax.vjp(position_term, values_all.astype(jnp.float32), vec[9:18], vec[8])[1]
    grad_values_pos, grad_taps, grad_pos_bias = position_pull(grad_attn_low.astype(jnp.float32))
    grad_queries, grad_keys, grad_values = attention_back(
        queries, keys_all, values_all, live, log_rows, log_cols, grad_attn_low
    )
    grad_values_all = (grad_values + grad_values_pos) * live[..., None].astype(jnp.float32)
    grad_mixed = jnp.concatenate([grad_queries, grad_keys, grad_values_all], axis=-1).reshape(
        -1, 3 * width_d
    )
    grad_query_bias = jnp.sum(grad_mixed[:, :width_d], axis=0)
    grad_value_bias = jnp.sum(grad_mixed[:, 2 * width_d :], axis=0)
    grad_mixed_low = grad_mixed.astype(jnp.bfloat16)
    grad_mix = jnp.einsum(
        "tc,tm->cm", normed_low, grad_mixed_low, preferred_element_type=jnp.float32
    )
    grad_normed = jnp.einsum("tm,cm->tc", grad_mixed_low, w_mix, preferred_element_type=jnp.float32)
    grad_in_norm, grad_gain_one, grad_shift_one = jax.vjp(layer_norm, flat_in, vec[0], vec[1])[1](
        grad_normed
    )
    grad_in = grad_after + grad_in_norm
    first_rows = jnp.stack(
        [
            grad_gain_one,
            grad_shift_one,
            grad_query_bias,
            grad_value_bias,
            grad_proj_bias,
            grad_gain_two,
            grad_shift_two,
            grad_out_bias,
            grad_pos_bias,
        ]
    )
    grad_vec = jnp.concatenate(
        [first_rows, grad_taps, grad_hidden_bias.reshape(-1, width_d)], axis=0
    )
    return (grad_in, (grad_mix, grad_outw, grad_up, grad_down, grad_vec))


def fetch_forward(layer_index, w_qkv, w_proj, w_fc1, w_fc2, vectors):
    return (
        lax.all_gather(w_qkv[layer_index], "fsdp", axis=0, tiled=True),
        lax.all_gather(w_proj[layer_index], "fsdp", axis=0, tiled=True),
        lax.all_gather(w_fc1[layer_index], "fsdp", axis=0, tiled=True),
        lax.all_gather(w_fc2[layer_index], "fsdp", axis=0, tiled=True),
        lax.all_gather(vectors[layer_index], "fsdp", axis=1, tiled=True),
    )


def fetch_backward(layer_index, w_qkv, w_proj, w_fc1, w_fc2, vectors):
    return (
        lax.all_gather(w_qkv[layer_index], "fsdp", axis=0, tiled=True),
        lax.all_gather(w_proj[layer_index], "fsdp", axis=0, tiled=True),
        lax.all_gather(w_fc1[layer_index], "fsdp", axis=0, tiled=True),
        lax.all_gather(w_fc2[layer_index], "fsdp", axis=0, tiled=True),
        lax.all_gather(vectors[layer_index], "fsdp", axis=1, tiled=True),
    )


def reduce_terms(terms):
    grad_mix, grad_outw, grad_up, grad_down, grad_vec = terms
    owned = (
        lax.psum_scatter(
            grad_mix.astype(jnp.bfloat16), "fsdp", scatter_dimension=0, tiled=True
        ).astype(jnp.float32),
        lax.psum_scatter(
            grad_outw.astype(jnp.bfloat16), "fsdp", scatter_dimension=0, tiled=True
        ).astype(jnp.float32),
        lax.psum_scatter(
            grad_up.astype(jnp.bfloat16), "fsdp", scatter_dimension=0, tiled=True
        ).astype(jnp.float32),
        lax.psum_scatter(
            grad_down.astype(jnp.bfloat16), "fsdp", scatter_dimension=0, tiled=True
        ).astype(jnp.float32),
        lax.psum_scatter(
            grad_vec.astype(jnp.bfloat16), "fsdp", scatter_dimension=1, tiled=True
        ).astype(jnp.float32),
    )
    part_mix, part_outw, part_up, part_down, part_vec = owned
    return (
        lax.psum(part_mix.astype(jnp.bfloat16), "rep").astype(jnp.float32),
        lax.psum(part_outw.astype(jnp.bfloat16), "rep").astype(jnp.float32),
        lax.psum(part_up.astype(jnp.bfloat16), "rep").astype(jnp.float32),
        lax.psum(part_down.astype(jnp.bfloat16), "rep").astype(jnp.float32),
        lax.psum(part_vec.astype(jnp.bfloat16), "rep").astype(jnp.float32),
    )


def shards(tokens, heights, widths, w_qkv, w_proj, w_fc1, w_fc2, vectors, cotangent):
    image_count = heights.shape[0]
    width_d = tokens.shape[1]
    row_index = lax.broadcasted_iota(jnp.int32, (image_count, HP, WP), 1)
    col_index = lax.broadcasted_iota(jnp.int32, (image_count, HP, WP), 2)
    live = (row_index < heights[:, None, None]) & (col_index < widths[:, None, None])
    layer_count = w_qkv.shape[0]
    hidden_state = tokens.astype(jnp.float32).reshape(image_count, HP, WP, width_d)
    stored = []
    gathered_all = []
    for layer_index in range(layer_count):
        gathered = fetch_forward(layer_index, w_qkv, w_proj, w_fc1, w_fc2, vectors)
        stored.append(hidden_state)
        gathered_all.append(gathered)
        result, unused = run_layer(hidden_state, live, gathered)
        hidden_state = result.reshape(image_count, HP, WP, width_d)
    final_state = hidden_state.reshape(-1, width_d)
    gradient = cotangent.astype(jnp.float32)
    grad_layers = [None] * layer_count
    for layer_index in reversed(range(layer_count)):
        gathered = fetch_backward(layer_index, w_qkv, w_proj, w_fc1, w_fc2, vectors)
        unused, saved = run_layer(stored[layer_index], live, gathered)
        gradient, terms = layer_back(gradient, saved, live, gathered)
        grad_layers[layer_index] = reduce_terms(terms)
    stacked = [
        jnp.stack([grad_layers[layer_index][member] for layer_index in range(layer_count)])
        for member in range(5)
    ]
    return (final_state, gradient, stacked[0], stacked[1], stacked[2], stacked[3], stacked[4])


def solution(mesh):
    placed = (
        P(("fsdp", "rep"), None),
        P(("fsdp", "rep")),
        P(("fsdp", "rep")),
        P(None, "fsdp", None),
        P(None, "fsdp", None),
        P(None, "fsdp", None),
        P(None, "fsdp", None),
        P(None, None, "fsdp"),
        P(("fsdp", "rep"), None),
    )
    return jax.shard_map(
        shards,
        mesh=mesh,
        in_specs=placed,
        out_specs=(
            P(("fsdp", "rep"), None),
            P(("fsdp", "rep"), None),
            P(None, "fsdp", None),
            P(None, "fsdp", None),
            P(None, "fsdp", None),
            P(None, "fsdp", None),
            P(None, None, "fsdp"),
        ),
        check_vma=False,
    )
```

profile of v0, /device:TPU:0, one launch (start us, length us, event | category | flops | bytes accessed | tf_op | source)
XLA Modules:
  0.0 1225.4 jit_solution(9609000567260567015)
XLA Ops:
  7.9 23.2 %all-gather.5 = bf16[1,22,256]{1,2,0:T(8,128)(2,1)S(1)} all-gather(bf16[1,22,16]{1,2,0:T(8,128)(2,1)S(1)} %get-tuple-element.526), channel_id=7, replica_groups=mesh['fsdp'=16,'rep'=2] {'fsdp'}, dimensions={2}, use_global_device_ids=true | all-gather | bytes 11968 | tf_op jit(solution)/shard_map/all_gather | solution.py:341
  32.0 17.7 %all-gather = bf16[1,22,256]{1,2,0:T(8,128)(2,1)S(1)} all-gather(bf16[1,22,16]{1,2,0:T(8,128)(2,1)S(1)} %get-tuple-element.527), channel_id=2, replica_groups=mesh['fsdp'=16,'rep'=2] {'fsdp'}, dimensions={2}, use_global_device_ids=true | all-gather | bytes 11968 | tf_op jit(solution)/shard_map/all_gather | solution.py:341
  56.3 19.9 %all-gather.1 = bf16[1,256,768]{2,1,0:T(8,128)(2,1)S(1)} all-gather(bf16[1,16,768]{2,1,0:T(8,128)(2,1)S(1)} %get-tuple-element.523), channel_id=3, replica_groups=mesh['fsdp'=16,'rep'=2] {'fsdp'}, dimensions={1}, use_global_device_ids=true | all-gather | bytes 417792 | tf_op jit(solution)/shard_map/all_gather | solution.py:337
  91.6 19.2 %all-gather.2 = bf16[1,256,256]{2,1,0:T(8,128)(2,1)} all-gather(bf16[1,16,256]{2,1,0:T(8,128)(2,1)S(1)} %get-tuple-element.525), channel_id=4, replica_groups=mesh['fsdp'=16,'rep'=2] {'fsdp'}, dimensions={1}, use_global_device_ids=true | all-gather | bytes 139264 | tf_op jit(solution)/shard_map/all_gather | solution.py:338
  112.7 21.2 %all-gather.6 = bf16[1,256,768]{2,1,0:T(8,128)(2,1)} all-gather(bf16[1,16,768]{2,1,0:T(8,128)(2,1)S(1)} %copy-done.148), channel_id=8, replica_groups=mesh['fsdp'=16,'rep'=2] {'fsdp'}, dimensions={1}, use_global_device_ids=true | all-gather | bytes 417792 | tf_op jit(solution)/shard_map/all_gather | solution.py:337
  134.0 20.3 %all-gather.4 = bf16[1,1024,256]{2,1,0:T(8,128)(2,1)} all-gather(bf16[1,64,256]{2,1,0:T(8,128)(2,1)S(1)} %get-tuple-element.515), channel_id=6, replica_groups=mesh['fsdp'=16,'rep'=2] {'fsdp'}, dimensions={1}, use_global_device_ids=true | all-gather | bytes 557056 | tf_op jit(solution)/shard_map/all_gather | solution.py:340
  154.2 22.1 %all-gather.3 = bf16[1,256,1024]{2,1,0:T(8,128)(2,1)} all-gather(bf16[1,16,1024]{2,1,0:T(8,128)(2,1)S(1)} %get-tuple-element.517), channel_id=5, replica_groups=mesh['fsdp'=16,'rep'=2] {'fsdp'}, dimensions={1}, use_global_device_ids=true | all-gather | bytes 557056 | tf_op jit(solution)/shard_map/all_gather | solution.py:339
  188.9 3.7 multiply_add_fusion.13
  196.2 3.6 multiply_add_fusion.12
  206.4 12.7 %copy.496 = bf16[6,196,4,32]{1,3,2,0:T(8,128)(2,1)S(1)} copy(bf16[6,196,4,32]{3,2,1,0:T(4,128)(2,1)S(1)} %reshape.1690) | data formatting | bytes 602112 | tf_op jit(solution)/shard_map/while/body/eval_jaxpr/reshape | solution.py:104
  243.7 13.1 %multiply_convert_fusion.5 = (bf16[1176,1024]{1,0:T(8,128)(2,1)S(1)}, f32[1176,1024]{1,0:T(8,128)}, f32[1176,1024]{1,0:T(8,128)}) fusion(f32[1024]{0:T(1024)S(1)} %bitcast.386, bf16[1,256,1024]{2,1,0:T(8,128)(2,1)S(1)} %copy-done.111, f32[1176,256]{1,0:T(8,128)S(1)} %get-tuple-element.535, f32[256]{0:T(256)S(1)} %copy-done.176, ...), kind=kOutput, calls=%fused_computation.47 | convolution fusion | flops 697546752 | bytes 13786304 | tf_op jit(solution)/shard_map/dot_general | solution.py:230
  260.9 3.8 reshape.1698
  269.6 17.8 %all-gather.7 = bf16[1,256,256]{2,1,0:T(8,128)(2,1)S(1)} all-gather(bf16[1,16,256]{2,1,0:T(8,128)(2,1)S(1)} %copy-done.172), channel_id=9, replica_groups=mesh['fsdp'=16,'rep'=2] {'fsdp'}, dimensions={1}, use_global_device_ids=true | all-gather | bytes 139264 | tf_op jit(solution)/shard_map/all_gather | solution.py:338
  289.4 21.6 %all-gather.9 = bf16[1,1024,256]{2,1,0:T(8,128)(2,1)} all-gather(bf16[1,64,256]{2,1,0:T(8,128)(2,1)S(1)} %copy-done.140), channel_id=11, replica_groups=mesh['fsdp'=16,'rep'=2] {'fsdp'}, dimensions={1}, use_global_device_ids=true | all-gather | bytes 557056 | tf_op jit(solution)/shard_map/all_gather | solution.py:340
  311.0 20.3 %all-gather.8 = bf16[1,256,1024]{2,1,0:T(8,128)(2,1)} all-gather(bf16[1,16,1024]{2,1,0:T(8,128)(2,1)S(1)} %copy-done.139), channel_id=10, replica_groups=mesh['fsdp'=16,'rep'=2] {'fsdp'}, dimensions={1}, use_global_device_ids=true | all-gather | bytes 557056 | tf_op jit(solution)/shard_map/all_gather | solution.py:339
  333.4 3.3 reshape.1705
  346.3 3.0 reshape.1838
  356.2 3.7 multiply_add_fusion.11
  364.6 4.3 multiply_add_fusion.10
  371.1 3.5 copy.507
  377.4 2.9 reshape.1703
  389.3 3.1 copy.524
  392.4 3.4 reshape.1708
  416.9 13.0 %multiply_convert_fusion.4 = (bf16[1176,1024]{1,0:T(8,128)(2,1)}, f32[1176,1024]{1,0:T(8,128)S(1)}, f32[1176,1024]{1,0:T(8,128)S(1)}) fusion(f32[1024]{0:T(1024)S(1)} %bitcast.387, bf16[1,256,1024]{2,1,0:T(8,128)(2,1)S(1)} %copy-done.115, f32[1176,256]{1,0:T(8,128)S(1)} %get-tuple-element.544, f32[256]{0:T(256)S(1)} %copy-done.178, f32[256]{0:T(256)S(1)} %copy-done.174, ...), kind=kOutput, calls=%fused_computation.34 | convolution fusion | flops 697546752 | bytes 13786304 | tf_op jit(solution)/shard_map/dot_general | solution.py:230
  429.9 3.1 fusion.174
  440.2 6.0 multiply_reduce_fusion.24
  446.3 3.6 broadcast_multiply_fusion.9
  450.6 6.1 multiply_reduce_fusion.32
  456.8 3.9 broadcast_multiply_fusion
  462.3 4.3 fusion.54
  466.6 3.7 multiply_reduce_fusion.3
  478.6 5.6 fusion.64
  484.2 2.9 multiply_reduce_fusion.1
  513.2 3.3 fusion.148
  517.1 3.5 convert_reduce_fusion.2
  552.0 6.2 fusion.176
  565.9 6.0 multiply_reduce_fusion.40
  571.9 3.6 broadcast_multiply_fusion.27
  576.2 6.1 multiply_reduce_fusion.48
  582.4 3.6 broadcast_multiply_fusion.18
  587.7 4.3 fusion.57
  592.0 3.7 multiply_reduce_fusion.2
  604.0 5.6 fusion.67
  609.7 2.9 multiply_reduce_fusion
  638.2 3.3 fusion.145
  642.1 3.5 convert_reduce_fusion.1
  669.9 3.6 convolution_convert_fusion.6
  673.6 3.3 convolution_convert_fusion.7
  677.1 3.6 convolution_convert_fusion.2
  680.7 3.7 convolution_convert_fusion.4
  684.5 3.9 convolution_convert_fusion.3
  688.6 3.7 convolution_convert_fusion.5
  692.4 3.2 add_add_fusion.4
  697.0 18.6 %reduce-scatter.31.cloned.1.call-done = bf16[16,22]{1,0:T(8,128)(2,1)} async-done(((bf16[256,22]{1,0:T(8,128)(2,1)}), bf16[16,22]{1,0:T(8,128)(2,1)}) %reduce-scatter.31.cloned.1.call-update) | async-done | bytes 720
  716.9 57.4 %reduce-scatter.21.cloned.1.call-done = bf16[16,256]{1,0:T(8,128)(2,1)} async-done(((bf16[256,256]{1,0:T(8,128)(2,1)}), bf16[16,256]{1,0:T(8,128)(2,1)}) %reduce-scatter.21.cloned.1.call-update) | async-done | bytes 8208 | tf_op jit(solution)/shard_map/reduce_scatter | solution.py:361
  774.3 58.6 %reduce-scatter.19.cloned.1.call-done = bf16[16,256]{1,0:T(8,128)(2,1)} async-done(((bf16[256,256]{1,0:T(8,128)(2,1)}), bf16[16,256]{1,0:T(8,128)(2,1)}) %reduce-scatter.19.cloned.1.call-update) | async-done | bytes 8208 | tf_op jit(solution)/shard_map/reduce_scatter | solution.py:361
  832.9 58.4 %reduce-scatter.17.cloned.1.call-done = bf16[16,768]{1,0:T(8,128)(2,1)} async-done(((bf16[256,768]{1,0:T(8,128)(2,1)}), bf16[16,768]{1,0:T(8,128)(2,1)}) %reduce-scatter.17.cloned.1.call-update) | async-done | bytes 24592 | tf_op jit(solution)/shard_map/reduce_scatter | solution.py:358
  891.4 58.4 %reduce-scatter.15.cloned.1.call-done = bf16[16,768]{1,0:T(8,128)(2,1)} async-done(((bf16[256,768]{1,0:T(8,128)(2,1)}), bf16[16,768]{1,0:T(8,128)(2,1)}) %reduce-scatter.15.cloned.1.call-update) | async-done | bytes 24592 | tf_op jit(solution)/shard_map/reduce_scatter | solution.py:358
  949.8 58.8 %reduce-scatter.29.cloned.1.call-done = bf16[64,256]{1,0:T(8,128)(2,1)} async-done(((bf16[1024,256]{1,0:T(8,128)(2,1)}), bf16[64,256]{1,0:T(8,128)(2,1)}) %reduce-scatter.29.cloned.1.call-update) | async-done | bytes 32784 | tf_op jit(solution)/shard_map/reduce_scatter | solution.py:367
  1008.6 59.4 %reduce-scatter.25.cloned.1.call-done = bf16[16,1024]{1,0:T(8,128)(2,1)} async-done(((bf16[256,1024]{1,0:T(8,128)(2,1)}), bf16[16,1024]{1,0:T(8,128)(2,1)}) %reduce-scatter.25.cloned.1.call-update) | async-done | bytes 32784 | tf_op jit(solution)/shard_map/reduce_scatter | solution.py:364
  1068.0 58.8 %reduce-scatter.27.cloned.1.call-done = bf16[64,256]{1,0:T(8,128)(2,1)} async-done(((bf16[1024,256]{1,0:T(8,128)(2,1)}), bf16[64,256]{1,0:T(8,128)(2,1)}) %reduce-scatter.27.cloned.1.call-update) | async-done | bytes 32784 | tf_op jit(solution)/shard_map/reduce_scatter | solution.py:367
  1126.8 58.7 %reduce-scatter.23.cloned.1.call-done = bf16[16,1024]{1,0:T(8,128)(2,1)} async-done(((bf16[256,1024]{1,0:T(8,128)(2,1)}), bf16[16,1024]{1,0:T(8,128)(2,1)}) %reduce-scatter.23.cloned.1.call-update) | async-done | bytes 32784 | tf_op jit(solution)/shard_map/reduce_scatter | solution.py:364
  1185.5 3.5 fusion.32
  1189.0 22.7 %all-reduce.83.cloned.1.call-done = (bf16[1,16,768]{2,1,0:T(8,128)(2,1)}, bf16[1,16,768]{2,1,0:T(8,128)(2,1)}, bf16[1,16,256]{2,1,0:T(8,128)(2,1)}, bf16[1,16,25...) async-done(((bf16[1,16,768]{2,1,0:T(8,128)(2,1)}, ...) | async-done | bytes 198032 | tf_op jit(solution)/shard_map/psum | solution.py:376
  (971 shorter events, 292.0 us)
Async XLA Ops:
  7.2 46.1 %copy-start.168 = (bf16[2,16,768]{2,1,0:T(8,128)(2,1)S(1)}, bf16[2,16,768]{2,1,0:T(8,128)(2,1)}, u32[]{:S(2)}) copy-start(bf16[2,16,768]{2,1,0:T(8,128)(2,1)} %param.12) | copy-start | bytes 147460
  7.2 688.5 %reduce-scatter.33.cloned.1.call-start = ((), (), s32[]{:S(2)}) async-start(), calls=%async_computation.19 | async-start | bytes 69632
  31.9 45.0 %copy-start.14 = (bf16[1176,256]{1,0:T(8,128)(2,1)S(1)}, bf16[1176,256]{1,0:T(8,128)(2,1)}, u32[]{:S(2)}) copy-start(bf16[1176,256]{1,0:T(8,128)(2,1)} %param.9) | copy-start | bytes 1806340
  51.1 25.7 %copy-start.129 = (f32[1176]{0:T(1024)}, f32[1176]{0:T(1024)S(1)}, u32[]{:S(2)}) copy-start(f32[1176]{0:T(1024)S(1)} %broadcast_multiply_fusion.39) | copy-start | bytes 14116
  53.2 23.6 %copy-start.151 = (f32[1176]{0:T(1024)}, f32[1176]{0:T(1024)S(1)}, u32[]{:S(2)}) copy-start(f32[1176]{0:T(1024)S(1)} %fusion.127) | copy-start | bytes 14116
  56.3 20.5 %copy-start.307 = (f32[256]{0:T(256)}, f32[256]{0:T(256)S(1)}, u32[]{:S(2)}) copy-start(f32[256]{0:T(256)S(1)} %get-tuple-element.401) | copy-start | bytes 3076
  56.3 22.7 %copy-start.181 = (f32[256]{0:T(256)}, f32[256]{0:T(256)S(1)}, u32[]{:S(2)}) copy-start(f32[256]{0:T(256)S(1)} %get-tuple-element.402) | copy-start | bytes 3076
  86.9 25.8 %copy-start.148 = (bf16[1,16,768]{2,1,0:T(8,128)(2,1)S(1)}, bf16[1,16,768]{2,1,0:T(8,128)(2,1)}, u32[]{:S(2)}) copy-start(bf16[1,16,768]{2,1,0:T(8,128)(2,1)} %get-tuple-element.522) | copy-start | bytes 73732
  88.2 88.1 %copy-start.107 = (bf16[1,28,42,128]{3,2,1,0:T(8,128)(2,1)S(1)}, bf16[1,28,42,128]{3,2,1,0:T(8,128)(2,1)}, u32[]{:S(2)}) copy-start(bf16[1,28,42,128]{3,2,1,0:T(8,128)(2,1)} %get-tuple-element.459) | copy-start | bytes 903172
  88.8 87.7 %copy-start.106 = (bf16[1,28,42,128]{3,2,1,0:T(8,128)(2,1)S(1)}, bf16[1,28,42,128]{3,2,1,0:T(8,128)(2,1)}, u32[]{:S(2)}) copy-start(bf16[1,28,42,128]{3,2,1,0:T(8,128)(2,1)} %get-tuple-element.460) | copy-start | bytes 903172
  91.5 127.5 %copy-start.156 = (f32[6,196]{1,0:T(8,128)}, f32[6,196]{1,0:T(8,128)S(1)}, u32[]{:S(2)}) copy-start(f32[6,196]{1,0:T(8,128)S(1)} %select_n.49) | copy-start | bytes 14116
  112.7 82.6 %copy-start.184 = (f32[128]{0:T(128)}, f32[128]{0:T(128)S(1)}, u32[]{:S(2)}) copy-start(f32[128]{0:T(128)S(1)} %get-tuple-element.404) | copy-start | bytes 1540
  112.7 82.6 %copy-start.186 = (f32[128]{0:T(128)}, f32[128]{0:T(128)S(1)}, u32[]{:S(2)}) copy-start(f32[128]{0:T(128)S(1)} %get-tuple-element.405) | copy-start | bytes 1540
  178.0 41.1 %copy-start.43 = (bf16[6,196,4,32]{1,3,2,0:T(8,128)(2,1)}, bf16[6,196,4,32]{1,3,2,0:T(8,128)(2,1)S(1)}, u32[]{:S(2)}) copy-start(bf16[6,196,4,32]{1,3,2,0:T(8,128)(2,1)S(1)} %copy.494) | copy-start | bytes 903172
  179.2 39.9 %copy-start.45 = (bf16[6,196,4,32]{1,3,2,0:T(8,128)(2,1)}, bf16[6,196,4,32]{1,3,2,0:T(8,128)(2,1)S(1)}, u32[]{:S(2)}) copy-start(bf16[6,196,4,32]{1,3,2,0:T(8,128)(2,1)S(1)} %copy.495) | copy-start | bytes 903172
  180.5 51.0 %copy-start.36 = (bf16[4,294,4,32]{1,3,2,0:T(8,128)(2,1)}, bf16[4,294,4,32]{1,3,2,0:T(8,128)(2,1)S(1)}, u32[]{:S(2)}) copy-start(bf16[4,294,4,32]{1,3,2,0:T(8,128)(2,1)S(1)} %copy.485) | copy-start | bytes 903172
  184.3 10.4 copy-start.50
  186.2 9.9 copy-start.192
  186.2 9.9 copy-start.194
  186.2 9.9 copy-start.196
  186.2 9.9 copy-start.198
  186.2 9.9 copy-start.200
  242.4 14.4 %copy-start.24 = (bf16[1176,256]{0,1:T(8,128)(2,1)}, bf16[1176,256]{0,1:T(8,128)(2,1)S(1)}, u32[]{:S(2)}) copy-start(bf16[1176,256]{0,1:T(8,128)(2,1)S(1)} %fusion.50) | copy-start | bytes 1806340
  243.0 13.9 %copy-start.6 = (f32[1176,256]{1,0:T(8,128)}, f32[1176,256]{1,0:T(8,128)S(1)}, u32[]{:S(2)}) copy-start(f32[1176,256]{1,0:T(8,128)S(1)} %get-tuple-element.535) | copy-start | bytes 3612676
  243.4 13.4 %copy-start.160 = (f32[1176]{0:T(1024)}, f32[1176]{0:T(1024)S(1)}, u32[]{:S(2)}) copy-start(f32[1176]{0:T(1024)S(1)} %multiply_reduce_fusion.12) | copy-start | bytes 14116
  243.4 13.4 %copy-start.131 = (f32[1176]{0:T(1024)}, f32[1176]{0:T(1024)S(1)}, u32[]{:S(2)}) copy-start(f32[1176]{0:T(1024)S(1)} %fusion.128) | copy-start | bytes 14116
  243.7 13.1 %copy-start.113 = (bf16[1,1024,256]{2,1,0:T(8,128)(2,1)S(1)}, bf16[1,1024,256]{2,1,0:T(8,128)(2,1)}, u32[]{:S(2)}) copy-start(bf16[1,1024,256]{2,1,0:T(8,128)(2,1)} %all-gather.4) | copy-start | bytes 1572868
  243.7 13.1 %copy-start.311 = (f32[256]{0:T(256)S(1)}, f32[256]{0:T(256)}, u32[]{:S(2)}) copy-start(f32[256]{0:T(256)} %get-tuple-element.394) | copy-start | bytes 3076
  258.3 157.3 %copy-start.16 = (f32[1176,256]{1,0:T(8,128)}, f32[1176,256]{1,0:T(8,128)S(1)}, u32[]{:S(2)}) copy-start(f32[1176,256]{1,0:T(8,128)S(1)} %get-tuple-element.538) | copy-start | bytes 3612676
  267.3 20.1 %copy-start.116 = (f32[1,4,256]{1,2,0:T(8,128)S(1)}, f32[1,4,256]{1,2,0:T(8,128)}, u32[]{:S(2)}) copy-start(f32[1,4,256]{1,2,0:T(8,128)} %slice.854) | copy-start | bytes 12292
  268.3 21.0 %copy-start.140 = (bf16[1,64,256]{2,1,0:T(8,128)(2,1)S(1)}, bf16[1,64,256]{2,1,0:T(8,128)(2,1)}, u32[]{:S(2)}) copy-start(bf16[1,64,256]{2,1,0:T(8,128)(2,1)} %get-tuple-element.514) | copy-start | bytes 98308
  268.3 42.6 %copy-start.139 = (bf16[1,16,1024]{2,1,0:T(8,128)(2,1)S(1)}, bf16[1,16,1024]{2,1,0:T(8,128)(2,1)}, u32[]{:S(2)}) copy-start(bf16[1,16,1024]{2,1,0:T(8,128)(2,1)} %get-tuple-element.516) | copy-start | bytes 98308
  289.3 74.4 %copy-start.220 = (f32[128]{0:T(128)}, f32[128]{0:T(128)S(1)}, u32[]{:S(2)}) copy-start(f32[128]{0:T(128)S(1)} %get-tuple-element.377) | copy-start | bytes 1540
  289.3 74.4 %copy-start.222 = (f32[128]{0:T(128)}, f32[128]{0:T(128)S(1)}, u32[]{:S(2)}) copy-start(f32[128]{0:T(128)S(1)} %get-tuple-element.378) | copy-start | bytes 1540
  289.3 74.4 %copy-start.224 = (f32[128]{0:T(128)}, f32[128]{0:T(128)S(1)}, u32[]{:S(2)}) copy-start(f32[128]{0:T(128)S(1)} %get-tuple-element.379) | copy-start | bytes 1540
  289.3 74.4 %copy-start.226 = (f32[128]{0:T(128)}, f32[128]{0:T(128)S(1)}, u32[]{:S(2)}) copy-start(f32[128]{0:T(128)S(1)} %get-tuple-element.390) | copy-start | bytes 1540
  289.3 74.4 %copy-start.228 = (f32[128]{0:T(128)}, f32[128]{0:T(128)S(1)}, u32[]{:S(2)}) copy-start(f32[128]{0:T(128)S(1)} %get-tuple-element.391) | copy-start | bytes 1540
  289.3 74.4 %copy-start.230 = (f32[128]{0:T(128)}, f32[128]{0:T(128)S(1)}, u32[]{:S(2)}) copy-start(f32[128]{0:T(128)S(1)} %get-tuple-element.392) | copy-start | bytes 1540
  346.2 55.7 %copy-start.40 = (bf16[4,294,4,32]{1,3,2,0:T(8,128)(2,1)}, bf16[4,294,4,32]{1,3,2,0:T(8,128)(2,1)S(1)}, u32[]{:S(2)}) copy-start(bf16[4,294,4,32]{1,3,2,0:T(8,128)(2,1)S(1)} %copy.511) | copy-start | bytes 903172
  353.5 11.1 copy-start.232
  353.5 11.1 copy-start.234
  353.5 11.1 copy-start.236
  415.5 14.3 %copy-start.23 = (bf16[1176,256]{0,1:T(8,128)(2,1)}, bf16[1176,256]{0,1:T(8,128)(2,1)S(1)}, u32[]{:S(2)}) copy-start(bf16[1176,256]{0,1:T(8,128)(2,1)S(1)} %fusion.51) | copy-start | bytes 1806340
  416.1 18.5 %copy-start.4 = (f32[1176,256]{1,0:T(8,128)}, f32[1176,256]{1,0:T(8,128)S(1)}, u32[]{:S(2)}) copy-start(f32[1176,256]{1,0:T(8,128)S(1)} %get-tuple-element.544) | copy-start | bytes 3612676
  416.1 18.5 %copy-start.125 = (f32[1176]{0:T(1024)}, f32[1176]{0:T(1024)S(1)}, u32[]{:S(2)}) copy-start(f32[1176]{0:T(1024)S(1)} %broadcast_multiply_fusion.36) | copy-start | bytes 14116
  416.6 18.1 %copy-start.134 = (f32[1176]{0:T(1024)}, f32[1176]{0:T(1024)S(1)}, u32[]{:S(2)}) copy-start(f32[1176]{0:T(1024)S(1)} %fusion.130) | copy-start | bytes 14116
  416.8 13.0 %copy-start.18 = (bf16[1176,256]{1,0:T(8,128)(2,1)S(1)}, bf16[1176,256]{1,0:T(8,128)(2,1)}, u32[]{:S(2)}) copy-start(bf16[1176,256]{1,0:T(8,128)(2,1)} %param.17) | copy-start | bytes 1806340
  416.9 13.0 %copy-start.92 = (bf16[1,1024,256]{2,1,0:T(8,128)(2,1)S(1)}, bf16[1,1024,256]{2,1,0:T(8,128)(2,1)}, u32[]{:S(2)}) copy-start(bf16[1,1024,256]{2,1,0:T(8,128)(2,1)} %all-gather.9) | copy-start | bytes 1572868
  473.1 11.1 slice-start.2
  493.2 20.0 %copy-start.127 = (f32[28,42]{1,0:T(8,128)}, f32[28,42]{1,0:T(8,128)S(1)}, u32[]{:S(2)}) copy-start(f32[28,42]{1,0:T(8,128)S(1)} %copy.564) | copy-start | bytes 14116
  548.6 12.0 copy-start.34
  551.9 163.7 %reduce-scatter.31.cloned.1.call-start = ((), (), s32[]{:S(2)}) async-start(), calls=%async_computation.18 | async-start | bytes 69632
  598.4 11.2 slice-start
  665.2 109.2 %reduce-scatter.21.cloned.1.call-start = ((), (), s32[]{:S(2)}) async-start(), calls=%async_computation.13 | async-start | bytes 139264 | tf_op jit(solution)/shard_map/reduce_scatter | solution.py:361
  667.6 165.3 %reduce-scatter.19.cloned.1.call-start = ((), (), s32[]{:S(2)}) async-start(), calls=%async_computation.12 | async-start | bytes 139264 | tf_op jit(solution)/shard_map/reduce_scatter | solution.py:361
  669.8 221.5 %reduce-scatter.17.cloned.1.call-start = ((), (), s32[]{:S(2)}) async-start(), calls=%async_computation.11 | async-start | bytes 417792 | tf_op jit(solution)/shard_map/reduce_scatter | solution.py:358
  673.6 276.2 %reduce-scatter.15.cloned.1.call-start = ((), (), s32[]{:S(2)}) async-start(), calls=%async_computation.10 | async-start | bytes 417792 | tf_op jit(solution)/shard_map/reduce_scatter | solution.py:358
  676.9 331.7 %reduce-scatter.29.cloned.1.call-start = ((), (), s32[]{:S(2)}) async-start(), calls=%async_computation.17 | async-start | bytes 557056 | tf_op jit(solution)/shard_map/reduce_scatter | solution.py:367
  680.6 387.4 %reduce-scatter.25.cloned.1.call-start = ((), (), s32[]{:S(2)}) async-start(), calls=%async_computation.15 | async-start | bytes 557056 | tf_op jit(solution)/shard_map/reduce_scatter | solution.py:364
  684.5 442.4 %reduce-scatter.27.cloned.1.call-start = ((), (), s32[]{:S(2)}) async-start(), calls=%async_computation.16 | async-start | bytes 557056 | tf_op jit(solution)/shard_map/reduce_scatter | solution.py:367
  688.4 497.1 %reduce-scatter.23.cloned.1.call-start = ((), (), s32[]{:S(2)}) async-start(), calls=%async_computation.14 | async-start | bytes 557056 | tf_op jit(solution)/shard_map/reduce_scatter | solution.py:364
  692.4 493.1 %copy-start.93 = (bf16[1,1024,256]{2,1,0:T(8,128)(2,1)S(1)}, bf16[1,1024,256]{2,1,0:T(8,128)(2,1)}, u32[]{:S(2)}) copy-start(bf16[1,1024,256]{2,1,0:T(8,128)(2,1)} %all-gather.9) | copy-start | bytes 1572868
  692.4 493.2 %copy-start.180 = (f32[256]{0:T(256)S(1)}, f32[256]{0:T(256)}, u32[]{:S(2)}) copy-start(f32[256]{0:T(256)} %get-tuple-element.357) | copy-start | bytes 3076
  692.4 519.3 %all-reduce.83.cloned.1.call-start = ((), (), s32[]{:S(2)}) async-start(), calls=%async_computation.20 | async-start | bytes 417792 | tf_op jit(solution)/shard_map/psum | solution.py:376
  (278 other events, 1022.7 us)
Sparse Core Ops, SparseCore 0:
  552.0 50.2 reduce-scatter.32
  665.3 50.2 reduce-scatter.30
  719.6 54.6 reduce-scatter.20
  778.2 54.6 reduce-scatter.18
  836.3 55.0 reduce-scatter.16
  894.7 55.0 reduce-scatter.14
  953.3 55.2 reduce-scatter.28
  1012.7 55.2 reduce-scatter.24
  1071.5 55.2 reduce-scatter.26
  1130.2 55.2 reduce-scatter.22
  1189.0 22.6 all-reduce.82
where the time goes:
time: 1230 us
  waiting for transfers between devices  510 us (41%)
  local copies, waits for them, and re-layouts  237 us (19%)
  blocking collectives  203 us (17%)
  matrix products  139 us (11%)
  other arithmetic  115 us (9%)
  between operations  20 us (2%)
    reduce_scatter x2, waiting for transfers between devices, reduce_terms(): lax.psum_scatter(grad_up.astype(jnp.bfloat16), 'fsdp', scatter_dimension=...  118 us
    reduce_scatter x2, waiting for transfers between devices, reduce_terms(): lax.psum_scatter(grad_down.astype(jnp.bfloat16), 'fsdp', scatter_dimensio...  118 us
    reduce_scatter x2, waiting for transfers between devices, reduce_terms(): lax.psum_scatter(grad_mix.astype(jnp.bfloat16), 'fsdp', scatter_dimension...  117 us
    reduce_scatter x2, waiting for transfers between devices, reduce_terms(): lax.psum_scatter(grad_outw.astype(jnp.bfloat16), 'fsdp', scatter_dimensio...  116 us
    all_gather x2, blocking collectives, fetch_forward(): lax.all_gather(w_fc1[layer_index], 'fsdp', axis=0, tiled=True)  42.3 us
    all_gather x2, blocking collectives, fetch_forward(): lax.all_gather(w_fc2[layer_index], 'fsdp', axis=0, tiled=True)  41.9 us
    all_gather x2, blocking collectives, fetch_forward(): lax.all_gather(w_qkv[layer_index], 'fsdp', axis=0, tiled=True)  41.1 us
    all_gather x2, blocking collectives, fetch_forward(): lax.all_gather(vectors[layer_index], 'fsdp', axis=1, tiled=True)  41 us
  transfers between devices with their start and end apart: 11, of which 10 were waited for; matrix products, arithmetic and copies ran while one was open for 12% of the time, Pallas kernels for 0%

commit v1 on v0

v1 whole, which is shorter than its diff:
```python
import functools
import jax
import jax.numpy as jnp
from jax import lax
from jax.experimental import pallas as pl
from jax.experimental.pallas import tpu as pltpu

HEAD = 32
STRIPE = 7
HP = 28
WP = 42
HEADS = 4
GROUP = 8
WG = WP // STRIPE
ROWS = HP * WG * GROUP
CHUNK = STRIPE * WG * GROUP
TALL = HP * GROUP
WIDE_R = 384
WIDE_C = 256
BF = jnp.bfloat16
F32 = jnp.float32
eps_norm = 1e-05
masked_score = -1000000000.0
LOG2E = 1.4426950408889634
LN2 = 0.6931471805599453
SCALE = HEAD ** (-0.5)
NN = (((1,), (0,)), ((), ()))
NT = (((1,), (1,)), ((), ()))
TN = (((0,), (0,)), ((), ()))


def mm(a, b, dims=NN):
    return lax.dot_general(a, b, dims, preferred_element_type=F32)


def iota(shape, dim):
    return lax.broadcasted_iota(jnp.int32, shape, dim)


def span(index, size):
    return pl.ds(pl.multiple_of(index * size, size), size)


def pad_groups(src, dst, scale=None):
    def body(j, carry):
        block = src[pl.ds(pl.multiple_of(j * 56, 8), 56), :].astype(F32).reshape(7, 8, -1)
        place = iota((8, block.shape[-1]), 0)
        for u in range(8):
            if u == 0:
                group = block[0]
            elif u == 7:
                group = pltpu.roll(block[6], 7, 0)
            else:
                group = jnp.where(
                    place < u, pltpu.roll(block[u - 1], u, 0), pltpu.roll(block[u], u, 0)
                )
            group = jnp.where(place < 7, group, 0.0)
            dst[pl.ds(pl.multiple_of(j * 64 + u * 8, 8), 8), :] = group
        return carry

    lax.fori_loop(0, ROWS // 64, body, 0)


def drop_groups(src, dst):
    def body(j, carry):
        block = src[pl.ds(pl.multiple_of(j * 64, 8), 64), :].reshape(8, 8, -1)
        place = iota((8, block.shape[-1]), 0)
        for t in range(7):
            lower = block[t] if t == 0 else pltpu.roll(block[t], 8 - t, 0)
            upper = pltpu.roll(block[t + 1], 7 - t, 0)
            dst[pl.ds(pl.multiple_of(j * 56 + t * 8, 8), 8), :] = jnp.where(
                place <= 6 - t, lower, upper
            )
        return carry

    lax.fori_loop(0, ROWS // 64, body, 0)


def norm_parts(x):
    centre = jnp.mean(x, axis=-1, keepdims=True)
    centred = x - centre
    rate = lax.rsqrt(jnp.mean(centred * centred, axis=-1, keepdims=True) + eps_norm)
    return centred * rate, rate


def norm_back(d_n, xhat, rate, gain):
    e = d_n * gain
    return rate * (
        e
        - jnp.mean(e, axis=-1, keepdims=True)
        - xhat * jnp.mean(e * xhat, axis=-1, keepdims=True)
    )


def colsum(x):
    return jnp.sum(x, axis=0, keepdims=True)


def rows_live(stripe, h, w, lanes):
    shape = (STRIPE, WG * GROUP, lanes)
    row = iota(shape, 0) + stripe * STRIPE
    place = iota(shape, 1)
    within = place & 7
    col = (place >> 3) * STRIPE + within
    live = (row < h) & (col < w) & (within < STRIPE)
    return jnp.where(live, 1.0, 0.0).reshape(CHUNK, lanes)


def cols_live(stripe, h, w, lanes):
    shape = (HP, GROUP, lanes)
    row = iota(shape, 0)
    within = iota(shape, 1)
    live = (row < h) & (within + stripe * STRIPE < w) & (within < STRIPE)
    return jnp.where(live, 1.0, 0.0).reshape(TALL, lanes)


def with_mask(keys, live):
    lane = iota(live.shape, 1)
    extra = jnp.where(lane == 0, jnp.where(live > 0.0, 0.0, masked_score), 0.0)
    return jnp.concatenate([keys, extra.astype(BF)], axis=-1)


def stack_heads(ref, x, wide):
    length = x.shape[0]
    lane = iota(x.shape, 1)
    for h in range(HEADS):
        kept = jnp.where((lane >> 5) == h, x, jnp.zeros_like(x))
        ref[h * wide : h * wide + length, 0:128] = kept


def widen(x, wide):
    length = x.shape[0]
    return jnp.concatenate([x, jnp.zeros((wide - length, x.shape[1]), x.dtype)], axis=0)


def attend(q, k_mask, vm, qs, out_t, lse, stripe, wide):
    length = q.shape[0]
    stack_heads(qs, q, wide)
    scores = mm(k_mask, qs[0 : HEADS * wide, :], NT)
    v_t = widen(vm.astype(F32), wide).T.astype(BF)[:, 0:length]
    for h in range(HEADS):
        s = scores[:, h * wide : (h + 1) * wide]
        top = jnp.max(s, axis=0, keepdims=True)
        p = jnp.exp2(s - top)
        total = jnp.sum(p, axis=0, keepdims=True)
        o = mm(v_t[HEAD * h : HEAD * (h + 1), :], p.astype(BF))
        out_t[stripe, HEAD * h : HEAD * (h + 1), :] = o / total
        lse[stripe, h : h + 1, :] = top + jnp.log2(total)


def attend_back(q, k, k_mask, vm, da, qs, ds_stack, p_all, g_all, out_t, lse, stripe, wide):
    length = q.shape[0]
    stack_heads(qs, q, wide)
    stack_heads(ds_stack, da, wide)
    da_t = widen(da.astype(F32), wide).T
    k_t = widen(k.astype(F32), wide).T.astype(BF)[:, 0:length]
    weighted = da_t * out_t[stripe]
    dq_t = []
    scores = mm(k_mask, qs[0 : HEADS * wide, :], NT)
    d_probs = mm(vm, ds_stack[0 : HEADS * wide, :], NT)
    for h in range(HEADS):
        lanes = slice(h * wide, (h + 1) * wide)
        inner = jnp.sum(weighted[HEAD * h : HEAD * (h + 1), :], axis=0, keepdims=True)
        p = jnp.exp2(scores[:, lanes] - lse[stripe, h : h + 1, :])
        g = (p * (d_probs[:, lanes] - inner)).astype(BF)
        p_all[0:length, lanes] = p.astype(BF)
        g_all[0:length, lanes] = g
        dq_t.append(mm(k_t[HEAD * h : HEAD * (h + 1), :], g))
    dv = mm(p_all[0:length, 0 : HEADS * wide], ds_stack[0 : HEADS * wide, :])
    dk = mm(g_all[0:length, 0 : HEADS * wide], qs[0 : HEADS * wide, 0:128]) * LN2
    dq = jnp.concatenate(dq_t, axis=0).T[0:length, :] * SCALE
    return dq, dk, dv


def earlier(x):
    return jnp.concatenate([jnp.zeros_like(x[:1]), x[:-1]], axis=0)


def later(x):
    return jnp.concatenate([x[1:], jnp.zeros_like(x[:1])], axis=0)


def row_neighbours(x):
    groups = x.reshape(STRIPE * WG, GROUP, 128)
    place = iota(groups.shape, 1)
    edge = jnp.zeros((STRIPE, 1, GROUP, 128), x.dtype)
    far = pltpu.roll(groups, 2, 1).reshape(STRIPE, WG, GROUP, 128)
    far = jnp.concatenate([edge, far[:, :-1]], axis=1).reshape(groups.shape)
    left = jnp.where(place == 0, far, pltpu.roll(groups, 1, 1))
    far = pltpu.roll(groups, 6, 1).reshape(STRIPE, WG, GROUP, 128)
    far = jnp.concatenate([far[:, 1:], edge], axis=1).reshape(groups.shape)
    right = jnp.where(place == 6, far, pltpu.roll(groups, 7, 1))
    shape = (STRIPE, WG * GROUP, 128)
    return left.reshape(shape), x.reshape(shape), right.reshape(shape)


def col_neighbours(x):
    cells = x.reshape(HP, GROUP, 128)
    return pltpu.roll(cells, 1, 1), cells, pltpu.roll(cells, 7, 1)


def position(near, taps):
    rows = [sum(taps[3 * a + b] * near[b] for b in range(3)) for a in range(3)]
    return earlier(rows[0]) + rows[1] + later(rows[2])


def position_back(near, taps):
    rows = [sum(taps[3 * a + b] * near[2 - b] for b in range(3)) for a in range(3)]
    return later(rows[0]) + rows[1] + earlier(rows[2])


def tap_sums(da, near):
    sums = []
    for a in range(3):
        for b in range(3):
            x = near[b]
            x = earlier(x) if a == 0 else later(x) if a == 2 else x
            sums.append(colsum((da * x).reshape(-1, 128)))
    return sums


def forward_layer(l, h, w, wt, r):
    vec = wt.vec[l].astype(F32)

    def project(s, carry):
        rows = span(s, CHUNK)
        xhat, rate = norm_parts(r.x[l, rows, :])
        n1 = (xhat * vec[0:1] + vec[1:2]).astype(BF)
        r.n1[l, rows, :] = n1
        live = rows_live(s, h, w, 256)
        mixed = mm(n1, wt.qkv[l])
        q = (mixed[:, 0:256] + vec[2:3]) * (SCALE * LOG2E)
        k = mixed[:, 256:512]
        v = (mixed[:, 512:768] + vec[3:4]) * live
        for i, part in enumerate((q, k, v)):
            r.row[i, l, rows, :] = part[:, 0:128].astype(BF)
            cells = part[:, 128:256].reshape(STRIPE, WG, GROUP, 128)
            for c in range(STRIPE):
                r.turn[i, :, s * STRIPE + c] = cells[c]
        return carry

    lax.fori_loop(0, HP // STRIPE, project, 0)

    def horizontal(s, carry):
        rows = span(s, CHUNK)
        q, k, v = (r.row[i, l, rows, :] for i in range(3))
        attend(q, with_mask(k, rows_live(s, h, w, 128)), v, r.qs_r, r.o_r.at[l], r.lse_r.at[l], s, WIDE_R)
        near = row_neighbours(v.astype(F32))
        taps = vec[9:18, 0:128]
        pos = position(near, [taps[i : i + 1] for i in range(9)]) + vec[8:9, 0:128]
        o = r.o_r[l, s].T[0:CHUNK, :]
        r.a[l, rows, 0:128] = (o + pos.reshape(CHUNK, 128)).astype(BF)
        return carry

    lax.fori_loop(0, HP // STRIPE, horizontal, 0)

    def vertical(s, carry):
        q, k, v = (r.turn[i, s].reshape(TALL, 128).astype(BF) for i in range(3))
        for i, part in enumerate((q, k, v)):
            r.col[i, l, s] = part
        attend(q, with_mask(k, cols_live(s, h, w, 128)), v, r.qs_c, r.o_c.at[l], r.lse_c.at[l], s, WIDE_C)
        near = col_neighbours(v.astype(F32))
        taps = vec[9:18, 128:256]
        pos = position(near, [taps[i : i + 1] for i in range(9)]) + vec[8:9, 128:256]
        o = r.o_c[l, s].T[0:TALL, :]
        r.back[0, :, s] = o.reshape(HP, GROUP, 128) + pos
        return carry

    lax.fori_loop(0, WG, vertical, 0)

    def feed(s, carry):
        rows = span(s, CHUNK)
        turned = r.back[0, pl.ds(s * STRIPE, STRIPE)].reshape(CHUNK, 128).astype(BF)
        r.a[l, rows, 128:256] = turned
        x1 = r.x[l, rows, :] + mm(r.a[l, rows, :], wt.proj[l]) + vec[4:5]
        r.after[l, rows, :] = x1
        xhat, rate = norm_parts(x1)
        n2 = (xhat * vec[5:6] + vec[6:7]).astype(BF)
        r.n2[l, rows, :] = n2
        hidden_bias = jnp.concatenate([vec[18 + j : 19 + j] for j in range(4)], axis=1)
        hid = mm(n2, wt.fc1[l]) + hidden_bias
        phi = 0.5 * lax.erf(hid * 0.7071067811865476) + 0.5
        slope = phi + hid * (jnp.exp2(hid * hid * (-0.5 * LOG2E)) * 0.3989422804014327)
        act = (hid * phi).astype(BF)
        r.act[l, rows, :] = act
        r.slope[l, rows, :] = slope.astype(BF)
        r.x[l + 1, rows, :] = x1 + mm(act, wt.fc2[l]) + vec[7:8]
        return carry

    lax.fori_loop(0, HP // STRIPE, feed, 0)


def backward_layer(l, h, w, wt, r, out):
    vec = wt.vec[l].astype(F32)
    r.gv[...] = jnp.zeros_like(r.gv)

    def add(row, value):
        r.gv[row : row + 1, :] += value

    def feed(s, carry):
        rows = span(s, CHUNK)
        g = r.g[rows, :]
        add(7, colsum(g))
        gy = g.astype(BF)
        r.gy[rows, :] = gy
        d_hid = mm(gy, wt.fc2[l], NT) * r.slope[l, rows, :].astype(F32)
        for j in range(4):
            add(18 + j, colsum(d_hid[:, 256 * j : 256 * (j + 1)]))
        dh = d_hid.astype(BF)
        r.dh[rows, :] = dh
        d_n2 = mm(dh, wt.fc1[l], NT)
        xhat, rate = norm_parts(r.after[l, rows, :])
        add(5, colsum(d_n2 * xhat))
        add(6, colsum(d_n2))
        g1 = g + norm_back(d_n2, xhat, rate, vec[5:6])
        r.g[rows, :] = g1
        add(4, colsum(g1))
        g1_low = g1.astype(BF)
        r.g1[rows, :] = g1_low
        da = mm(g1_low, wt.proj[l], NT)
        r.da_r[rows, :] = da[:, 0:128].astype(BF)
        add(8, colsum(da.astype(BF).astype(F32)))
        cells = da[:, 128:256].reshape(STRIPE, WG, GROUP, 128)
        for c in range(STRIPE):
            r.turn[0, :, s * STRIPE + c] = cells[c]
        return carry

    lax.fori_loop(0, HP // STRIPE, feed, 0)
    out.fc2[l] = mm(r.act[l], r.gy[...], TN).astype(BF)
    out.fc1[l] = mm(r.n2[l], r.dh[...], TN).astype(BF)
    out.proj[l] = mm(r.a[l], r.g1[...], TN).astype(BF)

    def horizontal(s, carry):
        rows = span(s, CHUNK)
        q, k, v = (r.row[i, l, rows, :] for i in range(3))
        da = r.da_r[rows, :]
        live = rows_live(s, h, w, 128)
        dq, dk, dv = attend_back(
            q, k, with_mask(k, live), v, da, r.qs_r, r.ds_r, r.p_all, r.g_all,
            r.o_r.at[l], r.lse_r.at[l], s, WIDE_R,
        )
        taps = [vec[9 + i : 10 + i, 0:128] for i in range(9)]
        da_near = row_neighbours(da.astype(F32))
        dv = (dv + position_back(da_near, taps).reshape(CHUNK, 128)) * live
        sums = tap_sums(da_near[1], row_neighbours(v.astype(F32)))
        for i in range(9):
            r.gv[9 + i : 10 + i, 0:128] += sums[i]
        r.gv[2:3, 0:128] += colsum(dq)
        r.gv[3:4, 0:128] += colsum(dv)
        for i, part in enumerate((dq, dk, dv)):
            r.dqkv[rows, 256 * i : 256 * i + 128] = part.astype(BF)
        return carry

    lax.fori_loop(0, HP // STRIPE, horizontal, 0)

    def vertical(s, carry):
        q, k, v = (r.col[i, l, s] for i in range(3))
        da = r.turn[0, s].reshape(TALL, 128).astype(BF)
        live = cols_live(s, h, w, 128)
        dq, dk, dv = attend_back(
            q, k, with_mask(k, live), v, da, r.qs_c, r.ds_c, r.p_all, r.g_all,
            r.o_c.at[l], r.lse_c.at[l], s, WIDE_C,
        )
        taps = [vec[9 + i : 10 + i, 128:256] for i in range(9)]
        da_near = col_neighbours(da.astype(F32))
        dv = (dv + position_back(da_near, taps).reshape(TALL, 128)) * live
        sums = tap_sums(da_near[1], col_neighbours(v.astype(F32)))
        for i in range(9):
            r.gv[9 + i : 10 + i, 128:256] += sums[i]
        r.gv[2:3, 128:256] += colsum(dq)
        r.gv[3:4, 128:256] += colsum(dv)
        for i, part in enumerate((dq, dk, dv)):
            r.back[i, :, s] = part.reshape(HP, GROUP, 128)
        return carry

    lax.fori_loop(0, WG, vertical, 0)

    def mix(s, carry):
        rows = span(s, CHUNK)
        for i in range(3):
            turned = r.back[i, pl.ds(s * STRIPE, STRIPE)].reshape(CHUNK, 128)
            r.dqkv[rows, 256 * i + 128 : 256 * i + 256] = turned.astype(BF)
        d_n1 = mm(r.dqkv[rows, :], wt.qkv[l], NT)
        xhat, rate = norm_parts(r.x[l, rows, :])
        add(0, colsum(d_n1 * xhat))
        add(1, colsum(d_n1))
        r.g[rows, :] += norm_back(d_n1, xhat, rate, vec[0:1])
        return carry

    lax.fori_loop(0, HP // STRIPE, mix, 0)
    out.qkv[l] = mm(r.n1[l], r.dqkv[...], TN).astype(BF)
    out.vec[l] = r.gv[...].astype(BF)


SCRATCH = dict(
    x=((3, ROWS, 256), F32),
    after=((2, ROWS, 256), F32),
    n1=((2, ROWS, 256), BF),
    n2=((2, ROWS, 256), BF),
    a=((2, ROWS, 256), BF),
    act=((2, ROWS, 1024), BF),
    slope=((2, ROWS, 1024), BF),
    row=((3, 2, ROWS, 128), BF),
    col=((3, 2, WG, TALL, 128), BF),
    turn=((3, WG, HP, GROUP, 128), F32),
    back=((3, HP, WG, GROUP, 128), F32),
    o_r=((2, HP // STRIPE, 128, WIDE_R), F32),
    o_c=((2, WG, 128, WIDE_C), F32),
    lse_r=((2, HP // STRIPE, 8, WIDE_R), F32),
    lse_c=((2, WG, 8, WIDE_C), F32),
    qs_r=((HEADS * WIDE_R, 256), BF),
    qs_c=((HEADS * WIDE_C, 256), BF),
    ds_r=((HEADS * WIDE_R, 128), BF),
    ds_c=((HEADS * WIDE_C, 128), BF),
    p_all=((CHUNK, HEADS * WIDE_R), BF),
    g_all=((CHUNK, HEADS * WIDE_R), BF),
    g=((ROWS, 256), F32),
    gy=((ROWS, 256), BF),
    g1=((ROWS, 256), BF),
    dh=((ROWS, 1024), BF),
    da_r=((ROWS, 128), BF),
    dqkv=((ROWS, 768), BF),
    gv=((24, 256), F32),
)


class Refs:
    def __init__(self, names, refs):
        self.__dict__.update(zip(names, refs))


WEIGHTS = ("qkv", "proj", "fc1", "fc2", "vec")


def step_kernel(*refs):
    h_ref, w_ref, tok, cot = refs[:4]
    wt = Refs(WEIGHTS, refs[4:9])
    y_ref, gt_ref = refs[9:11]
    out = Refs(WEIGHTS, refs[11:16])
    r = Refs(SCRATCH, refs[16:])
    h, w = h_ref[0], w_ref[0]
    layers = wt.qkv.shape[0]
    for stack in (r.qs_r, r.qs_c):
        stack[...] = jnp.where(iota(stack.shape, 1) == 128, 1.0, 0.0).astype(BF)
    for stack in (r.ds_r, r.ds_c):
        stack[...] = jnp.zeros_like(stack)
    pad_groups(tok, r.x.at[0])
    pad_groups(cot, r.g)

    def forward(l, carry):
        forward_layer(l, h, w, wt, r)
        return carry

    lax.fori_loop(0, layers, forward, 0)
    drop_groups(r.x.at[layers], y_ref)

    def backward(i, carry):
        backward_layer(layers - 1 - i, h, w, wt, r, out)
        return carry

    lax.fori_loop(0, layers, backward, 0)
    drop_groups(r.g, gt_ref)


def local_step(heights, widths, tokens, cotangent, full):
    vmem = pl.BlockSpec(memory_space=pltpu.VMEM)
    smem = pl.BlockSpec(memory_space=pltpu.SMEM)
    count, width = tokens.shape
    layers = full[0].shape[0]
    shapes = [jax.ShapeDtypeStruct((count, width), F32)] * 2
    shapes += [jax.ShapeDtypeStruct(m.shape, BF) for m in full[:4]]
    shapes += [jax.ShapeDtypeStruct((layers, 24, width), BF)]
    return pl.pallas_call(
        step_kernel,
        out_shape=shapes,
        in_specs=[smem, smem, vmem, vmem] + [vmem] * 5,
        out_specs=[vmem] * 7,
        scratch_shapes=[pltpu.VMEM(s, d) for s, d in SCRATCH.values()],
        compiler_params=pltpu.CompilerParams(vmem_limit_bytes=67043328),
    )(heights, widths, tokens, cotangent, *full)


MESH = pl.DeviceIdType.MESH


class Grid:
    def __init__(self, shards, copies):
        self.cores = 2
        self.zs = 4
        self.xs = shards // 8
        self.copies = copies
        index = lax.axis_index("fsdp")
        self.rep = lax.axis_index("rep")
        self.core = lax.rem(index, 2)
        chip = lax.div(index, 2)
        self.x = lax.rem(chip, self.xs)
        self.z = lax.div(chip, self.xs)

    def at(self, z, x, core):
        return {"fsdp": (z * self.xs + x) * 2 + core, "rep": self.rep}

    def z_peers(self):
        return [(d, lax.rem(self.z + d, self.zs)) for d in range(1, self.zs)]

    def x_peers(self):
        return [(d, lax.rem(self.x + d, self.xs)) for d in range(1, self.xs)]

    def rep_peers(self):
        return [(d, lax.rem(self.rep + d, self.copies)) for d in range(1, self.copies)]

    def z_device(self, z):
        return self.at(z, self.x, self.core)

    def x_device(self, x):
        return self.at(self.z, x, self.core)

    def sibling(self):
        return self.at(self.z, self.x, 1 - self.core)

    def rep_device(self, rep):
        index = (self.z * self.xs + self.x) * 2 + self.core
        return {"fsdp": index, "rep": rep}

    def steps(self):
        return self.zs - 1 + self.xs - 1 + 1

    def greet(self, copies):
        devices = [self.z_device(z) for _, z in self.z_peers()]
        devices += [self.x_device(x) for _, x in self.x_peers()] + [self.sibling()]
        if copies:
            devices += [self.rep_device(rep) for _, rep in self.rep_peers()]
        barrier = pltpu.get_barrier_semaphore()
        for device in devices:
            pl.semaphore_signal(barrier, inc=1, device_id=device, device_id_type=MESH)
        pl.semaphore_wait(barrier, len(devices))


def remote(src, dst, send, recv, device):
    return pltpu.make_async_remote_copy(
        src_ref=src, dst_ref=dst, send_sem=send, recv_sem=recv,
        device_id=device, device_id_type=MESH,
    )


class Gather:
    def __init__(self, grid, own, full, sems, row):
        self.grid, self.own, self.full = grid, own, full
        send, recv, local = sems
        g = grid
        mine = full.at[g.z, g.x, g.core]
        self.keep = pltpu.make_async_copy(own, mine, local.at[row])
        self.along_z = [
            remote(own, mine, send.at[row, d - 1], recv.at[row, d - 1], g.z_device(z))
            for d, z in g.z_peers()
        ]
        base = g.zs - 2
        lane = full.at[:, g.x, g.core]
        self.along_x = [
            remote(lane, lane, send.at[row, base + d], recv.at[row, base + d], g.x_device(x))
            for d, x in g.x_peers()
        ]
        last = g.zs - 1 + g.xs - 1
        plane = full.at[:, :, g.core]
        self.across = remote(plane, plane, send.at[row, last], recv.at[row, last], g.sibling())

    def begin(self):
        self.keep.start()
        for copy in self.along_z:
            copy.start()

    def second(self):
        self.keep.wait()
        for copy in self.along_z:
            copy.wait_recv()
        for copy in self.along_x:
            copy.start()

    def third(self):
        for copy in self.along_x:
            copy.wait_recv()
        self.across.start()

    def finish(self):
        self.across.wait_recv()

    def drain(self):
        for copy in self.along_z + self.along_x + [self.across]:
            copy.wait_send()


class Reduce:
    def __init__(self, grid, part, bufs, out, sems, row):
        self.grid, self.part, self.out = grid, part, out
        send, recv = sems
        g = grid
        self.from_sibling, self.chip, self.from_x, self.line, self.from_z, self.own, self.from_rep = bufs
        self.across = remote(
            part.at[:, :, 1 - g.core], self.from_sibling, send.at[row, 0], recv.at[row, 0], g.sibling()
        )
        self.along_x = [
            remote(self.chip.at[:, x], self.from_x.at[d - 1], send.at[row, d], recv.at[row, d], g.x_device(x))
            for d, x in g.x_peers()
        ]
        base = g.xs - 1
        self.along_z = [
            remote(self.line.at[z], self.from_z.at[d - 1], send.at[row, base + d], recv.at[row, base + d], g.z_device(z))
            for d, z in g.z_peers()
        ]
        base += g.zs - 1
        self.along_rep = [
            remote(self.own, self.from_rep.at[d - 1], send.at[row, base + d], recv.at[row, base + d], g.rep_device(rep))
            for d, rep in g.rep_peers()
        ]

    def begin(self):
        self.across.start()

    def second(self):
        self.across.wait_recv()
        mine = self.part[:, :, self.grid.core].astype(F32)
        self.chip[...] = (mine + self.from_sibling[...].astype(F32)).astype(BF)
        for copy in self.along_x:
            copy.start()

    def third(self):
        for copy in self.along_x:
            copy.wait_recv()
        total = self.chip[:, self.grid.x].astype(F32)
        for d, _ in self.grid.x_peers():
            total = total + self.from_x[d - 1].astype(F32)
        self.line[...] = total.astype(BF)
        for copy in self.along_z:
            copy.start()

    def fourth(self):
        for copy in self.along_z:
            copy.wait_recv()
        total = self.line[self.grid.z].astype(F32)
        for d, _ in self.grid.z_peers():
            total = total + self.from_z[d - 1].astype(F32)
        self.own[...] = total.astype(BF)
        for copy in self.along_rep:
            copy.start()

    def finish(self):
        for copy in self.along_rep:
            copy.wait_recv()
        total = self.own[...].astype(F32)
        for d, _ in self.grid.rep_peers():
            total = total + self.from_rep[d - 1].astype(F32)
        self.out[...] = total

    def drain(self):
        for copy in [self.across] + self.along_x + self.along_z + self.along_rep:
            copy.wait_send()


def reduce_bufs(zs, xs, copies, shape):
    dims = [(zs, xs), (zs, xs), (max(xs - 1, 1), zs), (zs,), (zs - 1,), (), (max(copies - 1, 1),)]
    return [pltpu.VMEM(d + tuple(shape), BF) for d in dims]


def gather_kernel(shards, copies, count, *refs):
    own, full, sems = refs[:count], refs[count : 2 * count], refs[2 * count :]
    g = Grid(shards, copies)
    g.greet(False)
    parts = [Gather(g, own[i], full[i], sems, i) for i in range(count)]
    for move in ("begin", "second", "third", "finish", "drain"):
        for part in parts:
            getattr(part, move)()


def gather_all(own, shards, copies):
    count = len(own)
    vmem = pl.BlockSpec(memory_space=pltpu.VMEM)
    lead = (4, shards // 8, 2)
    steps = lead[0] - 1 + lead[1] - 1 + 1
    return pl.pallas_call(
        functools.partial(gather_kernel, shards, copies, count),
        out_shape=[jax.ShapeDtypeStruct(lead + o.shape, o.dtype) for o in own],
        in_specs=[vmem] * count,
        out_specs=[vmem] * count,
        scratch_shapes=[
            pltpu.SemaphoreType.DMA((count, steps)),
            pltpu.SemaphoreType.DMA((count, steps)),
            pltpu.SemaphoreType.DMA((count,)),
        ],
        compiler_params=pltpu.CompilerParams(
            collective_id=0, has_side_effects=True, vmem_limit_bytes=67043328
        ),
    )(*own)


def reduce_kernel(shards, copies, count, *refs):
    parts, outs = refs[:count], refs[count : 2 * count]
    bufs = refs[2 * count : 2 * count + 7 * count]
    sems = refs[9 * count :]
    g = Grid(shards, copies)
    g.greet(True)
    sums = [
        Reduce(g, parts[i], bufs[7 * i : 7 * i + 7], outs[i], sems, i) for i in range(count)
    ]
    for move in ("begin", "second", "third", "fourth", "finish", "drain"):
        for one in sums:
            getattr(one, move)()


def reduce_all(parts, shards, copies):
    count = len(parts)
    vmem = pl.BlockSpec(memory_space=pltpu.VMEM)
    zs, xs = 4, shards // 8
    steps = 1 + xs - 1 + zs - 1 + copies - 1
    scratch = []
    for p in parts:
        scratch += reduce_bufs(zs, xs, copies, p.shape[3:])
    return pl.pallas_call(
        functools.partial(reduce_kernel, shards, copies, count),
        out_shape=[jax.ShapeDtypeStruct(p.shape[3:], F32) for p in parts],
        in_specs=[vmem] * count,
        out_specs=[vmem] * count,
        scratch_shapes=scratch
        + [pltpu.SemaphoreType.DMA((count, steps)), pltpu.SemaphoreType.DMA((count, steps))],
        compiler_params=pltpu.CompilerParams(
            collective_id=1, has_side_effects=True, vmem_limit_bytes=67043328
        ),
    )(*parts)


def shards_step(shards, copies, tokens, heights, widths, w_qkv, w_proj, w_fc1, w_fc2, vectors, cotangent):
    layers = w_qkv.shape[0]
    vec_own = vectors.astype(F32).transpose(0, 2, 1)
    gathered = gather_all([w_qkv, w_proj, w_fc1, w_fc2, vec_own], shards, copies)
    full = []
    for i, m in enumerate(gathered):
        m = m.reshape((shards,) + m.shape[3:]).transpose(1, 0, 2, 3)
        full.append(m.reshape(layers, -1, m.shape[-1]))
    full[4] = full[4].transpose(0, 2, 1).astype(BF)
    y, gt, *grads = local_step(heights, widths, tokens, cotangent, full)
    lead = (4, shards // 8, 2)
    parts = []
    grads[4] = grads[4].transpose(0, 2, 1)
    for m in grads:
        m = m.reshape(layers, shards, -1, m.shape[-1]).transpose(1, 0, 2, 3)
        parts.append(m.reshape(lead + m.shape[1:]))
    sums = reduce_all(parts, shards, copies)
    vec = sums[4].transpose(0, 2, 1)[:, : vectors.shape[1]]
    return (y, gt, *sums[:4], vec)


def solution(mesh):
    from jax.sharding import PartitionSpec as P

    images = P(("fsdp", "rep"), None)
    weights = P(None, "fsdp", None)
    return jax.shard_map(
        functools.partial(shards_step, mesh.shape["fsdp"], mesh.shape["rep"]),
        mesh=mesh,
        in_specs=(images, P(("fsdp", "rep")), P(("fsdp", "rep")), weights, weights, weights, weights, P(None, None, "fsdp"), images),
        out_specs=(images, images, weights, weights, weights, weights, P(None, None, "fsdp")),
        check_vma=False,
    )
```

time: 1230 us -> 178 us (0.14)
  waiting for transfers between devices: 510 us -> 0 us
  local copies, waits for them, and re-layouts: 237 us -> 20.8 us
  blocking collectives: 203 us -> 0 us
  Pallas kernels: 0 us -> 154 us
  matrix products: 139 us -> 0 us
  other arithmetic: 115 us -> 1.32 us
  between operations: 20 us -> 2.01 us
    reduce_scatter x8 -> x0, waiting for transfers between devices: 469 us -> none  [the longest x2 118 us: reduce_terms(): lax.psum_scatter(grad_up.astype(jnp.bfloat16), 'fsdp', scatter_dimension=...]
    all_gather x10 -> x0, blocking collectives: 203 us -> none  [the longest x2 42.3 us: fetch_forward(): lax.all_gather(w_fc1[layer_index], 'fsdp', axis=0, tiled=True)]
    pallas_call x0 -> x3, Pallas kernels: none -> 154 us  [the longest x1 78.8 us: local_step(): pl.pallas_call(step_kernel, out_shape=shapes, in_specs=[smem, smem, vmem,...]
    dot_general x48 -> x0, matrix products: 139 us -> none  [the longest x2 26.1 us: run_layer(): jnp.dot(normed_two_low, w_up, preferred_element_type=jnp.float32)]
    reshape x56 -> x9, local copies, waits for them, and re-layouts: 93.3 us -> 10.8 us  [the longest x5 5.79 us: shards_step(): m = m.reshape(layers, shards, -1, m.shape[-1]).transpose(1, 0, 2, 3)]
    reduce_sum x26 -> x0, other arithmetic: 47.5 us -> none  [the longest x4 13.5 us: position_term(): padded[:, offset_row:offset_row + height, :, offset_col:offset_col + STRI...]
    concatenate x28 -> x0, local copies, waits for them, and re-layouts: 30.6 us -> none  [the longest x16 11.8 us: layer_back(): jnp.concatenate([grad_queries, grad_keys, grad_values_all], axis=-1)]
    slice x30 -> x0, local copies, waits for them, and re-layouts: 28.9 us -> none  [the longest x4 6.97 us: attention_forward(): values_all[..., :half_dim]]
  transfers between devices with their start and end apart: 11 -> 0, of which waited for: 10 -> 0; matrix products, arithmetic and copies ran while one was open for 12% -> 0% of each run, Pallas kernels for 0% -> 0%
where the time goes in v1:
time: 178 us
  Pallas kernels  154 us (87%)
  local copies, waits for them, and re-layouts  20.8 us (12%)
  between operations  2.01 us (1%)
    pallas_call x1, Pallas kernels, local_step(): pl.pallas_call(step_kernel, out_shape=shapes, in_specs=[smem, smem, vmem,...  78.8 us
    pallas_call x1, Pallas kernels, reduce_all(): pl.pallas_call(functools.partial(reduce_kernel, shards, copies, count), o...  37.7 us
    pallas_call x1, Pallas kernels, gather_all(): pl.pallas_call(functools.partial(gather_kernel, shards, copies, count), o...  37.3 us
    unnamed x19, local copies, waits for them, and re-layouts  7.9 us
    reshape x5, local copies, waits for them, and re-layouts, shards_step(): m = m.reshape(layers, shards, -1, m.shape[-1]).transpose(1, 0, 2, 3)  5.79 us
    reshape x4, local copies, waits for them, and re-layouts, shards_step(): m = m.reshape((shards,) + m.shape[3:]).transpose(1, 0, 2, 3)  5.02 us

profile of v1, /device:TPU:0, one launch (start us, length us, event | category | flops | bytes accessed | tf_op | source)
XLA Modules:
  0.0 177.9 jit_solution(16075743328327795192)
XLA Ops:
  1.9 1.3 convert_bitcast_fusion.refs_4_
  3.2 37.3 %shard_map.144 = (bf16[4,2,2,2,16,768]{5,4,3,2,1,0:T(8,128)(2,1)}, bf16[4,2,2,2,16,256]{5,4,3,2,1,0:T(8,128)(2,1)}, bf16[4,2,2,2,16,1024]{5,4,3,2,1,0:T(8,128)(2...) custom-call(bf16[2,16,768]{2,1,0:T(8,128)(2,1)} %refs_0_.2, bf16[2,16,256]{2,1,0:T(8,128)(2,1)} %refs_1_.2, ...), custom_call_target="tpu_custom_call" | custom-call | tf_op jit(solution)/shard_map/pallas_call | solution.py:678
  40.5 0.0 copy-start.6
  40.5 0.0 copy-start.5
  40.5 0.0 copy-start.3
  40.5 2.2 %copy.26 = bf16[16,2,16,768]{3,2,0,1:T(8,128)(2,1)} copy(bf16[16,2,16,768]{3,2,1,0:T(8,128)(2,1)} %bitcast.63) | data formatting | bytes 1572864 | tf_op jit(solution)/shard_map/reshape | solution.py:735
  42.7 0.0 copy-done.6
  42.7 0.7 copy.27
  43.4 0.0 copy-done.5
  43.5 0.4 copy.30
  43.9 0.0 copy-start.2
  43.9 0.2 convert_element_type.15
  44.1 0.6 copy.38
  44.7 0.0 copy-done.3
  44.7 1.1 copy.28
  45.8 0.0 copy-done.2
  45.8 1.1 copy.29
  46.9 78.8 %shard_map.145 = (f32[1176,256]{1,0:T(8,128)}, f32[1176,256]{1,0:T(8,128)}, bf16[2,256,768]{2,1,0:T(8,128)(2,1)}, bf16[2,256,256]{2,1,0:T(8,128)(2,1)}, bf16[2,2...) custom-call(s32[1]{0:T(128)S(6)} %copy.44.refs_0_, s32[1]{0:T(128)S(6)} %copy.45.refs_1_, ...), custom_call_target="tpu_custom_call" | custom-call | tf_op jit(solution)/shard_map/pallas_call | solution.py:473
  125.7 0.0 copy-start.4
  125.7 1.0 reshape.88
  126.7 0.0 copy-start.1
  126.7 0.9 copy.36
  127.6 1.7 copy.33
  129.3 0.0 copy-done.4
  129.3 1.0 copy.32
  130.2 0.0 copy-start
  130.2 0.0 copy-done.1
  130.2 1.1 copy.34
  131.3 0.5 copy-done
  131.8 1.0 copy.35
  132.9 37.7 %shard_map.146 = (f32[2,16,768]{2,1,0:T(8,128)}, f32[2,16,256]{2,1,0:T(8,128)}, f32[2,16,1024]{2,1,0:T(8,128)}, f32[2,64,256]{2,1,0:T(8,128)}, f32[2,16,24]{2,1,0:T(8,128)}) custom-call(bf16[4,2,2,2,16,768]{5,4,3,2,1,0:T(8,128)(2,1)} %bitcast.55, bf16[4,2,2,2,16,256]{5,4,3,2,1,0:T(8,128)(2,1)} %bitcast.57, bf16[4,2,2,2,16,1024]{5,4,3,2,1,0:T(8,128)(2,1)} %bitcast.52, ...), custom_call_target="tpu_custom_call" | custom-call | tf_op jit(solution)/shard_map/pallas_call | solution.py:716
  170.6 1.5 copy.46
  172.1 1.4 copy.47
  173.5 1.6 copy.48
  175.0 1.6 copy.49
  176.6 1.3 copy.50
  (1 shorter events, 0.0 us)
Async XLA Ops:
  40.5 2.2 %copy-start.6 = (bf16[4,2,2,2,16,256]{5,4,3,2,1,0:T(8,128)(2,1)S(1)}, bf16[4,2,2,2,16,256]{5,4,3,2,1,0:T(8,128)(2,1)}, u32[]{:S(2)}) copy-start(bf16[4,2,2,2,16,256]{5,4,3,2,1,0:T(8,128)(2,1)} %get-tuple-element.25) | copy-start | bytes 786436
  40.5 2.9 %copy-start.5 = (f32[4,2,2,2,16,22]{5,4,3,2,1,0:T(8,128)S(1)}, f32[4,2,2,2,16,22]{5,4,3,2,1,0:T(8,128)}, u32[]{:S(2)}) copy-start(f32[4,2,2,2,16,22]{5,4,3,2,1,0:T(8,128)} %get-tuple-element.28) | copy-start | bytes 135172
  40.5 4.2 %copy-start.3 = (bf16[4,2,2,2,16,1024]{5,4,3,2,1,0:T(8,128)(2,1)S(1)}, bf16[4,2,2,2,16,1024]{5,4,3,2,1,0:T(8,128)(2,1)}, u32[]{:S(2)}) copy-start(bf16[4,2,2,2,16,1024]{5,4,3,2,1,0:T(8,128)(2,1)} %get-tuple-element.26) | copy-start | bytes 3145732
  43.9 1.9 %copy-start.2 = (bf16[4,2,2,2,64,256]{5,4,3,2,1,0:T(8,128)(2,1)S(1)}, bf16[4,2,2,2,64,256]{5,4,3,2,1,0:T(8,128)(2,1)}, u32[]{:S(2)}) copy-start(bf16[4,2,2,2,64,256]{5,4,3,2,1,0:T(8,128)(2,1)} %get-tuple-element.27) | copy-start | bytes 3145732
  125.7 3.6 %copy-start.4 = (bf16[2,256,768]{2,1,0:T(8,128)(2,1)S(1)}, bf16[2,256,768]{2,1,0:T(8,128)(2,1)}, u32[]{:S(2)}) copy-start(bf16[2,256,768]{2,1,0:T(8,128)(2,1)} %get-tuple-element.31) | copy-start | bytes 2359300
  126.7 3.6 %copy-start.1 = (bf16[2,256,1024]{2,1,0:T(8,128)(2,1)S(1)}, bf16[2,256,1024]{2,1,0:T(8,128)(2,1)}, u32[]{:S(2)}) copy-start(bf16[2,256,1024]{2,1,0:T(8,128)(2,1)} %get-tuple-element.33) | copy-start | bytes 3145732
  130.2 1.6 copy-start

commit v2 on v1

v2 whole, which is shorter than its diff:
```python
import functools
import jax
import jax.numpy as jnp
from jax import lax
from jax.experimental import pallas as pl
from jax.experimental.pallas import tpu as pltpu
from jax.sharding import PartitionSpec as P

HEAD = 32
STRIPE = 7
HP = 28
WP = 42
HEADS = 4
GROUP = 8
WG = WP // STRIPE
ROWS = HP * WG * GROUP
CHUNK = STRIPE * WG * GROUP
TALL = HP * GROUP
WIDE_R = 384
WIDE_C = 256
BF = jnp.bfloat16
F32 = jnp.float32
eps_norm = 1e-05
masked_score = -1000000000.0
LOG2E = 1.4426950408889634
LN2 = 0.6931471805599453
SCALE = HEAD ** (-0.5)
NN = (((1,), (0,)), ((), ()))
NT = (((1,), (1,)), ((), ()))
TN = (((0,), (0,)), ((), ()))


def mm(a, b, dims=NN):
    return lax.dot_general(a, b, dims, preferred_element_type=F32)


def iota(shape, dim):
    return lax.broadcasted_iota(jnp.int32, shape, dim)


def span(index, size):
    return pl.ds(pl.multiple_of(index * size, size), size)


def pad_groups(src, dst, scale=None):
    def body(j, carry):
        block = src[pl.ds(pl.multiple_of(j * 56, 8), 56), :].astype(F32).reshape(7, 8, -1)
        place = iota((8, block.shape[-1]), 0)
        for u in range(8):
            if u == 0:
                group = block[0]
            elif u == 7:
                group = pltpu.roll(block[6], 7, 0)
            else:
                group = jnp.where(
                    place < u, pltpu.roll(block[u - 1], u, 0), pltpu.roll(block[u], u, 0)
                )
            group = jnp.where(place < 7, group, 0.0)
            dst[pl.ds(pl.multiple_of(j * 64 + u * 8, 8), 8), :] = group
        return carry

    lax.fori_loop(0, ROWS // 64, body, 0)


def drop_groups(src, dst):
    def body(j, carry):
        block = src[pl.ds(pl.multiple_of(j * 64, 8), 64), :].reshape(8, 8, -1)
        place = iota((8, block.shape[-1]), 0)
        for t in range(7):
            lower = block[t] if t == 0 else pltpu.roll(block[t], 8 - t, 0)
            upper = pltpu.roll(block[t + 1], 7 - t, 0)
            dst[pl.ds(pl.multiple_of(j * 56 + t * 8, 8), 8), :] = jnp.where(
                place <= 6 - t, lower, upper
            )
        return carry

    lax.fori_loop(0, ROWS // 64, body, 0)


def norm_parts(x):
    centre = jnp.mean(x, axis=-1, keepdims=True)
    centred = x - centre
    rate = lax.rsqrt(jnp.mean(centred * centred, axis=-1, keepdims=True) + eps_norm)
    return centred * rate, rate


def norm_back(d_n, xhat, rate, gain):
    e = d_n * gain
    return rate * (
        e
        - jnp.mean(e, axis=-1, keepdims=True)
        - xhat * jnp.mean(e * xhat, axis=-1, keepdims=True)
    )


def colsum(x):
    return jnp.sum(x, axis=0, keepdims=True)


def rows_live(stripe, h, w, lanes):
    shape = (STRIPE, WG * GROUP, lanes)
    row = iota(shape, 0) + stripe * STRIPE
    place = iota(shape, 1)
    within = place & 7
    col = (place >> 3) * STRIPE + within
    live = (row < h) & (col < w) & (within < STRIPE)
    return jnp.where(live, 1.0, 0.0).reshape(CHUNK, lanes)


def cols_live(stripe, h, w, lanes):
    shape = (HP, GROUP, lanes)
    row = iota(shape, 0)
    within = iota(shape, 1)
    live = (row < h) & (within + stripe * STRIPE < w) & (within < STRIPE)
    return jnp.where(live, 1.0, 0.0).reshape(TALL, lanes)


def with_mask(keys, live):
    lane = iota(live.shape, 1)
    extra = jnp.where(lane == 0, jnp.where(live > 0.0, 0.0, masked_score), 0.0)
    return jnp.concatenate([keys, extra.astype(BF)], axis=-1)


def stack_heads(ref, x, wide):
    length = x.shape[0]
    lane = iota(x.shape, 1)
    for h in range(HEADS):
        kept = jnp.where((lane >> 5) == h, x, jnp.zeros_like(x))
        ref[h * wide : h * wide + length, 0:128] = kept


def widen(x, wide):
    length = x.shape[0]
    return jnp.concatenate([x, jnp.zeros((wide - length, x.shape[1]), x.dtype)], axis=0)


def attend(q, k_mask, vm, qs, out_t, lse, stripe, wide):
    length = q.shape[0]
    stack_heads(qs, q, wide)
    scores = mm(k_mask, qs[0 : HEADS * wide, :], NT)
    v_t = widen(vm.astype(F32), wide).T.astype(BF)[:, 0:length]
    for h in range(HEADS):
        s = scores[:, h * wide : (h + 1) * wide]
        top = jnp.max(s, axis=0, keepdims=True)
        p = jnp.exp2(s - top)
        total = jnp.sum(p, axis=0, keepdims=True)
        o = mm(v_t[HEAD * h : HEAD * (h + 1), :], p.astype(BF))
        out_t[stripe, HEAD * h : HEAD * (h + 1), :] = o / total
        lse[stripe, h : h + 1, :] = top + jnp.log2(total)


def attend_back(q, k, k_mask, vm, da, qs, ds_stack, p_all, g_all, out_t, lse, stripe, wide):
    length = q.shape[0]
    stack_heads(qs, q, wide)
    stack_heads(ds_stack, da, wide)
    da_t = widen(da.astype(F32), wide).T
    k_t = widen(k.astype(F32), wide).T.astype(BF)[:, 0:length]
    weighted = da_t * out_t[stripe]
    dq_t = []
    scores = mm(k_mask, qs[0 : HEADS * wide, :], NT)
    d_probs = mm(vm, ds_stack[0 : HEADS * wide, :], NT)
    for h in range(HEADS):
        lanes = slice(h * wide, (h + 1) * wide)
        inner = jnp.sum(weighted[HEAD * h : HEAD * (h + 1), :], axis=0, keepdims=True)
        p = jnp.exp2(scores[:, lanes] - lse[stripe, h : h + 1, :])
        g = (p * (d_probs[:, lanes] - inner)).astype(BF)
        p_all[0:length, lanes] = p.astype(BF)
        g_all[0:length, lanes] = g
        dq_t.append(mm(k_t[HEAD * h : HEAD * (h + 1), :], g))
    dv = mm(p_all[0:length, 0 : HEADS * wide], ds_stack[0 : HEADS * wide, :])
    dk = mm(g_all[0:length, 0 : HEADS * wide], qs[0 : HEADS * wide, 0:128]) * LN2
    dq = jnp.concatenate(dq_t, axis=0).T[0:length, :] * SCALE
    return dq, dk, dv


def earlier(x):
    return jnp.concatenate([jnp.zeros_like(x[:1]), x[:-1]], axis=0)


def later(x):
    return jnp.concatenate([x[1:], jnp.zeros_like(x[:1])], axis=0)


def row_neighbours(x):
    groups = x.reshape(STRIPE * WG, GROUP, 128)
    place = iota(groups.shape, 1)
    edge = jnp.zeros((STRIPE, 1, GROUP, 128), x.dtype)
    far = pltpu.roll(groups, 2, 1).reshape(STRIPE, WG, GROUP, 128)
    far = jnp.concatenate([edge, far[:, :-1]], axis=1).reshape(groups.shape)
    left = jnp.where(place == 0, far, pltpu.roll(groups, 1, 1))
    far = pltpu.roll(groups, 6, 1).reshape(STRIPE, WG, GROUP, 128)
    far = jnp.concatenate([far[:, 1:], edge], axis=1).reshape(groups.shape)
    right = jnp.where(place == 6, far, pltpu.roll(groups, 7, 1))
    shape = (STRIPE, WG * GROUP, 128)
    return left.reshape(shape), x.reshape(shape), right.reshape(shape)


def col_neighbours(x):
    cells = x.reshape(HP, GROUP, 128)
    return pltpu.roll(cells, 1, 1), cells, pltpu.roll(cells, 7, 1)


def position(near, taps):
    rows = [sum(taps[3 * a + b] * near[b] for b in range(3)) for a in range(3)]
    return earlier(rows[0]) + rows[1] + later(rows[2])


def position_back(near, taps):
    rows = [sum(taps[3 * a + b] * near[2 - b] for b in range(3)) for a in range(3)]
    return later(rows[0]) + rows[1] + earlier(rows[2])


def tap_sums(da, near):
    sums = []
    for a in range(3):
        for b in range(3):
            x = near[b]
            x = earlier(x) if a == 0 else later(x) if a == 2 else x
            sums.append(colsum((da * x).reshape(-1, 128)))
    return sums


def forward_layer(l, h, w, wt, r, at):
    vec = r.vec[l]

    def project(s, carry):
        rows = span(s, CHUNK)
        xhat, rate = norm_parts(r.x[l, rows, :])
        n1 = (xhat * vec[0:1] + vec[1:2]).astype(BF)
        r.n1[l, rows, :] = n1
        live = rows_live(s, h, w, 256)
        mixed = mm(n1, wt.qkv(l))
        q = (mixed[:, 0:256] + vec[2:3]) * (SCALE * LOG2E)
        k = mixed[:, 256:512]
        v = (mixed[:, 512:768] + vec[3:4]) * live
        for i, part in enumerate((q, k, v)):
            r.row[i, l, rows, :] = part[:, 0:128].astype(BF)
            cells = part[:, 128:256].reshape(STRIPE, WG, GROUP, 128)
            for c in range(STRIPE):
                r.turn[i, :, s * STRIPE + c] = cells[c]
        return carry

    lax.fori_loop(0, HP // STRIPE, project, 0)
    at("projected", l)

    def horizontal(s, carry):
        rows = span(s, CHUNK)
        q, k, v = (r.row[i, l, rows, :] for i in range(3))
        attend(q, with_mask(k, rows_live(s, h, w, 128)), v, r.qs_r, r.o_r.at[l], r.lse_r.at[l], s, WIDE_R)
        near = row_neighbours(v.astype(F32))
        taps = vec[9:18, 0:128]
        pos = position(near, [taps[i : i + 1] for i in range(9)]) + vec[8:9, 0:128]
        o = r.o_r[l, s].T[0:CHUNK, :]
        r.a[l, rows, 0:128] = (o + pos.reshape(CHUNK, 128)).astype(BF)
        return carry

    lax.fori_loop(0, HP // STRIPE, horizontal, 0)
    at("horizontal", l)

    def vertical(s, carry):
        q, k, v = (r.turn[i, s].reshape(TALL, 128).astype(BF) for i in range(3))
        for i, part in enumerate((q, k, v)):
            r.col[i, l, s] = part
        attend(q, with_mask(k, cols_live(s, h, w, 128)), v, r.qs_c, r.o_c.at[l], r.lse_c.at[l], s, WIDE_C)
        near = col_neighbours(v.astype(F32))
        taps = vec[9:18, 128:256]
        pos = position(near, [taps[i : i + 1] for i in range(9)]) + vec[8:9, 128:256]
        o = r.o_c[l, s].T[0:TALL, :]
        r.back[0, :, s] = o.reshape(HP, GROUP, 128) + pos
        return carry

    lax.fori_loop(0, WG, vertical, 0)
    at("vertical", l)

    def feed(s, carry):
        rows = span(s, CHUNK)
        turned = r.back[0, pl.ds(s * STRIPE, STRIPE)].reshape(CHUNK, 128).astype(BF)
        r.a[l, rows, 128:256] = turned
        x1 = r.x[l, rows, :] + mm(r.a[l, rows, :], wt.proj(l)) + vec[4:5]
        r.after[l, rows, :] = x1
        xhat, rate = norm_parts(x1)
        n2 = (xhat * vec[5:6] + vec[6:7]).astype(BF)
        r.n2[l, rows, :] = n2
        hidden_bias = jnp.concatenate([vec[18 + j : 19 + j] for j in range(4)], axis=1)
        hid = mm(n2, wt.fc1(l)) + hidden_bias
        phi = 0.5 * lax.erf(hid * 0.7071067811865476) + 0.5
        slope = phi + hid * (jnp.exp2(hid * hid * (-0.5 * LOG2E)) * 0.3989422804014327)
        act = (hid * phi).astype(BF)
        r.act[l, rows, :] = act
        r.slope[l, rows, :] = slope.astype(BF)
        r.x[l + 1, rows, :] = x1 + mm(act, wt.fc2(l)) + vec[7:8]
        return carry

    lax.fori_loop(0, HP // STRIPE, feed, 0)
    at("fed", l)


def backward_layer(l, h, w, wt, r, out, at):
    vec = r.vec[l]
    r.gv[...] = jnp.zeros_like(r.gv)

    def add(row, value):
        r.gv[row : row + 1, :] += value

    def feed(s, carry):
        rows = span(s, CHUNK)
        g = r.g[rows, :]
        add(7, colsum(g))
        gy = g.astype(BF)
        r.gy[rows, :] = gy
        d_hid = mm(gy, wt.fc2(l), NT) * r.slope[l, rows, :].astype(F32)
        for j in range(4):
            add(18 + j, colsum(d_hid[:, 256 * j : 256 * (j + 1)]))
        dh = d_hid.astype(BF)
        r.slope[l, rows, :] = dh
        d_n2 = mm(dh, wt.fc1(l), NT)
        xhat, rate = norm_parts(r.after[l, rows, :])
        add(5, colsum(d_n2 * xhat))
        add(6, colsum(d_n2))
        g1 = g + norm_back(d_n2, xhat, rate, vec[5:6])
        r.g[rows, :] = g1
        add(4, colsum(g1))
        g1_low = g1.astype(BF)
        r.g1[rows, :] = g1_low
        da = mm(g1_low, wt.proj(l), NT)
        r.da_r[rows, :] = da[:, 0:128].astype(BF)
        add(8, colsum(da.astype(BF).astype(F32)))
        cells = da[:, 128:256].reshape(STRIPE, WG, GROUP, 128)
        for c in range(STRIPE):
            r.turn[0, :, s * STRIPE + c] = cells[c]
        return carry

    lax.fori_loop(0, HP // STRIPE, feed, 0)
    at("back fed", l)
    out.put("fc2", l, mm(r.act[l], r.gy[...], TN))
    out.put("fc1", l, mm(r.n2[l], r.slope[l], TN))
    out.put("proj", l, mm(r.a[l], r.g1[...], TN))
    at("back summed", l)

    def horizontal(s, carry):
        rows = span(s, CHUNK)
        q, k, v = (r.row[i, l, rows, :] for i in range(3))
        da = r.da_r[rows, :]
        live = rows_live(s, h, w, 128)
        dq, dk, dv = attend_back(
            q, k, with_mask(k, live), v, da, r.qs_r, r.ds_r, r.p_all, r.g_all,
            r.o_r.at[l], r.lse_r.at[l], s, WIDE_R,
        )
        taps = [vec[9 + i : 10 + i, 0:128] for i in range(9)]
        da_near = row_neighbours(da.astype(F32))
        dv = (dv + position_back(da_near, taps).reshape(CHUNK, 128)) * live
        sums = tap_sums(da_near[1], row_neighbours(v.astype(F32)))
        for i in range(9):
            r.gv[9 + i : 10 + i, 0:128] += sums[i]
        r.gv[2:3, 0:128] += colsum(dq)
        r.gv[3:4, 0:128] += colsum(dv)
        for i, part in enumerate((dq, dk, dv)):
            r.dqkv_r[rows, 128 * i : 128 * i + 128] = part.astype(BF)
        return carry

    lax.fori_loop(0, HP // STRIPE, horizontal, 0)
    out.put("qkv_r", l, mm(r.n1[l], r.dqkv_r[...], TN))
    at("back horizontal", l)

    def vertical(s, carry):
        q, k, v = (r.col[i, l, s] for i in range(3))
        da = r.turn[0, s].reshape(TALL, 128).astype(BF)
        live = cols_live(s, h, w, 128)
        dq, dk, dv = attend_back(
            q, k, with_mask(k, live), v, da, r.qs_c, r.ds_c, r.p_all, r.g_all,
            r.o_c.at[l], r.lse_c.at[l], s, WIDE_C,
        )
        taps = [vec[9 + i : 10 + i, 128:256] for i in range(9)]
        da_near = col_neighbours(da.astype(F32))
        dv = (dv + position_back(da_near, taps).reshape(TALL, 128)) * live
        sums = tap_sums(da_near[1], col_neighbours(v.astype(F32)))
        for i in range(9):
            r.gv[9 + i : 10 + i, 128:256] += sums[i]
        r.gv[2:3, 128:256] += colsum(dq)
        r.gv[3:4, 128:256] += colsum(dv)
        for i, part in enumerate((dq, dk, dv)):
            r.back[i, :, s] = part.reshape(HP, GROUP, 128)
        return carry

    lax.fori_loop(0, WG, vertical, 0)

    def turn(s, carry):
        rows = span(s, CHUNK)
        for i in range(3):
            cells = r.back[i, pl.ds(s * STRIPE, STRIPE)].reshape(CHUNK, 128)
            r.dqkv_c[rows, 128 * i : 128 * i + 128] = cells.astype(BF)
        return carry

    lax.fori_loop(0, HP // STRIPE, turn, 0)
    out.put("qkv_c", l, mm(r.n1[l], r.dqkv_c[...], TN))
    at("back vertical", l)

    def mix(s, carry):
        rows = span(s, CHUNK)
        parts = []
        for i in range(3):
            lanes = slice(128 * i, 128 * i + 128)
            parts += [r.dqkv_r[rows, lanes], r.dqkv_c[rows, lanes]]
        d_n1 = mm(jnp.concatenate(parts, axis=1), wt.qkv(l), NT)
        xhat, rate = norm_parts(r.x[l, rows, :])
        add(0, colsum(d_n1 * xhat))
        add(1, colsum(d_n1))
        r.g[rows, :] += norm_back(d_n1, xhat, rate, vec[0:1])
        return carry

    lax.fori_loop(0, HP // STRIPE, mix, 0)
    out.put("vec", l, r.gv[...].T)
    at("back mixed", l)


MESH = pl.DeviceIdType.MESH


class Grid:
    def __init__(self, shards, copies):
        self.cores = 2
        self.zs = 4
        self.xs = shards // 8
        self.copies = copies
        index = lax.axis_index("fsdp")
        self.rep = lax.axis_index("rep")
        self.core = lax.rem(index, 2)
        chip = lax.div(index, 2)
        self.x = lax.rem(chip, self.xs)
        self.z = lax.div(chip, self.xs)

    def at(self, z, x, core):
        return {"fsdp": (z * self.xs + x) * 2 + core, "rep": self.rep}

    def z_peers(self):
        return [(d, lax.rem(self.z + d, self.zs)) for d in range(1, self.zs)]

    def x_peers(self):
        return [(d, lax.rem(self.x + d, self.xs)) for d in range(1, self.xs)]

    def rep_peers(self):
        return [(d, lax.rem(self.rep + d, self.copies)) for d in range(1, self.copies)]

    def z_device(self, z):
        return self.at(z, self.x, self.core)

    def x_device(self, x):
        return self.at(self.z, x, self.core)

    def sibling(self):
        return self.at(self.z, self.x, 1 - self.core)

    def rep_device(self, rep):
        index = (self.z * self.xs + self.x) * 2 + self.core
        return {"fsdp": index, "rep": rep}

    def steps(self):
        return self.zs - 1 + self.xs - 1 + 1

    def peers(self):
        devices = [self.z_device(z) for _, z in self.z_peers()]
        devices += [self.x_device(x) for _, x in self.x_peers()] + [self.sibling()]
        return devices + [self.rep_device(rep) for _, rep in self.rep_peers()]

    def signal(self):
        for device in self.peers():
            pl.semaphore_signal(
                pltpu.get_barrier_semaphore(), inc=1, device_id=device, device_id_type=MESH
            )

    def wait(self):
        pl.semaphore_wait(pltpu.get_barrier_semaphore(), len(self.peers()))


def remote(src, dst, send, recv, device):
    return pltpu.make_async_remote_copy(
        src_ref=src, dst_ref=dst, send_sem=send, recv_sem=recv,
        device_id=device, device_id_type=MESH,
    )


class Gather:
    def __init__(self, grid, own, full, sems, row):
        self.grid, self.own, self.full = grid, own, full
        send, recv, local = sems
        g = grid
        mine = full.at[g.z, g.x, g.core]
        self.keep = pltpu.make_async_copy(own, mine, local.at[row])
        self.along_z = [
            remote(own, mine, send.at[row, d - 1], recv.at[row, d - 1], g.z_device(z))
            for d, z in g.z_peers()
        ]
        base = g.zs - 2
        lane = full.at[:, g.x, g.core]
        self.along_x = [
            remote(lane, lane, send.at[row, base + d], recv.at[row, base + d], g.x_device(x))
            for d, x in g.x_peers()
        ]
        last = g.zs - 1 + g.xs - 1
        plane = full.at[:, :, g.core]
        self.across = remote(plane, plane, send.at[row, last], recv.at[row, last], g.sibling())

    def begin(self):
        self.keep.start()
        for copy in self.along_z:
            copy.start()

    def second(self):
        self.keep.wait()
        for copy in self.along_z:
            copy.wait_recv()
        for copy in self.along_x:
            copy.start()

    def third(self):
        for copy in self.along_x:
            copy.wait_recv()
        self.across.start()

    def finish(self):
        self.across.wait_recv()

    def drain(self):
        for copy in self.along_z + self.along_x + [self.across]:
            copy.wait_send()


class Reduce:
    def __init__(self, grid, part, bufs, out, sems, row):
        self.grid, self.part, self.out = grid, part, out
        send, recv = sems
        g = grid
        self.from_sibling, self.chip, self.from_x, self.line, self.from_z, self.own, self.from_rep = bufs
        self.across = remote(
            part.at[:, :, 1 - g.core], self.from_sibling, send.at[row, 0], recv.at[row, 0], g.sibling()
        )
        self.along_x = [
            remote(self.chip.at[:, x], self.from_x.at[d - 1], send.at[row, d], recv.at[row, d], g.x_device(x))
            for d, x in g.x_peers()
        ]
        base = g.xs - 1
        self.along_z = [
            remote(self.line.at[z], self.from_z.at[d - 1], send.at[row, base + d], recv.at[row, base + d], g.z_device(z))
            for d, z in g.z_peers()
        ]
        base += g.zs - 1
        self.along_rep = [
            remote(self.own, self.from_rep.at[d - 1], send.at[row, base + d], recv.at[row, base + d], g.rep_device(rep))
            for d, rep in g.rep_peers()
        ]

    def begin(self):
        self.across.start()

    def second(self):
        self.across.wait_recv()
        mine = self.part[:, :, self.grid.core].astype(F32)
        self.chip[...] = (mine + self.from_sibling[...].astype(F32)).astype(BF)
        for copy in self.along_x:
            copy.start()

    def third(self):
        for copy in self.along_x:
            copy.wait_recv()
        total = self.chip[:, self.grid.x].astype(F32)
        for d, _ in self.grid.x_peers():
            total = total + self.from_x[d - 1].astype(F32)
        self.line[...] = total.astype(BF)
        for copy in self.along_z:
            copy.start()

    def fourth(self):
        for copy in self.along_z:
            copy.wait_recv()
        total = self.line[self.grid.z].astype(F32)
        for d, _ in self.grid.z_peers():
            total = total + self.from_z[d - 1].astype(F32)
        self.own[...] = total.astype(BF)
        for copy in self.along_rep:
            copy.start()

    def finish(self):
        for copy in self.along_rep:
            copy.wait_recv()
        total = self.own[...].astype(F32)
        for d, _ in self.grid.rep_peers():
            total = total + self.from_rep[d - 1].astype(F32)
        out, half = self.out
        if half is None:
            out[...] = total
            return
        for i in range(3):
            lanes = slice(256 * i + 128 * half, 256 * i + 128 * half + 128)
            out[:, lanes] = total[:, 128 * i : 128 * i + 128]

    def drain(self):
        for copy in [self.across] + self.along_x + self.along_z + self.along_rep:
            copy.wait_send()


def reduce_bufs(zs, xs, copies, shape):
    dims = [(zs, xs), (zs, xs), (max(xs - 1, 1), zs), (zs,), (zs - 1,), (), (max(copies - 1, 1),)]
    return [pltpu.VMEM(d + tuple(shape), BF) for d in dims]


SCRATCH = dict(
    x=((3, ROWS, 256), F32),
    after=((2, ROWS, 256), F32),
    n1=((2, ROWS, 256), BF),
    n2=((2, ROWS, 256), BF),
    a=((2, ROWS, 256), BF),
    act=((2, ROWS, 1024), BF),
    slope=((2, ROWS, 1024), BF),
    row=((3, 2, ROWS, 128), BF),
    col=((3, 2, WG, TALL, 128), BF),
    turn=((3, WG, HP, GROUP, 128), F32),
    back=((3, HP, WG, GROUP, 128), F32),
    o_r=((2, HP // STRIPE, 128, WIDE_R), F32),
    o_c=((2, WG, 128, WIDE_C), F32),
    lse_r=((2, HP // STRIPE, 8, WIDE_R), F32),
    lse_c=((2, WG, 8, WIDE_C), F32),
    qs_r=((HEADS * WIDE_R, 256), BF),
    qs_c=((HEADS * WIDE_C, 256), BF),
    ds_r=((HEADS * WIDE_R, 128), BF),
    ds_c=((HEADS * WIDE_C, 128), BF),
    p_all=((CHUNK, HEADS * WIDE_R), BF),
    g_all=((CHUNK, HEADS * WIDE_R), BF),
    g=((ROWS, 256), F32),
    gy=((ROWS, 256), BF),
    g1=((ROWS, 256), BF),
    da_r=((ROWS, 128), BF),
    dqkv_r=((ROWS, 384), BF),
    dqkv_c=((ROWS, 384), BF),
    gv=((128, 256), F32),
    vec=((2, 128, 256), F32),
)


class Refs:
    def __init__(self, names, refs):
        self.__dict__.update(zip(names, refs))


MATRICES = ("qkv", "proj", "fc1", "fc2")
SUMMED = ("fc2", "fc1", "proj", "qkv_r", "qkv_c", "vec")


class Weights:
    def __init__(self, full):
        self.full = full

    def whole(self, name, l):
        value = self.full[name][l]
        return value.reshape(-1, value.shape[-1])

    def qkv(self, l):
        return self.whole("qkv", l)

    def proj(self, l):
        return self.whole("proj", l)

    def fc1(self, l):
        return self.whole("fc1", l)

    def fc2(self, l):
        return self.whole("fc2", l)


class Queue:
    def __init__(self, moves):
        self.moves = moves
        self.under_way = []

    def begin(self, *parts):
        for part in parts:
            getattr(part, self.moves[0])()
        self.under_way += [[part, 1] for part in parts]

    def advance(self, parts=None):
        for entry in self.under_way:
            if (parts is None or entry[0] in parts) and entry[1] < len(self.moves):
                getattr(entry[0], self.moves[entry[1]])()
                entry[1] += 1

    def complete(self, parts=None):
        while any(
            e[1] < len(self.moves) for e in self.under_way if parts is None or e[0] in parts
        ):
            self.advance(parts)

    def drain(self):
        for part, _ in self.under_way:
            part.drain()


class Gradients:
    def __init__(self, parts):
        self.parts = parts

    def put(self, name, l, value):
        ref = self.parts[name, l]
        ref[...] = value.astype(BF).reshape(ref.shape)


def plan(shards, copies, layers, width, hidden):
    zs, xs = 4, shards // 8
    place = (zs, xs, 2)
    d, f = width // shards, hidden // shards
    shapes = {k: pltpu.VMEM(*v) for k, v in SCRATCH.items()}
    own = dict(qkv=(d, 3 * width), proj=(d, width), fc1=(d, hidden), fc2=(f, width))
    for name in MATRICES:
        shapes["full", name] = pltpu.VMEM((layers,) + place + own[name], BF)
    shapes["own", "vec"] = pltpu.VMEM((layers, d, 128), F32)
    shapes["full", "vec"] = pltpu.VMEM(place + (layers, d, 128), F32)
    gathers = len(MATRICES) * layers + 1
    hops = zs - 1 + xs - 1 + 1
    for name in ("gather send", "gather recv"):
        shapes[name] = pltpu.SemaphoreType.DMA((gathers, hops))
    shapes["gather local"] = pltpu.SemaphoreType.DMA((gathers,))
    own.update(qkv_r=(d, 3 * width // 2), qkv_c=(d, 3 * width // 2), vec=(d, 128))
    sums = len(SUMMED) * layers
    hops += copies - 1
    for l in range(layers):
        for name in SUMMED:
            shapes["part", name, l] = pltpu.VMEM(place + own[name], BF)
            for i, buf in enumerate(reduce_bufs(zs, xs, copies, own[name])):
                shapes["buf", name, l, i] = buf
    for name in ("sum send", "sum recv"):
        shapes[name] = pltpu.SemaphoreType.DMA((sums, hops))
    shapes["out"] = pltpu.SemaphoreType.DMA((2,))
    return shapes


def step_kernel(shards, copies, names, *refs):
    h_ref, w_ref, tok, cot = refs[:4]
    own = dict(zip(MATRICES, refs[4:8]))
    vec_own = refs[8]
    y_ref, gt_ref = refs[9:11]
    outs = dict(zip(MATRICES + ("vec",), refs[11:16]))
    s = dict(zip(names, refs[16:]))
    r = Refs(SCRATCH, [s[k] for k in SCRATCH])
    layers = own["qkv"].shape[0]
    grid = Grid(shards, copies)
    grid.signal()
    h, w = h_ref[0], w_ref[0]

    held = vec_own.shape[1]
    eye = (iota((held, 128), 0) == iota((held, 128), 1)).astype(F32).astype(BF)
    for l in range(layers):
        s["own", "vec"][l] = mm(vec_own[l], eye, TN)
    sems = [s["gather send"], s["gather recv"], s["gather local"]]
    order = [(name, l) for l in range(layers) for name in MATRICES]
    gathers = {
        (name, l): Gather(grid, own[name].at[l], s["full", name].at[l], sems, i)
        for i, (name, l) in enumerate(order)
    }
    gathers["vec"] = Gather(grid, s["own", "vec"], s["full", "vec"], sems, len(order))
    wt = Weights({name: s["full", name] for name in MATRICES})
    gather_queue = Queue(("begin", "second", "third", "finish"))
    first = [gathers["qkv", 0], gathers["vec"]]
    rest = [gathers[key] for key in order if key != ("qkv", 0)]
    early, late = rest[:3], rest[3:]

    grid.wait()
    gather_queue.begin(*first)
    for stack in (r.qs_r, r.qs_c):
        stack[...] = jnp.where(iota(stack.shape, 1) == 128, 1.0, 0.0).astype(BF)
    for stack in (r.ds_r, r.ds_c):
        stack[...] = jnp.zeros_like(stack)
    r.gv[...] = jnp.zeros_like(r.gv)
    pad_groups(tok, r.x.at[0])
    pad_groups(cot, r.g)
    gather_queue.advance(first)
    gather_queue.begin(*early)
    gather_queue.begin(*late)
    gather_queue.complete(first)
    for l in range(layers):
        value = s["full", "vec"][:, :, :, l]
        r.vec[l] = value.reshape(-1, 128).T

    def after_forward(point, l):
        if l == 0:
            if point == "horizontal":
                gather_queue.advance(early)
            if point == "vertical":
                gather_queue.complete(early)
                gather_queue.advance(late)
            if point == "fed":
                gather_queue.complete(late)

    for l in range(layers):
        forward_layer(l, h, w, wt, r, after_forward)
    y_copy = pltpu.make_async_copy(r.x.at[layers], y_ref, s["out"].at[0])
    y_copy.start()

    sum_queue = Queue(("begin", "second", "third", "fourth", "finish"))
    width = 128
    sums = {}
    for l in range(layers):
        for i, name in enumerate(SUMMED):
            if name in ("qkv_r", "qkv_c"):
                out = (outs["qkv"].at[l], 0 if name == "qkv_r" else 1)
            else:
                out = (outs[name].at[l], None)
            bufs = [s["buf", name, l, j] for j in range(7)]
            row = l * len(SUMMED) + i
            sums[name, l] = Reduce(
                grid, s["part", name, l], bufs, out, [s["sum send"], s["sum recv"]], row
            )
    gradients = Gradients({(name, l): s["part", name, l] for l in range(layers) for name in SUMMED})

    def after_backward(point, l):
        if point == "back summed":
            sum_queue.advance()
            sum_queue.begin(*(sums[name, l] for name in ("fc2", "fc1", "proj")))
        if point == "back horizontal":
            sum_queue.advance()
            sum_queue.begin(sums["qkv_r", l])
        if point == "back vertical":
            sum_queue.advance()
            sum_queue.begin(sums["qkv_c", l])
        if point == "back mixed":
            sum_queue.advance()
            sum_queue.begin(sums["vec", l])

    for l in reversed(range(layers)):
        backward_layer(l, h, w, wt, r, gradients, after_backward)
    g_copy = pltpu.make_async_copy(r.g, gt_ref, s["out"].at[1])
    g_copy.start()
    sum_queue.complete()
    gather_queue.drain()
    sum_queue.drain()
    y_copy.wait()
    g_copy.wait()


def finish_kernel(count, *refs):
    y, g = refs[:2]
    drop_groups(y, refs[count])
    drop_groups(g, refs[count + 1])
    for i in range(2, count - 1):
        refs[count + i][...] = refs[i][...]
    vec, out = refs[count - 1], refs[2 * count - 1]
    layers, held, places = out.shape
    for l in range(layers):
        turned = widen(vec[l], 128).T
        out[l] = turned[0:held, 0:places]


def shards_step(shards, copies, tokens, heights, widths, w_qkv, w_proj, w_fc1, w_fc2, vectors, cotangent):
    layers, _, hidden = w_fc1.shape
    count, width = tokens.shape
    vmem = pl.BlockSpec(memory_space=pltpu.VMEM)
    smem = pl.BlockSpec(memory_space=pltpu.SMEM)
    hbm = pl.BlockSpec(memory_space=pl.ANY)
    scratch = plan(shards, copies, layers, width, hidden)
    matrices = [w_qkv, w_proj, w_fc1, w_fc2]
    results = [jax.ShapeDtypeStruct((ROWS, width), F32)] * 2
    results += [jax.ShapeDtypeStruct(m.shape, F32) for m in matrices]
    results += [jax.ShapeDtypeStruct((layers, width // shards, 128), F32)]
    raw = pl.pallas_call(
        functools.partial(step_kernel, shards, copies, list(scratch)),
        out_shape=results,
        in_specs=[smem, smem, vmem, vmem] + [vmem] * 5,
        out_specs=[hbm, hbm] + [vmem] * 5,
        scratch_shapes=list(scratch.values()),
        compiler_params=pltpu.CompilerParams(
            collective_id=0, has_side_effects=True, vmem_limit_bytes=67043328
        ),
    )(heights, widths, tokens, cotangent, *matrices, vectors)
    final = [jax.ShapeDtypeStruct((count, width), F32)] * 2
    final += [jax.ShapeDtypeStruct(m.shape, F32) for m in matrices + [vectors]]
    return tuple(
        pl.pallas_call(
            functools.partial(finish_kernel, len(raw)),
            out_shape=final,
            in_specs=[vmem] * len(raw),
            out_specs=[vmem] * len(raw),
            compiler_params=pltpu.CompilerParams(vmem_limit_bytes=67043328),
        )(*raw)
    )


def solution(mesh):
    images = P(("fsdp", "rep"), None)
    weights = P(None, "fsdp", None)
    return jax.shard_map(
        functools.partial(shards_step, mesh.shape["fsdp"], mesh.shape["rep"]),
        mesh=mesh,
        in_specs=(images, P(("fsdp", "rep")), P(("fsdp", "rep")), weights, weights, weights, weights, P(None, None, "fsdp"), images),
        out_specs=(images, images, weights, weights, weights, weights, P(None, None, "fsdp")),
        check_vma=False,
    )
```

time: 178 us -> 140 us (0.79)
  Pallas kernels: 154 us -> 135 us
  local copies, waits for them, and re-layouts: 20.8 us -> 2.81 us
    pallas_call x3 -> x2, Pallas kernels: 154 us -> 135 us  [the longest x1 131 us: shards_step(): pl.pallas_call(functools.partial(step_kernel, shards, copies, list(scratc...]
    reshape x9 -> x0, local copies, waits for them, and re-layouts: 10.8 us -> none  [the longest x5 5.79 us: shards_step(): m = m.reshape(layers, shards, -1, m.shape[-1]).transpose(1, 0, 2, 3)]
    unnamed x19 -> x1, local copies, waits for them, and re-layouts: 7.9 us -> 1.39 us
where the time goes in v2:
time: 140 us
  Pallas kernels  135 us (96%)
  local copies, waits for them, and re-layouts  2.81 us (2%)
  between operations  1.93 us (1%)
    pallas_call x1, Pallas kernels, shards_step(): pl.pallas_call(functools.partial(step_kernel, shards, copies, list(scratc...  131 us
    pallas_call x1, Pallas kernels, shards_step(): pl.pallas_call(functools.partial(finish_kernel, len(raw)), out_shape=fina...  3.96 us

profile of v2, /device:TPU:0, one launch (start us, length us, event | category | flops | bytes accessed | tf_op | source)
XLA Modules:
  0.0 139.8 jit_solution(6260838865079110100)
XLA Ops:
  1.9 1.4 copy.16.refs_8_
  3.3 131.1 %shard_map.144 = (f32[1344,256]{1,0:T(8,128)}, f32[1344,256]{1,0:T(8,128)}, f32[2,16,768]{2,1,0:T(8,128)}, f32[2,16,256]{2,1,0:T(8,128)}, f32[2,16,1024]{2,1,0:T...) custom-call(s32[1]{0:T(128)S(6)} %copy.18.refs_0_, s32[1]{0:T(128)S(6)} %copy.19.refs_1_, ...), custom_call_target="tpu_custom_call" | custom-call | tf_op jit(solution)/shard_map/pallas_call | solution.py:861
  134.4 4.0 %shard_map.145 = (f32[1176,256]{1,0:T(8,128)}, f32[1176,256]{1,0:T(8,128)}, f32[2,16,768]{2,1,0:T(8,128)}, f32[2,16,256]{2,1,0:T(8,128)}, f32[2,16,1024]{2,1,0:T...) custom-call(f32[1344,256]{1,0:T(8,128)} %get-tuple-element.14.refs_0_, f32[1344,256]{1,0:T(8,128)} %get-tuple-element.15.refs_1_, ...), custom_call_target="tpu_custom_call" | custom-call | tf_op jit(solution)/shard_map/pallas_call | solution.py:874
  138.4 1.4 %copy.17 = f32[2,22,16]{1,2,0:T(8,128)} copy(f32[2,22,16]{2,1,0:T(8,128)} %get-tuple-element.27) | data formatting | bytes 5632 | tf_op jit(solution)/shard_map/pallas_call | solution.py:874

commit v3 on v2

--- a/solution.py
+++ b/solution.py
@@ -221,6 +221,7 @@
 
 
 def forward_layer(l, h, w, wt, r, at):
+    at("P", l)
     vec = r.vec[l]
 
     def project(s, carry):
@@ -238,10 +239,12 @@
             cells = part[:, 128:256].reshape(STRIPE, WG, GROUP, 128)
             for c in range(STRIPE):
                 r.turn[i, :, s * STRIPE + c] = cells[c]
+        at("P", l, s)
         return carry
 
     lax.fori_loop(0, HP // STRIPE, project, 0)
-    at("projected", l)
+
+    at("H", l)
 
     def horizontal(s, carry):
         rows = span(s, CHUNK)
@@ -252,10 +255,10 @@
         pos = position(near, [taps[i : i + 1] for i in range(9)]) + vec[8:9, 0:128]
         o = r.o_r[l, s].T[0:CHUNK, :]
         r.a[l, rows, 0:128] = (o + pos.reshape(CHUNK, 128)).astype(BF)
+        at("H", l, s)
         return carry
 
     lax.fori_loop(0, HP // STRIPE, horizontal, 0)
-    at("horizontal", l)
 
     def vertical(s, carry):
         q, k, v = (r.turn[i, s].reshape(TALL, 128).astype(BF) for i in range(3))
@@ -267,10 +270,12 @@
         pos = position(near, [taps[i : i + 1] for i in range(9)]) + vec[8:9, 128:256]
         o = r.o_c[l, s].T[0:TALL, :]
         r.back[0, :, s] = o.reshape(HP, GROUP, 128) + pos
+        at("V", l, s)
         return carry
 
     lax.fori_loop(0, WG, vertical, 0)
-    at("vertical", l)
+
+    at("F", l)
 
     def feed(s, carry):
         rows = span(s, CHUNK)
@@ -288,11 +293,20 @@
         act = (hid * phi).astype(BF)
         r.act[l, rows, :] = act
         r.slope[l, rows, :] = slope.astype(BF)
-        r.x[l + 1, rows, :] = x1 + mm(act, wt.fc2(l)) + vec[7:8]
+        at("F", l, s)
         return carry
 
     lax.fori_loop(0, HP // STRIPE, feed, 0)
-    at("fed", l)
+    at("G", l)
+
+    def close(s, carry):
+        rows = span(s, CHUNK)
+        x1 = r.after[l, rows, :]
+        r.x[l + 1, rows, :] = x1 + mm(r.act[l, rows, :], wt.fc2(l)) + vec[7:8]
+        at("G", l, s)
+        return carry
+
+    lax.fori_loop(0, HP // STRIPE, close, 0)
 
 
 def backward_layer(l, h, w, wt, r, out, at):
@@ -328,14 +342,15 @@
         cells = da[:, 128:256].reshape(STRIPE, WG, GROUP, 128)
         for c in range(STRIPE):
             r.turn[0, :, s * STRIPE + c] = cells[c]
+        at("BF", l, s)
         return carry
 
     lax.fori_loop(0, HP // STRIPE, feed, 0)
-    at("back fed", l)
     out.put("fc2", l, mm(r.act[l], r.gy[...], TN))
+    at("B2", l)
     out.put("fc1", l, mm(r.n2[l], r.slope[l], TN))
     out.put("proj", l, mm(r.a[l], r.g1[...], TN))
-    at("back summed", l)
+    at("BS", l)
 
     def horizontal(s, carry):
         rows = span(s, CHUNK)
@@ -356,11 +371,12 @@
         r.gv[3:4, 0:128] += colsum(dv)
         for i, part in enumerate((dq, dk, dv)):
             r.dqkv_r[rows, 128 * i : 128 * i + 128] = part.astype(BF)
+        at("BH", l, s)
         return carry
 
     lax.fori_loop(0, HP // STRIPE, horizontal, 0)
     out.put("qkv_r", l, mm(r.n1[l], r.dqkv_r[...], TN))
-    at("back horizontal", l)
+    at("BR", l)
 
     def vertical(s, carry):
         q, k, v = (r.col[i, l, s] for i in range(3))
@@ -380,6 +396,7 @@
         r.gv[3:4, 128:256] += colsum(dv)
         for i, part in enumerate((dq, dk, dv)):
             r.back[i, :, s] = part.reshape(HP, GROUP, 128)
+        at("BV", l, s)
         return carry
 
     lax.fori_loop(0, WG, vertical, 0)
@@ -389,11 +406,12 @@
         for i in range(3):
             cells = r.back[i, pl.ds(s * STRIPE, STRIPE)].reshape(CHUNK, 128)
             r.dqkv_c[rows, 128 * i : 128 * i + 128] = cells.astype(BF)
+        at("BT", l, s)
         return carry
 
     lax.fori_loop(0, HP // STRIPE, turn, 0)
     out.put("qkv_c", l, mm(r.n1[l], r.dqkv_c[...], TN))
-    at("back vertical", l)
+    at("BC", l)
 
     def mix(s, carry):
         rows = span(s, CHUNK)
@@ -406,11 +424,12 @@
         add(0, colsum(d_n1 * xhat))
         add(1, colsum(d_n1))
         r.g[rows, :] += norm_back(d_n1, xhat, rate, vec[0:1])
+        at("BM", l, s)
         return carry
 
     lax.fori_loop(0, HP // STRIPE, mix, 0)
     out.put("vec", l, r.gv[...].T)
-    at("back mixed", l)
+    at("BX", l)
 
 
 MESH = pl.DeviceIdType.MESH
@@ -666,31 +685,77 @@
         return self.whole("fc2", l)
 
 
-class Queue:
-    def __init__(self, moves):
-        self.moves = moves
-        self.under_way = []
-
-    def begin(self, *parts):
-        for part in parts:
-            getattr(part, self.moves[0])()
-        self.under_way += [[part, 1] for part in parts]
-
-    def advance(self, parts=None):
-        for entry in self.under_way:
-            if (parts is None or entry[0] in parts) and entry[1] < len(self.moves):
-                getattr(entry[0], self.moves[entry[1]])()
-                entry[1] += 1
-
-    def complete(self, parts=None):
-        while any(
-            e[1] < len(self.moves) for e in self.under_way if parts is None or e[0] in parts
-        ):
-            self.advance(parts)
-
-    def drain(self):
-        for part, _ in self.under_way:
-            part.drain()
+GATHER_MOVES = {
+    ("P", 0, 3): ["proj 0 second", "fc1 0 second"],
+    ("H", 0, 1): ["fc2 0 second", "qkv 1 begin"],
+    ("V", 0, 0): ["proj 1 begin"],
+    ("V", 0, 3): ["proj 0 third", "fc1 0 third"],
+    ("V", 0, 4): ["qkv 1 second", "fc1 1 begin"],
+    ("F", 0, None): ["proj 0 finish", "fc1 0 finish"],
+    ("F", 0, 1): ["fc2 0 third", "fc2 1 begin"],
+    ("G", 0, None): ["fc2 0 finish"],
+    ("G", 0, 0): ["qkv 1 third"],
+    ("G", 0, 3): ["proj 1 second", "fc1 1 second"],
+    ("P", 1, None): ["qkv 1 finish"],
+    ("P", 1, 3): ["fc2 1 second"],
+    ("H", 1, 3): ["proj 1 third", "fc1 1 third"],
+    ("V", 1, 3): ["fc2 1 third"],
+    ("F", 1, None): ["proj 1 finish", "fc1 1 finish"],
+    ("G", 1, None): ["fc2 1 finish"],
+}
+SUM_MOVES = {
+    ("B2", 1, None): ["fc2 1 begin"],
+    ("BS", 1, None): ["fc1 1 begin", "proj 1 begin"],
+    ("BH", 1, 0): ["fc2 1 second", "fc1 1 second", "proj 1 second"],
+    ("BR", 1, None): ["qkv_r 1 begin", "fc2 1 third"],
+    ("BV", 1, 0): ["qkv_r 1 second"],
+    ("BV", 1, 2): ["fc1 1 third", "proj 1 third"],
+    ("BV", 1, 4): ["qkv_r 1 third"],
+    ("BC", 1, None): ["qkv_c 1 begin"],
+    ("BM", 1, 0): ["fc2 1 fourth"],
+    ("BM", 1, 2): ["qkv_c 1 second"],
+    ("BX", 1, None): ["vec 1 begin"],
+    ("BF", 0, 1): ["fc1 1 fourth", "proj 1 fourth", "vec 1 second"],
+    ("BF", 0, 3): ["fc2 1 finish", "qkv_r 1 fourth", "qkv_c 1 third"],
+    ("B2", 0, None): ["fc2 0 begin"],
+    ("BS", 0, None): ["fc1 0 begin", "proj 0 begin"],
+    ("BH", 0, 0): ["fc2 0 second", "fc1 0 second", "proj 0 second", "vec 1 third"],
+    ("BH", 0, 1): ["fc1 1 finish", "proj 1 finish", "qkv_r 1 finish"],
+    ("BH", 0, 2): ["qkv_c 1 fourth", "vec 1 fourth"],
+    ("BR", 0, None): ["qkv_r 0 begin", "fc2 0 third"],
+    ("BV", 0, 0): ["qkv_r 0 second"],
+    ("BV", 0, 2): ["fc1 0 third", "proj 0 third"],
+    ("BV", 0, 3): ["qkv_c 1 finish", "vec 1 finish"],
+    ("BV", 0, 4): ["qkv_r 0 third"],
+    ("BC", 0, None): ["qkv_c 0 begin"],
+    ("BM", 0, 0): ["fc2 0 fourth"],
+    ("BM", 0, 2): ["qkv_c 0 second"],
+    ("BX", 0, None): ["vec 0 begin"],
+}
+LAST_MOVES = [
+    ("vec", 0, "second"), ("fc1", 0, "fourth"), ("proj", 0, "fourth"), ("qkv_c", 0, "third"),
+    ("vec", 0, "third"), ("qkv_r", 0, "fourth"), ("fc2", 0, "finish"), ("fc1", 0, "finish"),
+    ("proj", 0, "finish"), ("qkv_r", 0, "finish"), ("qkv_c", 0, "fourth"), ("vec", 0, "fourth"),
+    ("qkv_c", 0, "finish"), ("vec", 0, "finish"),
+]
+
+
+class Moves:
+    def __init__(self, table, parts):
+        self.table, self.parts = table, parts
+
+    def take(self, moves):
+        for move in moves:
+            name, l, verb = move.split()
+            getattr(self.parts[name, int(l)], verb)()
+
+    def __call__(self, phase, l, step=None):
+        if step is None:
+            self.take(self.table.get((phase, l, None), []))
+            return
+        for (name, block, when), moves in self.table.items():
+            if (name, block) == (phase, l) and when is not None:
+                pl.when(step == when)(functools.partial(self.take, moves))
 
 
 class Gradients:
@@ -702,7 +767,7 @@
         ref[...] = value.astype(BF).reshape(ref.shape)
 
 
-def plan(shards, copies, layers, width, hidden):
+def plan(shards, copies, layers, width, hidden, held):
     zs, xs = 4, shards // 8
     place = (zs, xs, 2)
     d, f = width // shards, hidden // shards
@@ -710,8 +775,7 @@
     own = dict(qkv=(d, 3 * width), proj=(d, width), fc1=(d, hidden), fc2=(f, width))
     for name in MATRICES:
         shapes["full", name] = pltpu.VMEM((layers,) + place + own[name], BF)
-    shapes["own", "vec"] = pltpu.VMEM((layers, d, 128), F32)
-    shapes["full", "vec"] = pltpu.VMEM(place + (layers, d, 128), F32)
+    shapes["full", "vec"] = pltpu.VMEM(place + (layers, d, held), BF)
     gathers = len(MATRICES) * layers + 1
     hops = zs - 1 + xs - 1 + 1
     for name in ("gather send", "gather recv"):
@@ -744,25 +808,20 @@
     grid.signal()
     h, w = h_ref[0], w_ref[0]
 
-    held = vec_own.shape[1]
-    eye = (iota((held, 128), 0) == iota((held, 128), 1)).astype(F32).astype(BF)
-    for l in range(layers):
-        s["own", "vec"][l] = mm(vec_own[l], eye, TN)
     sems = [s["gather send"], s["gather recv"], s["gather local"]]
     order = [(name, l) for l in range(layers) for name in MATRICES]
     gathers = {
         (name, l): Gather(grid, own[name].at[l], s["full", name].at[l], sems, i)
         for i, (name, l) in enumerate(order)
     }
-    gathers["vec"] = Gather(grid, s["own", "vec"], s["full", "vec"], sems, len(order))
+    gathers["vec", 0] = Gather(grid, vec_own, s["full", "vec"], sems, len(order))
     wt = Weights({name: s["full", name] for name in MATRICES})
-    gather_queue = Queue(("begin", "second", "third", "finish"))
-    first = [gathers["qkv", 0], gathers["vec"]]
-    rest = [gathers[key] for key in order if key != ("qkv", 0)]
-    early, late = rest[:3], rest[3:]
+    wt = Weights({name: s["full", name] for name in MATRICES})
 
     grid.wait()
-    gather_queue.begin(*first)
+    first = [gathers["qkv", 0], gathers["vec", 0]]
+    for one in first:
+        one.begin()
     for stack in (r.qs_r, r.qs_c):
         stack[...] = jnp.where(iota(stack.shape, 1) == 128, 1.0, 0.0).astype(BF)
     for stack in (r.ds_r, r.ds_c):
@@ -770,31 +829,27 @@
     r.gv[...] = jnp.zeros_like(r.gv)
     pad_groups(tok, r.x.at[0])
     pad_groups(cot, r.g)
-    gather_queue.advance(first)
-    gather_queue.begin(*early)
-    gather_queue.begin(*late)
-    gather_queue.complete(first)
+    for one in first:
+        one.second()
+    gathers["proj", 0].begin()
+    gathers["fc1", 0].begin()
+    for one in first:
+        one.third()
+    gathers["fc2", 0].begin()
+    for one in first:
+        one.finish()
     for l in range(layers):
-        value = s["full", "vec"][:, :, :, l]
-        r.vec[l] = value.reshape(-1, 128).T
-
-    def after_forward(point, l):
-        if l == 0:
-            if point == "horizontal":
-                gather_queue.advance(early)
-            if point == "vertical":
-                gather_queue.complete(early)
-                gather_queue.advance(late)
-            if point == "fed":
-                gather_queue.complete(late)
-
+        value = s["full", "vec"][:, :, :, l].astype(F32)
+        value = value.reshape(-1, value.shape[-1])
+        value = jnp.concatenate([value, jnp.zeros((value.shape[0], 128 - value.shape[1]), F32)], axis=1)
+        r.vec[l] = value.T
+
+    at = Moves(GATHER_MOVES, gathers)
     for l in range(layers):
-        forward_layer(l, h, w, wt, r, after_forward)
+        forward_layer(l, h, w, wt, r, at)
     y_copy = pltpu.make_async_copy(r.x.at[layers], y_ref, s["out"].at[0])
     y_copy.start()
 
-    sum_queue = Queue(("begin", "second", "third", "fourth", "finish"))
-    width = 128
     sums = {}
     for l in range(layers):
         for i, name in enumerate(SUMMED):
@@ -809,27 +864,15 @@
             )
     gradients = Gradients({(name, l): s["part", name, l] for l in range(layers) for name in SUMMED})
 
-    def after_backward(point, l):
-        if point == "back summed":
-            sum_queue.advance()
-            sum_queue.begin(*(sums[name, l] for name in ("fc2", "fc1", "proj")))
-        if point == "back horizontal":
-            sum_queue.advance()
-            sum_queue.begin(sums["qkv_r", l])
-        if point == "back vertical":
-            sum_queue.advance()
-            sum_queue.begin(sums["qkv_c", l])
-        if point == "back mixed":
-            sum_queue.advance()
-            sum_queue.begin(sums["vec", l])
-
+    at = Moves(SUM_MOVES, sums)
     for l in reversed(range(layers)):
-        backward_layer(l, h, w, wt, r, gradients, after_backward)
+        backward_layer(l, h, w, wt, r, gradients, at)
     g_copy = pltpu.make_async_copy(r.g, gt_ref, s["out"].at[1])
     g_copy.start()
-    sum_queue.complete()
-    gather_queue.drain()
-    sum_queue.drain()
+    for name, l, move in LAST_MOVES:
+        getattr(sums[name, l], move)()
+    for one in list(gathers.values()) + list(sums.values()):
+        one.drain()
     y_copy.wait()
     g_copy.wait()
 
@@ -841,10 +884,7 @@
     for i in range(2, count - 1):
         refs[count + i][...] = refs[i][...]
     vec, out = refs[count - 1], refs[2 * count - 1]
-    layers, held, places = out.shape
-    for l in range(layers):
-        turned = widen(vec[l], 128).T
-        out[l] = turned[0:held, 0:places]
+    out[...] = vec[:, :, 0 : out.shape[2]]
 
 
 def shards_step(shards, copies, tokens, heights, widths, w_qkv, w_proj, w_fc1, w_fc2, vectors, cotangent):
@@ -853,7 +893,8 @@
     vmem = pl.BlockSpec(memory_space=pltpu.VMEM)
     smem = pl.BlockSpec(memory_space=pltpu.SMEM)
     hbm = pl.BlockSpec(memory_space=pl.ANY)
-    scratch = plan(shards, copies, layers, width, hidden)
+    turned = vectors.transpose(0, 2, 1)
+    scratch = plan(shards, copies, layers, width, hidden, turned.shape[2])
     matrices = [w_qkv, w_proj, w_fc1, w_fc2]
     results = [jax.ShapeDtypeStruct((ROWS, width), F32)] * 2
     results += [jax.ShapeDtypeStruct(m.shape, F32) for m in matrices]
@@ -867,18 +908,17 @@
         compiler_params=pltpu.CompilerParams(
             collective_id=0, has_side_effects=True, vmem_limit_bytes=67043328
         ),
-    )(heights, widths, tokens, cotangent, *matrices, vectors)
+    )(heights, widths, tokens, cotangent, *matrices, turned)
     final = [jax.ShapeDtypeStruct((count, width), F32)] * 2
-    final += [jax.ShapeDtypeStruct(m.shape, F32) for m in matrices + [vectors]]
-    return tuple(
-        pl.pallas_call(
-            functools.partial(finish_kernel, len(raw)),
-            out_shape=final,
-            in_specs=[vmem] * len(raw),
-            out_specs=[vmem] * len(raw),
-            compiler_params=pltpu.CompilerParams(vmem_limit_bytes=67043328),
-        )(*raw)
-    )
+    final += [jax.ShapeDtypeStruct(m.shape, F32) for m in matrices + [turned]]
+    *arrays, vec = pl.pallas_call(
+        functools.partial(finish_kernel, len(raw)),
+        out_shape=final,
+        in_specs=[vmem] * len(raw),
+        out_specs=[vmem] * len(raw),
+        compiler_params=pltpu.CompilerParams(vmem_limit_bytes=67043328),
+    )(*raw)
+    return (*arrays, vec.transpose(0, 2, 1))
 
 
 def solution(mesh):

time: 140 us -> 116 us (0.83)
  Pallas kernels: 135 us -> 114 us
  local copies, waits for them, and re-layouts: 2.81 us -> 0 us
    pallas_call x1, Pallas kernels: 131 us -> 110 us  [shards_step(): pl.pallas_call(functools.partial(step_kernel, shards, copies, list(scratc...]
    pallas_call x1 -> x0, local copies, waits for them, and re-layouts: 1.42 us -> none  [shards_step(): pl.pallas_call(functools.partial(finish_kernel, len(raw)), out_shape=fina...]
where the time goes in v3:
time: 116 us; the launch traced here: 115 us
  Pallas kernels  114 us (98%)
  between operations  1.93 us (2%)
    pallas_call x1, Pallas kernels, shards_step(): pl.pallas_call(functools.partial(step_kernel, shards, copies, list(scratc...  110 us
    pallas_call x1, Pallas kernels, shards_step(): pl.pallas_call(functools.partial(finish_kernel, len(raw)), out_shape=fina...  3.96 us

profile of v3, /device:TPU:0, one launch (start us, length us, event | category | flops | bytes accessed | tf_op | source)
XLA Modules:
  0.0 115.5 jit_solution(10296890905605893784)
XLA Ops:
  1.9 109.6 %shard_map.144 = (f32[1344,256]{1,0:T(8,128)}, f32[1344,256]{1,0:T(8,128)}, f32[2,16,768]{2,1,0:T(8,128)}, f32[2,16,256]{2,1,0:T(8,128)}, f32[2,16,1024]{2,1,0:T...) custom-call(s32[1]{0:T(128)S(6)} %copy.16.refs_0_, s32[1]{0:T(128)S(6)} %copy.17.refs_1_, ...), custom_call_target="tpu_custom_call" | custom-call | tf_op jit(solution)/shard_map/pallas_call | solution.py:902
  111.5 4.0 %shard_map.145 = (f32[1176,256]{1,0:T(8,128)}, f32[1176,256]{1,0:T(8,128)}, f32[2,16,768]{2,1,0:T(8,128)}, f32[2,16,256]{2,1,0:T(8,128)}, f32[2,16,1024]{2,1,0:T...) custom-call(f32[1344,256]{1,0:T(8,128)} %get-tuple-element.21.refs_0_, f32[1344,256]{1,0:T(8,128)} %get-tuple-element.22.refs_1_, ...), custom_call_target="tpu_custom_call" | custom-call | tf_op jit(solution)/shard_map/pallas_call | solution.py:914

commit v4 on v3

--- a/solution.py
+++ b/solution.py
@@ -42,6 +42,10 @@
     return pl.ds(pl.multiple_of(index * size, size), size)
 
 
+def map_rows(stripe):
+    return pl.ds(stripe * STRIPE, STRIPE)
+
+
 def pad_groups(src, dst, scale=None):
     def body(j, carry):
         block = src[pl.ds(pl.multiple_of(j * 56, 8), 56), :].astype(F32).reshape(7, 8, -1)
@@ -134,7 +138,7 @@
     return jnp.concatenate([x, jnp.zeros((wide - length, x.shape[1]), x.dtype)], axis=0)
 
 
-def attend(q, k_mask, vm, qs, out_t, lse, stripe, wide):
+def attend(q, k_mask, vm, qs, out_t, inv, probs, stripe, wide):
     length = q.shape[0]
     stack_heads(qs, q, wide)
     scores = mm(k_mask, qs[0 : HEADS * wide, :], NT)
@@ -144,30 +148,34 @@
         top = jnp.max(s, axis=0, keepdims=True)
         p = jnp.exp2(s - top)
         total = jnp.sum(p, axis=0, keepdims=True)
-        o = mm(v_t[HEAD * h : HEAD * (h + 1), :], p.astype(BF))
-        out_t[stripe, HEAD * h : HEAD * (h + 1), :] = o / total
-        lse[stripe, h : h + 1, :] = top + jnp.log2(total)
-
-
-def attend_back(q, k, k_mask, vm, da, qs, ds_stack, p_all, g_all, out_t, lse, stripe, wide):
+        p_low = p.astype(BF)
+        probs[stripe, :, h * wide : (h + 1) * wide] = p_low
+        rate = 1.0 / total
+        inv[stripe, h : h + 1, :] = rate
+        o = mm(v_t[HEAD * h : HEAD * (h + 1), :], p_low)
+        out_t[stripe, HEAD * h : HEAD * (h + 1), :] = o * rate
+
+
+def attend_back(q, k, vm, da, qs, da_stack, g_all, out_t, inv, probs, stripe, wide):
     length = q.shape[0]
     stack_heads(qs, q, wide)
-    stack_heads(ds_stack, da, wide)
     da_t = widen(da.astype(F32), wide).T
     k_t = widen(k.astype(F32), wide).T.astype(BF)[:, 0:length]
-    weighted = da_t * out_t[stripe]
+    inner = []
+    for h in range(HEADS):
+        rows = slice(HEAD * h, HEAD * (h + 1))
+        scaled = (da_t[rows, :] * inv[stripe, h : h + 1, :]).astype(BF)
+        da_stack[rows, h * wide : (h + 1) * wide] = scaled
+        inner.append(colsum(scaled.astype(F32) * out_t[stripe, rows, :]))
+    d_probs = mm(vm, da_stack[...])
     dq_t = []
-    scores = mm(k_mask, qs[0 : HEADS * wide, :], NT)
-    d_probs = mm(vm, ds_stack[0 : HEADS * wide, :], NT)
     for h in range(HEADS):
         lanes = slice(h * wide, (h + 1) * wide)
-        inner = jnp.sum(weighted[HEAD * h : HEAD * (h + 1), :], axis=0, keepdims=True)
-        p = jnp.exp2(scores[:, lanes] - lse[stripe, h : h + 1, :])
-        g = (p * (d_probs[:, lanes] - inner)).astype(BF)
-        p_all[0:length, lanes] = p.astype(BF)
+        p = probs[stripe, :, lanes].astype(F32)
+        g = (p * (d_probs[:, lanes] - inner[h])).astype(BF)
         g_all[0:length, lanes] = g
         dq_t.append(mm(k_t[HEAD * h : HEAD * (h + 1), :], g))
-    dv = mm(p_all[0:length, 0 : HEADS * wide], ds_stack[0 : HEADS * wide, :])
+    dv = mm(probs[stripe], da_stack[...], NT)
     dk = mm(g_all[0:length, 0 : HEADS * wide], qs[0 : HEADS * wide, 0:128]) * LN2
     dq = jnp.concatenate(dq_t, axis=0).T[0:length, :] * SCALE
     return dq, dk, dv
@@ -221,65 +229,85 @@
 
 
 def forward_layer(l, h, w, wt, r, at):
-    at("P", l)
+    at(P_, l)
     vec = r.vec[l]
 
-    def project(s, carry):
+    def keep_row(rows, parts):
+        for i, part in enumerate(parts):
+            r.row[i, l, rows, :] = part.astype(BF)
+
+    def keep_col(s, parts):
+        for i, part in enumerate(parts):
+            r.cells[i, map_rows(s)] = part.reshape(STRIPE, WG, GROUP, 128)
+
+    def split(mixed, s, half, lanes):
+        here = slice(128 * half, 128 * half + 128)
+        q = (mixed[:, lanes[0]] + vec[2:3, here]) * (SCALE * LOG2E)
+        v = (mixed[:, lanes[2]] + vec[3:4, here]) * rows_live(s, h, w, 128)
+        return q, mixed[:, lanes[1]], v
+
+    def norm(s):
         rows = span(s, CHUNK)
         xhat, rate = norm_parts(r.x[l, rows, :])
         n1 = (xhat * vec[0:1] + vec[1:2]).astype(BF)
         r.n1[l, rows, :] = n1
-        live = rows_live(s, h, w, 256)
+        return rows, n1
+
+    alone = [slice(128 * i, 128 * i + 128) for i in range(3)]
+
+    def project(s):
+        rows, n1 = norm(s)
         mixed = mm(n1, wt.qkv(l))
-        q = (mixed[:, 0:256] + vec[2:3]) * (SCALE * LOG2E)
-        k = mixed[:, 256:512]
-        v = (mixed[:, 512:768] + vec[3:4]) * live
-        for i, part in enumerate((q, k, v)):
-            r.row[i, l, rows, :] = part[:, 0:128].astype(BF)
-            cells = part[:, 128:256].reshape(STRIPE, WG, GROUP, 128)
-            for c in range(STRIPE):
-                r.turn[i, :, s * STRIPE + c] = cells[c]
-        at("P", l, s)
-        return carry
-
-    lax.fori_loop(0, HP // STRIPE, project, 0)
-
-    at("H", l)
-
-    def horizontal(s, carry):
+        for half in range(2):
+            lanes = [slice(256 * i + 128 * half, 256 * i + 128 * half + 128) for i in range(3)]
+            parts = split(mixed, s, half, lanes)
+            keep_col(s, parts) if half else keep_row(rows, parts)
+
+    def project_row(s):
+        rows, n1 = norm(s)
+        keep_row(rows, split(mm(n1, wt.qkv_half(l, 0)), s, 0, alone))
+
+    def project_col(s):
+        n1 = r.n1[l, span(s, CHUNK), :]
+        keep_col(s, split(mm(n1, wt.qkv_half(l, 1)), s, 1, alone))
+
+    sweep(P_, l, HP // STRIPE, project if l else project_row, at)
+
+    at(H_, l)
+
+    def horizontal(s):
         rows = span(s, CHUNK)
         q, k, v = (r.row[i, l, rows, :] for i in range(3))
-        attend(q, with_mask(k, rows_live(s, h, w, 128)), v, r.qs_r, r.o_r.at[l], r.lse_r.at[l], s, WIDE_R)
+        attend(q, with_mask(k, rows_live(s, h, w, 128)), v, r.qs_r, r.o_r.at[l], r.inv_r.at[l], r.p_r, s, WIDE_R)
         near = row_neighbours(v.astype(F32))
         taps = vec[9:18, 0:128]
         pos = position(near, [taps[i : i + 1] for i in range(9)]) + vec[8:9, 0:128]
         o = r.o_r[l, s].T[0:CHUNK, :]
         r.a[l, rows, 0:128] = (o + pos.reshape(CHUNK, 128)).astype(BF)
-        at("H", l, s)
-        return carry
-
-    lax.fori_loop(0, HP // STRIPE, horizontal, 0)
-
-    def vertical(s, carry):
-        q, k, v = (r.turn[i, s].reshape(TALL, 128).astype(BF) for i in range(3))
+
+    sweep(H_, l, HP // STRIPE, horizontal, at)
+    at(PC_, l)
+    if l == 0:
+        sweep(PC_, l, HP // STRIPE, project_col, at)
+
+    def vertical(s):
+        q, k, v = (r.cells[i, :, s].reshape(TALL, 128).astype(BF) for i in range(3))
         for i, part in enumerate((q, k, v)):
             r.col[i, l, s] = part
-        attend(q, with_mask(k, cols_live(s, h, w, 128)), v, r.qs_c, r.o_c.at[l], r.lse_c.at[l], s, WIDE_C)
+        attend(q, with_mask(k, cols_live(s, h, w, 128)), v, r.qs_c, r.o_c.at[l], r.inv_c.at[l], r.p_c, s, WIDE_C)
         near = col_neighbours(v.astype(F32))
         taps = vec[9:18, 128:256]
         pos = position(near, [taps[i : i + 1] for i in range(9)]) + vec[8:9, 128:256]
         o = r.o_c[l, s].T[0:TALL, :]
-        r.back[0, :, s] = o.reshape(HP, GROUP, 128) + pos
-        at("V", l, s)
-        return carry
-
-    lax.fori_loop(0, WG, vertical, 0)
-
-    at("F", l)
-
-    def feed(s, carry):
+        r.cells[3, :, s] = o.reshape(HP, GROUP, 128) + pos
+
+    sweep(V_, l, WG, vertical, at)
+
+    at(F_, l)
+
+    def feed(s):
         rows = span(s, CHUNK)
-        turned = r.back[0, pl.ds(s * STRIPE, STRIPE)].reshape(CHUNK, 128).astype(BF)
+        turned = r.cells[3, map_rows(s)].reshape(CHUNK, 128).astype(BF)
         r.a[l, rows, 128:256] = turned
         x1 = r.x[l, rows, :] + mm(r.a[l, rows, :], wt.proj(l)) + vec[4:5]
         r.after[l, rows, :] = x1
@@ -293,20 +321,16 @@
         act = (hid * phi).astype(BF)
         r.act[l, rows, :] = act
         r.slope[l, rows, :] = slope.astype(BF)
-        at("F", l, s)
-        return carry
-
-    lax.fori_loop(0, HP // STRIPE, feed, 0)
-    at("G", l)
-
-    def close(s, carry):
+
+    sweep(F_, l, HP // STRIPE, feed, at)
+    at(G_, l)
+
+    def close(s):
         rows = span(s, CHUNK)
         x1 = r.after[l, rows, :]
         r.x[l + 1, rows, :] = x1 + mm(r.act[l, rows, :], wt.fc2(l)) + vec[7:8]
-        at("G", l, s)
-        return carry
-
-    lax.fori_loop(0, HP // STRIPE, close, 0)
+
+    sweep(G_, l, HP // STRIPE, close, at)
 
 
 def backward_layer(l, h, w, wt, r, out, at):
@@ -316,7 +340,7 @@
     def add(row, value):
         r.gv[row : row + 1, :] += value
 
-    def feed(s, carry):
+    def feed(s):
         rows = span(s, CHUNK)
         g = r.g[rows, :]
         add(7, colsum(g))
@@ -339,27 +363,22 @@
         da = mm(g1_low, wt.proj(l), NT)
         r.da_r[rows, :] = da[:, 0:128].astype(BF)
         add(8, colsum(da.astype(BF).astype(F32)))
-        cells = da[:, 128:256].reshape(STRIPE, WG, GROUP, 128)
-        for c in range(STRIPE):
-            r.turn[0, :, s * STRIPE + c] = cells[c]
-        at("BF", l, s)
-        return carry
-
-    lax.fori_loop(0, HP // STRIPE, feed, 0)
-    out.put("fc2", l, mm(r.act[l], r.gy[...], TN))
-    at("B2", l)
-    out.put("fc1", l, mm(r.n2[l], r.slope[l], TN))
-    out.put("proj", l, mm(r.a[l], r.g1[...], TN))
-    at("BS", l)
-
-    def horizontal(s, carry):
+        r.cells[3, map_rows(s)] = da[:, 128:256].reshape(STRIPE, WG, GROUP, 128)
+
+    sweep(BF_, l, HP // STRIPE, feed, at)
+    out.put(FC2, l, mm(r.gy[...], r.act[l], TN).astype(BF).T)
+    at(B2_, l)
+    out.put(FC1, l, mm(r.n2[l], r.slope[l], TN))
+    out.put(PROJ, l, mm(r.a[l], r.g1[...], TN))
+    at(BS_, l)
+
+    def horizontal(s):
         rows = span(s, CHUNK)
         q, k, v = (r.row[i, l, rows, :] for i in range(3))
         da = r.da_r[rows, :]
         live = rows_live(s, h, w, 128)
         dq, dk, dv = attend_back(
-            q, k, with_mask(k, live), v, da, r.qs_r, r.ds_r, r.p_all, r.g_all,
-            r.o_r.at[l], r.lse_r.at[l], s, WIDE_R,
+            q, k, v, da, r.qs_r, r.dt_r, r.g_all, r.o_r.at[l], r.inv_r.at[l], r.p_r, s, WIDE_R
         )
         taps = [vec[9 + i : 10 + i, 0:128] for i in range(9)]
         da_near = row_neighbours(da.astype(F32))
@@ -371,20 +390,17 @@
         r.gv[3:4, 0:128] += colsum(dv)
         for i, part in enumerate((dq, dk, dv)):
             r.dqkv_r[rows, 128 * i : 128 * i + 128] = part.astype(BF)
-        at("BH", l, s)
-        return carry
-
-    lax.fori_loop(0, HP // STRIPE, horizontal, 0)
-    out.put("qkv_r", l, mm(r.n1[l], r.dqkv_r[...], TN))
-    at("BR", l)
-
-    def vertical(s, carry):
+
+    sweep(BH_, l, HP // STRIPE, horizontal, at)
+    out.put(QKV_R, l, mm(r.n1[l], r.dqkv_r[...], TN))
+    at(BR_, l)
+
+    def vertical(s):
         q, k, v = (r.col[i, l, s] for i in range(3))
-        da = r.turn[0, s].reshape(TALL, 128).astype(BF)
+        da = r.cells[3, :, s].reshape(TALL, 128).astype(BF)
         live = cols_live(s, h, w, 128)
         dq, dk, dv = attend_back(
-            q, k, with_mask(k, live), v, da, r.qs_c, r.ds_c, r.p_all, r.g_all,
-            r.o_c.at[l], r.lse_c.at[l], s, WIDE_C,
+            q, k, v, da, r.qs_c, r.dt_c, r.g_all, r.o_c.at[l], r.inv_c.at[l], r.p_c, s, WIDE_C
         )
         taps = [vec[9 + i : 10 + i, 128:256] for i in range(9)]
         da_near = col_neighbours(da.astype(F32))
@@ -395,25 +411,21 @@
         r.gv[2:3, 128:256] += colsum(dq)
         r.gv[3:4, 128:256] += colsum(dv)
         for i, part in enumerate((dq, dk, dv)):
-            r.back[i, :, s] = part.reshape(HP, GROUP, 128)
-        at("BV", l, s)
-        return carry
-
-    lax.fori_loop(0, WG, vertical, 0)
-
-    def turn(s, carry):
+            r.cells[i, :, s] = part.reshape(HP, GROUP, 128)
+
+    sweep(BV_, l, WG, vertical, at)
+
+    def turn(s):
         rows = span(s, CHUNK)
         for i in range(3):
-            cells = r.back[i, pl.ds(s * STRIPE, STRIPE)].reshape(CHUNK, 128)
+            cells = r.cells[i, map_rows(s)].reshape(CHUNK, 128)
             r.dqkv_c[rows, 128 * i : 128 * i + 128] = cells.astype(BF)
-        at("BT", l, s)
-        return carry
-
-    lax.fori_loop(0, HP // STRIPE, turn, 0)
-    out.put("qkv_c", l, mm(r.n1[l], r.dqkv_c[...], TN))
-    at("BC", l)
-
-    def mix(s, carry):
+
+    sweep(BT_, l, HP // STRIPE, turn, at)
+    out.put(QKV_C, l, mm(r.n1[l], r.dqkv_c[...], TN))
+    at(BC_, l)
+
+    def mix(s):
         rows = span(s, CHUNK)
         parts = []
         for i in range(3):
@@ -424,12 +436,10 @@
         add(0, colsum(d_n1 * xhat))
         add(1, colsum(d_n1))
         r.g[rows, :] += norm_back(d_n1, xhat, rate, vec[0:1])
-        at("BM", l, s)
-        return carry
-
-    lax.fori_loop(0, HP // STRIPE, mix, 0)
-    out.put("vec", l, r.gv[...].T)
-    at("BX", l)
+
+    sweep(BM_, l, HP // STRIPE, mix, at)
+    out.put(VEC, l, r.gv[...].T)
+    at(BX_, l)
 
 
 MESH = pl.DeviceIdType.MESH
@@ -544,12 +554,38 @@
             copy.wait_send()
 
 
+class Group:
+    def __init__(self, parts):
+        self.parts = parts
+
+    def each(self, verb):
+        for part in self.parts:
+            getattr(part, verb)()
+
+    def begin(self):
+        self.each(VERBS[BEGIN])
+
+    def second(self):
+        self.each(VERBS[SECOND])
+
+    def third(self):
+        self.each(VERBS[THIRD])
+
+    def finish(self):
+        self.each(VERBS[FINISH])
+
+    def drain(self):
+        for part in self.parts:
+            part.drain()
+
+
 class Reduce:
     def __init__(self, grid, part, bufs, out, sems, row):
         self.grid, self.part, self.out = grid, part, out
         send, recv = sems
         g = grid
-        self.from_sibling, self.chip, self.from_x, self.line, self.from_z, self.own, self.from_rep = bufs
+        self.from_sibling, self.from_x, self.from_z, self.from_rep = bufs
+        self.chip, self.line, self.own = self.from_sibling, self.from_x.at[0], self.from_z.at[0]
         self.across = remote(
             part.at[:, :, 1 - g.core], self.from_sibling, send.at[row, 0], recv.at[row, 0], g.sibling()
         )
@@ -574,7 +610,7 @@
     def second(self):
         self.across.wait_recv()
         mine = self.part[:, :, self.grid.core].astype(F32)
-        self.chip[...] = (mine + self.from_sibling[...].astype(F32)).astype(BF)
+        self.chip[...] = (mine + self.chip[...].astype(F32)).astype(BF)
         for copy in self.along_x:
             copy.start()
 
@@ -604,21 +640,24 @@
         total = self.own[...].astype(F32)
         for d, _ in self.grid.rep_peers():
             total = total + self.from_rep[d - 1].astype(F32)
-        out, half = self.out
+        held, half, self.leave = self.out
         if half is None:
-            out[...] = total
-            return
-        for i in range(3):
-            lanes = slice(256 * i + 128 * half, 256 * i + 128 * half + 128)
-            out[:, lanes] = total[:, 128 * i : 128 * i + 128]
+            held[...] = total[:, 0 : held.shape[1]]
+        else:
+            for i in range(3):
+                held[:, lanes_of(i, half)] = total[:, 128 * i : 128 * i + 128]
+        if self.leave is not None:
+            self.leave.start()
 
     def drain(self):
         for copy in [self.across] + self.along_x + self.along_z + self.along_rep:
             copy.wait_send()
+        if self.leave is not None:
+            self.leave.wait()
 
 
 def reduce_bufs(zs, xs, copies, shape):
-    dims = [(zs, xs), (zs, xs), (max(xs - 1, 1), zs), (zs,), (zs - 1,), (), (max(copies - 1, 1),)]
+    dims = [(zs, xs), (xs - 1, zs), (zs - 1,), (copies - 1,)]
     return [pltpu.VMEM(d + tuple(shape), BF) for d in dims]
 
 
@@ -632,17 +671,17 @@
     slope=((2, ROWS, 1024), BF),
     row=((3, 2, ROWS, 128), BF),
     col=((3, 2, WG, TALL, 128), BF),
-    turn=((3, WG, HP, GROUP, 128), F32),
-    back=((3, HP, WG, GROUP, 128), F32),
+    cells=((4, HP, WG, GROUP, 128), F32),
     o_r=((2, HP // STRIPE, 128, WIDE_R), F32),
     o_c=((2, WG, 128, WIDE_C), F32),
-    lse_r=((2, HP // STRIPE, 8, WIDE_R), F32),
-    lse_c=((2, WG, 8, WIDE_C), F32),
+    inv_r=((2, HP // STRIPE, 8, WIDE_R), F32),
+    inv_c=((2, WG, 8, WIDE_C), F32),
+    p_r=((HP // STRIPE, CHUNK, HEADS * WIDE_R), BF),
+    p_c=((WG, TALL, HEADS * WIDE_C), BF),
     qs_r=((HEADS * WIDE_R, 256), BF),
     qs_c=((HEADS * WIDE_C, 256), BF),
-    ds_r=((HEADS * WIDE_R, 128), BF),
-    ds_c=((HEADS * WIDE_C, 128), BF),
-    p_all=((CHUNK, HEADS * WIDE_R), BF),
+    dt_r=((128, HEADS * WIDE_R), BF),
+    dt_c=((128, HEADS * WIDE_C), BF),
     g_all=((CHUNK, HEADS * WIDE_R), BF),
     g=((ROWS, 256), F32),
     gy=((ROWS, 256), BF),
@@ -655,13 +694,25 @@
 )
 
 
+KEPT = ("p_r", "p_c")
+
+
 class Refs:
     def __init__(self, names, refs):
         self.__dict__.update(zip(names, refs))
 
 
-MATRICES = ("qkv", "proj", "fc1", "fc2")
-SUMMED = ("fc2", "fc1", "proj", "qkv_r", "qkv_c", "vec")
+QKV, PROJ, FC1, FC2, QKV_R, QKV_C, VEC, SAVE, LOAD_R, LOAD_C = range(10)
+MATRICES = (QKV, PROJ, FC1, FC2)
+SUMMED = (FC2, FC1, PROJ, QKV_R, QKV_C, VEC)
+BEGIN, SECOND, THIRD, FOURTH, FINISH = range(5)
+VERBS = ("begin", "second", "third", "fourth", "finish")
+P_, H_, V_, F_, G_, BF_, B2_, BS_, BH_, BR_, BV_, BT_, BC_, BM_, BX_, PC_ = range(16)
+STRIDE = {P_: 4, F_: 4, BM_: 4, BT_: 4, G_: 4}
+
+
+def lanes_of(block, half):
+    return slice(256 * block + 128 * half, 256 * block + 128 * half + 128)
 
 
 class Weights:
@@ -672,72 +723,99 @@
         value = self.full[name][l]
         return value.reshape(-1, value.shape[-1])
 
+    def qkv_half(self, l, half):
+        parts = []
+        for i in range(3):
+            value = self.full[QKV][l, :, :, :, :, lanes_of(i, half)]
+            parts.append(value.reshape(-1, 128))
+        return jnp.concatenate(parts, axis=1)
+
     def qkv(self, l):
-        return self.whole("qkv", l)
+        return self.whole(QKV, l)
 
     def proj(self, l):
-        return self.whole("proj", l)
+        return self.whole(PROJ, l)
 
     def fc1(self, l):
-        return self.whole("fc1", l)
+        return self.whole(FC1, l)
 
     def fc2(self, l):
-        return self.whole("fc2", l)
+        return self.whole(FC2, l)
 
 
 GATHER_MOVES = {
-    ("P", 0, 3): ["proj 0 second", "fc1 0 second"],
-    ("H", 0, 1): ["fc2 0 second", "qkv 1 begin"],
-    ("V", 0, 0): ["proj 1 begin"],
-    ("V", 0, 3): ["proj 0 third", "fc1 0 third"],
-    ("V", 0, 4): ["qkv 1 second", "fc1 1 begin"],
-    ("F", 0, None): ["proj 0 finish", "fc1 0 finish"],
-    ("F", 0, 1): ["fc2 0 third", "fc2 1 begin"],
-    ("G", 0, None): ["fc2 0 finish"],
-    ("G", 0, 0): ["qkv 1 third"],
-    ("G", 0, 3): ["proj 1 second", "fc1 1 second"],
-    ("P", 1, None): ["qkv 1 finish"],
-    ("P", 1, 3): ["fc2 1 second"],
-    ("H", 1, 3): ["proj 1 third", "fc1 1 third"],
-    ("V", 1, 3): ["fc2 1 third"],
-    ("F", 1, None): ["proj 1 finish", "fc1 1 finish"],
-    ("G", 1, None): ["fc2 1 finish"],
+    (P_, 0, 3): [(QKV_C, 0, SECOND)],
+    (H_, 0, 2): [(PROJ, 0, SECOND), (FC1, 0, SECOND), (QKV_C, 0, THIRD)],
+    (H_, 0, 3): [(QKV, 1, BEGIN)],
+    (PC_, 0, None): [(QKV_C, 0, FINISH)],
+    (V_, 0, 0): [(FC2, 0, SECOND), (PROJ, 1, BEGIN)],
+    (V_, 0, 3): [(FC1, 1, BEGIN)],
+    (V_, 0, 4): [(PROJ, 0, THIRD), (FC1, 0, THIRD), (QKV, 1, SECOND)],
+    (F_, 0, None): [(PROJ, 0, FINISH), (FC1, 0, FINISH), (SAVE, 0, BEGIN)],
+    (F_, 0, 1): [(FC2, 0, THIRD), (FC2, 1, BEGIN)],
+    (G_, 0, None): [(FC2, 0, FINISH)],
+    (G_, 0, 1): [(QKV, 1, THIRD)],
+    (P_, 1, None): [(QKV, 1, FINISH), (PROJ, 1, SECOND), (FC1, 1, SECOND)],
+    (P_, 1, 3): [(SAVE, 0, FINISH)],
+    (H_, 1, 1): [(FC2, 1, SECOND)],
+    (V_, 1, 1): [(PROJ, 1, THIRD), (FC1, 1, THIRD)],
+    (V_, 1, 4): [(FC2, 1, THIRD)],
+    (F_, 1, None): [(PROJ, 1, FINISH), (FC1, 1, FINISH)],
+    (G_, 1, None): [(FC2, 1, FINISH)],
 }
 SUM_MOVES = {
-    ("B2", 1, None): ["fc2 1 begin"],
-    ("BS", 1, None): ["fc1 1 begin", "proj 1 begin"],
-    ("BH", 1, 0): ["fc2 1 second", "fc1 1 second", "proj 1 second"],
-    ("BR", 1, None): ["qkv_r 1 begin", "fc2 1 third"],
-    ("BV", 1, 0): ["qkv_r 1 second"],
-    ("BV", 1, 2): ["fc1 1 third", "proj 1 third"],
-    ("BV", 1, 4): ["qkv_r 1 third"],
-    ("BC", 1, None): ["qkv_c 1 begin"],
-    ("BM", 1, 0): ["fc2 1 fourth"],
-    ("BM", 1, 2): ["qkv_c 1 second"],
-    ("BX", 1, None): ["vec 1 begin"],
-    ("BF", 0, 1): ["fc1 1 fourth", "proj 1 fourth", "vec 1 second"],
-    ("BF", 0, 3): ["fc2 1 finish", "qkv_r 1 fourth", "qkv_c 1 third"],
-    ("B2", 0, None): ["fc2 0 begin"],
-    ("BS", 0, None): ["fc1 0 begin", "proj 0 begin"],
-    ("BH", 0, 0): ["fc2 0 second", "fc1 0 second", "proj 0 second", "vec 1 third"],
-    ("BH", 0, 1): ["fc1 1 finish", "proj 1 finish", "qkv_r 1 finish"],
-    ("BH", 0, 2): ["qkv_c 1 fourth", "vec 1 fourth"],
-    ("BR", 0, None): ["qkv_r 0 begin", "fc2 0 third"],
-    ("BV", 0, 0): ["qkv_r 0 second"],
-    ("BV", 0, 2): ["fc1 0 third", "proj 0 third"],
-    ("BV", 0, 3): ["qkv_c 1 finish", "vec 1 finish"],
-    ("BV", 0, 4): ["qkv_r 0 third"],
-    ("BC", 0, None): ["qkv_c 0 begin"],
-    ("BM", 0, 0): ["fc2 0 fourth"],
-    ("BM", 0, 2): ["qkv_c 0 second"],
-    ("BX", 0, None): ["vec 0 begin"],
+    (B2_, 1, None): [(FC2, 1, BEGIN)],
+    (BS_, 1, None): [(FC1, 1, BEGIN), (PROJ, 1, BEGIN)],
+    (BH_, 1, 0): [(FC2, 1, SECOND)],
+    (BH_, 1, 1): [(FC1, 1, SECOND), (PROJ, 1, SECOND)],
+    (BR_, 1, None): [(QKV_R, 1, BEGIN), (LOAD_R, 0, BEGIN)],
+    (BV_, 1, 0): [(FC2, 1, THIRD)],
+    (BV_, 1, 1): [(QKV_R, 1, SECOND)],
+    (BV_, 1, 3): [(FC1, 1, THIRD), (PROJ, 1, THIRD)],
+    (BV_, 1, 5): [(QKV_R, 1, THIRD)],
+    (BC_, 1, None): [(QKV_C, 1, BEGIN), (LOAD_C, 0, BEGIN)],
+    (BM_, 1, 1): [(FC2, 1, FOURTH)],
+    (BM_, 1, 3): [(QKV_C, 1, SECOND)],
+    (BX_, 1, None): [(VEC, 1, BEGIN)],
+    (BF_, 0, 1): [(VEC, 1, SECOND)],
+    (BF_, 0, 3): [(QKV_C, 1, THIRD), (FC1, 1, FOURTH), (PROJ, 1, FOURTH), (QKV_R, 1, FOURTH)],
+    (B2_, 0, None): [(FC2, 0, BEGIN), (FC2, 1, FINISH)],
+    (BS_, 0, None): [(FC1, 0, BEGIN), (PROJ, 0, BEGIN), (LOAD_R, 0, FINISH), (VEC, 1, THIRD)],
+    (BH_, 0, 0): [(FC2, 0, SECOND)],
+    (BH_, 0, 1): [
+        (FC1, 0, SECOND), (PROJ, 0, SECOND), (FC1, 1, FINISH), (PROJ, 1, FINISH),
+        (QKV_R, 1, FINISH),
+    ],
+    (BH_, 0, 3): [(QKV_C, 1, FOURTH), (VEC, 1, FOURTH)],
+    (BR_, 0, None): [(QKV_R, 0, BEGIN), (LOAD_C, 0, FINISH)],
+    (BV_, 0, 0): [(FC2, 0, THIRD)],
+    (BV_, 0, 1): [(QKV_R, 0, SECOND)],
+    (BV_, 0, 2): [(QKV_C, 1, FINISH), (VEC, 1, FINISH)],
+    (BV_, 0, 3): [(FC1, 0, THIRD), (PROJ, 0, THIRD)],
+    (BV_, 0, 5): [(QKV_R, 0, THIRD)],
+    (BC_, 0, None): [(QKV_C, 0, BEGIN)],
+    (BM_, 0, 1): [(FC2, 0, FOURTH), (QKV_C, 0, SECOND)],
+    (BX_, 0, None): [(VEC, 0, BEGIN)],
 }
 LAST_MOVES = [
-    ("vec", 0, "second"), ("fc1", 0, "fourth"), ("proj", 0, "fourth"), ("qkv_c", 0, "third"),
-    ("vec", 0, "third"), ("qkv_r", 0, "fourth"), ("fc2", 0, "finish"), ("fc1", 0, "finish"),
-    ("proj", 0, "finish"), ("qkv_r", 0, "finish"), ("qkv_c", 0, "fourth"), ("vec", 0, "fourth"),
-    ("qkv_c", 0, "finish"), ("vec", 0, "finish"),
+    (VEC, 0, SECOND), (FC1, 0, FOURTH), (PROJ, 0, FOURTH), (QKV_C, 0, THIRD),
+    (VEC, 0, THIRD), (QKV_R, 0, FOURTH), (FC2, 0, FINISH), (FC1, 0, FINISH),
+    (PROJ, 0, FINISH), (QKV_R, 0, FINISH), (QKV_C, 0, FOURTH), (VEC, 0, FOURTH),
+    (QKV_C, 0, FINISH), (VEC, 0, FINISH),
 ]
+
+
+class Local:
+    def __init__(self, *copies):
+        self.copies = copies
+
+    def begin(self):
+        for copy in self.copies:
+            copy.start()
+
+    def finish(self):
+        for copy in self.copies:
+            copy.wait()
 
 
 class Moves:
@@ -746,16 +824,38 @@
 
     def take(self, moves):
         for move in moves:
-            name, l, verb = move.split()
-            getattr(self.parts[name, int(l)], verb)()
+            name, l, verb = move
+            getattr(self.parts[name, l], VERBS[verb])()
 
     def __call__(self, phase, l, step=None):
         if step is None:
             self.take(self.table.get((phase, l, None), []))
             return
+        start, turn, stride = step
         for (name, block, when), moves in self.table.items():
-            if (name, block) == (phase, l) and when is not None:
-                pl.when(step == when)(functools.partial(self.take, moves))
+            if (name, block) != (phase, l) or when is None or when % stride != turn:
+                continue
+            if start is None:
+                self.take(moves)
+            else:
+                pl.when(start == when // stride)(functools.partial(self.take, moves))
+
+
+def sweep(phase, l, count, body, at):
+    stride = STRIDE.get(phase, 1)
+    if stride == count:
+        for s in range(count):
+            body(s)
+            at(phase, l, (None, s, stride))
+        return
+
+    def steps(i, carry):
+        for turn in range(stride):
+            body(i * stride + turn)
+            at(phase, l, (i, turn, stride))
+        return carry
+
+    lax.fori_loop(0, count // stride, steps, 0)
 
 
 class Gradients:
@@ -772,16 +872,17 @@
     place = (zs, xs, 2)
     d, f = width // shards, hidden // shards
     shapes = {k: pltpu.VMEM(*v) for k, v in SCRATCH.items()}
-    own = dict(qkv=(d, 3 * width), proj=(d, width), fc1=(d, hidden), fc2=(f, width))
+    own = {QKV: (d, 3 * width), PROJ: (d, width), FC1: (d, hidden), FC2: (f, width)}
     for name in MATRICES:
         shapes["full", name] = pltpu.VMEM((layers,) + place + own[name], BF)
-    shapes["full", "vec"] = pltpu.VMEM(place + (layers, d, held), BF)
-    gathers = len(MATRICES) * layers + 1
+    shapes["full", VEC] = pltpu.VMEM(place + (layers, d, held), BF)
+    gathers = len(MATRICES) * layers + 1 + 6
     hops = zs - 1 + xs - 1 + 1
     for name in ("gather send", "gather recv"):
         shapes[name] = pltpu.SemaphoreType.DMA((gathers, hops))
     shapes["gather local"] = pltpu.SemaphoreType.DMA((gathers,))
-    own.update(qkv_r=(d, 3 * width // 2), qkv_c=(d, 3 * width // 2), vec=(d, 128))
+    half = (d, 3 * width // 2)
+    own.update({QKV_R: half, QKV_C: half, VEC: (d, 128)})
     sums = len(SUMMED) * layers
     hops += copies - 1
     for l in range(layers):
@@ -791,7 +892,12 @@
                 shapes["buf", name, l, i] = buf
     for name in ("sum send", "sum recv"):
         shapes[name] = pltpu.SemaphoreType.DMA((sums, hops))
-    shapes["out"] = pltpu.SemaphoreType.DMA((2,))
+    shapes["out"] = pltpu.SemaphoreType.DMA((8 + 6 * layers,))
+    for name in MATRICES:
+        shapes["sum", name] = pltpu.VMEM((layers,) + own[name], F32)
+    shapes["sum", VEC] = pltpu.VMEM((layers, d, held), F32)
+    for name in ("tok", "cot"):
+        shapes[name] = pltpu.VMEM((HP * WP, width), BF)
     return shapes
 
 
@@ -800,91 +906,130 @@
     own = dict(zip(MATRICES, refs[4:8]))
     vec_own = refs[8]
     y_ref, gt_ref = refs[9:11]
-    outs = dict(zip(MATRICES + ("vec",), refs[11:16]))
-    s = dict(zip(names, refs[16:]))
+    outs = dict(zip(MATRICES + (VEC,), refs[11:16]))
+    p_r_ref, p_c_ref = refs[16:18]
+    s = dict(zip(names, refs[18:]))
     r = Refs(SCRATCH, [s[k] for k in SCRATCH])
-    layers = own["qkv"].shape[0]
+    layers = own[QKV].shape[0]
     grid = Grid(shards, copies)
     grid.signal()
     h, w = h_ref[0], w_ref[0]
 
     sems = [s["gather send"], s["gather recv"], s["gather local"]]
-    order = [(name, l) for l in range(layers) for name in MATRICES]
+    order = [(name, l) for l in range(layers) for name in MATRICES][1:]
     gathers = {
         (name, l): Gather(grid, own[name].at[l], s["full", name].at[l], sems, i)
         for i, (name, l) in enumerate(order)
     }
-    gathers["vec", 0] = Gather(grid, vec_own, s["full", "vec"], sems, len(order))
+    gathers[VEC, 0] = Gather(grid, vec_own, s["full", VEC], sems, len(order))
+    for half, name in enumerate((QKV_R, QKV_C)):
+        parts = []
+        for i in range(3):
+            lanes = lanes_of(i, half)
+            full = s["full", QKV].at[0, :, :, :, :, lanes]
+            row = len(order) + 1 + 3 * half + i
+            parts.append(Gather(grid, own[QKV].at[0, :, lanes], full, sems, row))
+        gathers[name, 0] = Group(parts)
     wt = Weights({name: s["full", name] for name in MATRICES})
-    wt = Weights({name: s["full", name] for name in MATRICES})
-
+
+    def local(src, dst, i):
+        return pltpu.make_async_copy(src, dst, s["out"].at[i])
+
+    tok_copy, cot_copy = local(tok, s["tok"], 6), local(cot, s["cot"], 7)
+    tok_copy.start()
+    cot_copy.start()
     grid.wait()
-    first = [gathers["qkv", 0], gathers["vec", 0]]
+    first = [gathers[QKV_R, 0], gathers[VEC, 0]]
     for one in first:
         one.begin()
     for stack in (r.qs_r, r.qs_c):
         stack[...] = jnp.where(iota(stack.shape, 1) == 128, 1.0, 0.0).astype(BF)
-    for stack in (r.ds_r, r.ds_c):
+    for stack in (r.dt_r, r.dt_c):
         stack[...] = jnp.zeros_like(stack)
     r.gv[...] = jnp.zeros_like(r.gv)
-    pad_groups(tok, r.x.at[0])
-    pad_groups(cot, r.g)
+    tok_copy.wait()
+    pad_groups(s["tok"], r.x.at[0])
+    cot_copy.wait()
+    pad_groups(s["cot"], r.g)
     for one in first:
         one.second()
-    gathers["proj", 0].begin()
-    gathers["fc1", 0].begin()
+    gathers[QKV_C, 0].begin()
     for one in first:
         one.third()
-    gathers["fc2", 0].begin()
+    gathers[PROJ, 0].begin()
+    gathers[FC1, 0].begin()
     for one in first:
         one.finish()
+    gathers[FC2, 0].begin()
     for l in range(layers):
-        value = s["full", "vec"][:, :, :, l].astype(F32)
+        value = s["full", VEC][:, :, :, l].astype(F32)
         value = value.reshape(-1, value.shape[-1])
         value = jnp.concatenate([value, jnp.zeros((value.shape[0], 128 - value.shape[1]), F32)], axis=1)
         r.vec[l] = value.T
 
-    at = Moves(GATHER_MOVES, gathers)
+    save = Local(local(r.p_r, p_r_ref, 2), local(r.p_c, p_c_ref, 3))
+    at = Moves(GATHER_MOVES, {**gathers, (SAVE, 0): save})
     for l in range(layers):
         forward_layer(l, h, w, wt, r, at)
-    y_copy = pltpu.make_async_copy(r.x.at[layers], y_ref, s["out"].at[0])
-    y_copy.start()
 
     sums = {}
     for l in range(layers):
         for i, name in enumerate(SUMMED):
-            if name in ("qkv_r", "qkv_c"):
-                out = (outs["qkv"].at[l], 0 if name == "qkv_r" else 1)
-            else:
-                out = (outs[name].at[l], None)
-            bufs = [s["buf", name, l, j] for j in range(7)]
+            whole = QKV if name in (QKV_R, QKV_C) else name
+            held = s["sum", whole].at[l]
+            half = {QKV_R: 0, QKV_C: 1}.get(name)
+            leave = None if half == 0 else local(held, outs[whole].at[l], 8 + l * 6 + i)
+            out = (held, half, leave)
+            bufs = [s["buf", name, l, j] for j in range(4)]
             row = l * len(SUMMED) + i
             sums[name, l] = Reduce(
                 grid, s["part", name, l], bufs, out, [s["sum send"], s["sum recv"]], row
             )
     gradients = Gradients({(name, l): s["part", name, l] for l in range(layers) for name in SUMMED})
 
-    at = Moves(SUM_MOVES, sums)
+    load_r = Local(local(p_r_ref, r.p_r, 4))
+    load_c = Local(local(p_c_ref, r.p_c, 5))
+    at = Moves(SUM_MOVES, {**sums, (LOAD_R, 0): load_r, (LOAD_C, 0): load_c})
     for l in reversed(range(layers)):
         backward_layer(l, h, w, wt, r, gradients, at)
-    g_copy = pltpu.make_async_copy(r.g, gt_ref, s["out"].at[1])
+    flat = pl.ds(0, HP * WP)
+    drop_groups(r.g, r.g)
+    g_copy = local(r.g.at[flat], gt_ref, 1)
     g_copy.start()
-    for name, l, move in LAST_MOVES:
-        getattr(sums[name, l], move)()
+    at.take(LAST_MOVES[:1])
+    drop_groups(r.x.at[layers], r.x.at[layers])
+    y_copy = local(r.x.at[layers, flat], y_ref, 0)
+    y_copy.start()
+    at.take(LAST_MOVES[1:])
     for one in list(gathers.values()) + list(sums.values()):
         one.drain()
     y_copy.wait()
     g_copy.wait()
 
 
+PIECES = 3
+
+
 def finish_kernel(count, *refs):
-    y, g = refs[:2]
-    drop_groups(y, refs[count])
-    drop_groups(g, refs[count + 1])
-    for i in range(2, count - 1):
-        refs[count + i][...] = refs[i][...]
-    vec, out = refs[count - 1], refs[2 * count - 1]
-    out[...] = vec[:, :, 0 : out.shape[2]]
+    src, dst, held = refs[:count], refs[count : 2 * count], refs[2 * count : 3 * count]
+    sem_in, sem_out = refs[3 * count :]
+    moves = []
+    for i in range(count):
+        pieces = PIECES if i < 2 else 1
+        size = src[i].shape[0] // pieces
+        for j in range(pieces):
+            part = pl.ds(j * size, size)
+            place = (i, j)
+            first = pltpu.make_async_copy(src[i].at[part], held[i].at[part], sem_in.at[place])
+            last = pltpu.make_async_copy(held[i].at[part], dst[i].at[part], sem_out.at[place])
+            moves.append((first, last))
+    for first, _ in moves:
+        first.start()
+    for first, last in moves:
+        first.wait()
+        last.start()
+    for _, last in moves:
+        last.wait()
 
 
 def shards_step(shards, copies, tokens, heights, widths, w_qkv, w_proj, w_fc1, w_fc2, vectors, cotangent):
@@ -896,14 +1041,15 @@
     turned = vectors.transpose(0, 2, 1)
     scratch = plan(shards, copies, layers, width, hidden, turned.shape[2])
     matrices = [w_qkv, w_proj, w_fc1, w_fc2]
-    results = [jax.ShapeDtypeStruct((ROWS, width), F32)] * 2
+    results = [jax.ShapeDtypeStruct((count, width), F32)] * 2
     results += [jax.ShapeDtypeStruct(m.shape, F32) for m in matrices]
-    results += [jax.ShapeDtypeStruct((layers, width // shards, 128), F32)]
-    raw = pl.pallas_call(
+    results += [jax.ShapeDtypeStruct(turned.shape, F32)]
+    results += [jax.ShapeDtypeStruct(*SCRATCH[k]) for k in KEPT]
+    *raw, _, _ = pl.pallas_call(
         functools.partial(step_kernel, shards, copies, list(scratch)),
         out_shape=results,
-        in_specs=[smem, smem, vmem, vmem] + [vmem] * 5,
-        out_specs=[hbm, hbm] + [vmem] * 5,
+        in_specs=[smem, smem, hbm, hbm] + [hbm] * 5,
+        out_specs=[hbm] * 9,
         scratch_shapes=list(scratch.values()),
         compiler_params=pltpu.CompilerParams(
             collective_id=0, has_side_effects=True, vmem_limit_bytes=67043328
@@ -911,11 +1057,13 @@
     )(heights, widths, tokens, cotangent, *matrices, turned)
     final = [jax.ShapeDtypeStruct((count, width), F32)] * 2
     final += [jax.ShapeDtypeStruct(m.shape, F32) for m in matrices + [turned]]
+    sems = pltpu.SemaphoreType.DMA((len(raw), PIECES))
     *arrays, vec = pl.pallas_call(
         functools.partial(finish_kernel, len(raw)),
         out_shape=final,
-        in_specs=[vmem] * len(raw),
-        out_specs=[vmem] * len(raw),
+        in_specs=[hbm] * len(raw),
+        out_specs=[hbm] * len(raw),
+        scratch_shapes=[pltpu.VMEM(f.shape, F32) for f in final] + [sems, sems],
         compiler_params=pltpu.CompilerParams(vmem_limit_bytes=67043328),
     )(*raw)
     return (*arrays, vec.transpose(0, 2, 1))

time: 116 us -> 106 us (0.914)
  Pallas kernels: 114 us -> 104 us
    pallas_call x1, Pallas kernels: 110 us -> 101 us  [shards_step(): pl.pallas_call(functools.partial(step_kernel, shards, copies, list(scratc...]
where the time goes in v4:
time: 106 us
  Pallas kernels  104 us (98%)
  between operations  2.11 us (2%)
    pallas_call x1, Pallas kernels, shards_step(): pl.pallas_call(functools.partial(step_kernel, shards, copies, list(scratc...  101 us
    pallas_call x1, Pallas kernels, shards_step(): pl.pallas_call(functools.partial(finish_kernel, len(raw)), out_shape=fina...  2.91 us

profile of v4, /device:TPU:0, one launch (start us, length us, event | category | flops | bytes accessed | tf_op | source)
XLA Modules:
  0.0 106.0 jit_solution(2534754253830537615)
XLA Ops:
  1.9 101.0 %shard_map.144 = (f32[1176,256]{1,0:T(8,128)}, f32[1176,256]{1,0:T(8,128)}, f32[2,16,768]{2,1,0:T(8,128)}, f32[2,16,256]{2,1,0:T(8,128)}, f32[2,16,1024]{2,1,0:T...) custom-call(s32[1]{0:T(128)S(6)} %copy.16.refs_0_, ...), custom_call_target="tpu_custom_call" | custom-call | tf_op jit(solution)/shard_map/pallas_call | solution.py:1048
  102.9 2.9 %shard_map.145 = (f32[1176,256]{1,0:T(8,128)}, f32[1176,256]{1,0:T(8,128)}, f32[2,16,768]{2,1,0:T(8,128)}, f32[2,16,256]{2,1,0:T(8,128)}, f32[2,16,1024]{2,1,0:T...) custom-call(f32[1176,256]{1,0:T(8,128)} %get-tuple-element.21.refs_0_, f32[1176,256]{1,0:T(8,128)} %get-tuple-element.22.refs_1_, ...), custom_call_target="tpu_custom_call" | custom-call | tf_op jit(solution)/shard_map/pallas_call | solution.py:1061

commit v5 on v4

--- a/solution.py
+++ b/solution.py
@@ -458,8 +458,9 @@
         self.x = lax.rem(chip, self.xs)
         self.z = lax.div(chip, self.xs)
 
-    def at(self, z, x, core):
-        return {"fsdp": (z * self.xs + x) * 2 + core, "rep": self.rep}
+    def at(self, z, x, core, rep=None):
+        index = (z * self.xs + x) * 2 + core
+        return {"fsdp": index, "rep": self.rep if rep is None else rep}
 
     def z_peers(self):
         return [(d, lax.rem(self.z + d, self.zs)) for d in range(1, self.zs)]
@@ -479,17 +480,16 @@
     def sibling(self):
         return self.at(self.z, self.x, 1 - self.core)
 
-    def rep_device(self, rep):
-        index = (self.z * self.xs + self.x) * 2 + self.core
-        return {"fsdp": index, "rep": rep}
-
-    def steps(self):
-        return self.zs - 1 + self.xs - 1 + 1
-
     def peers(self):
-        devices = [self.z_device(z) for _, z in self.z_peers()]
-        devices += [self.x_device(x) for _, x in self.x_peers()] + [self.sibling()]
-        return devices + [self.rep_device(rep) for _, rep in self.rep_peers()]
+        devices = [self.sibling()]
+        for dz in range(self.zs):
+            for dx in range(self.xs):
+                for dr in range(self.copies):
+                    if dz + dx + dr:
+                        z, x = lax.rem(self.z + dz, self.zs), lax.rem(self.x + dx, self.xs)
+                        rep = lax.rem(self.rep + dr, self.copies)
+                        devices.append(self.at(z, x, self.core, rep))
+        return devices
 
     def signal(self):
         for device in self.peers():
@@ -508,138 +508,157 @@
     )
 
 
+def take_all(ref, sem):
+    pltpu.make_async_copy(ref, ref, sem).wait()
+
+
 class Gather:
-    def __init__(self, grid, own, full, sems, row):
-        self.grid, self.own, self.full = grid, own, full
+    def __init__(self, grid, parts, like, sems, row):
+        self.grid, self.like = grid, like
+        g = grid
         send, recv, local = sems
-        g = grid
-        mine = full.at[g.z, g.x, g.core]
-        self.keep = pltpu.make_async_copy(own, mine, local.at[row])
-        self.along_z = [
-            remote(own, mine, send.at[row, d - 1], recv.at[row, d - 1], g.z_device(z))
-            for d, z in g.z_peers()
-        ]
-        base = g.zs - 2
-        lane = full.at[:, g.x, g.core]
-        self.along_x = [
-            remote(lane, lane, send.at[row, base + d], recv.at[row, base + d], g.x_device(x))
-            for d, x in g.x_peers()
-        ]
-        last = g.zs - 1 + g.xs - 1
-        plane = full.at[:, :, g.core]
-        self.across = remote(plane, plane, send.at[row, last], recv.at[row, last], g.sibling())
+        self.send, self.local = send.at[row], local.at[row]
+        self.recv = [recv.at[row, i] for i in range(3)]
+        self.keep, self.along_z, self.along_x, self.across = [], [], [], []
+        for own, full in parts:
+            mine = full.at[g.z, g.x, g.core]
+            line, plane = full.at[:, g.x, g.core], full.at[:, :, g.core]
+            self.keep.append(pltpu.make_async_copy(own, mine, self.local))
+            for _, z in g.z_peers():
+                self.along_z.append(remote(own, mine, self.send, self.recv[0], g.z_device(z)))
+            for _, x in g.x_peers():
+                self.along_x.append(remote(line, line, self.send, self.recv[1], g.x_device(x)))
+            self.across.append(remote(plane, plane, self.send, self.recv[2], g.sibling()))
+
+    def start(self, copies):
+        for copy in copies:
+            copy.start()
+
+    def taken(self, phase, ref):
+        take_all(ref, self.recv[phase])
+        take_all(ref, self.send)
 
     def begin(self):
-        self.keep.start()
-        for copy in self.along_z:
-            copy.start()
+        self.start(self.keep)
+        self.start(self.along_z)
 
     def second(self):
-        self.keep.wait()
-        for copy in self.along_z:
-            copy.wait_recv()
-        for copy in self.along_x:
-            copy.start()
+        g = self.grid
+        take_all(self.like.at[0, 0, 0], self.local)
+        self.taken(0, self.like.at[0 : g.zs - 1, g.x, g.core])
+        self.start(self.along_x)
 
     def third(self):
-        for copy in self.along_x:
-            copy.wait_recv()
-        self.across.start()
+        g = self.grid
+        self.taken(1, self.like.at[:, 0 : g.xs - 1, g.core])
+        self.start(self.across)
 
     def finish(self):
-        self.across.wait_recv()
-
-    def drain(self):
-        for copy in self.along_z + self.along_x + [self.across]:
-            copy.wait_send()
-
-
-class Group:
-    def __init__(self, parts):
-        self.parts = parts
-
-    def each(self, verb):
-        for part in self.parts:
-            getattr(part, verb)()
-
-    def begin(self):
-        self.each(VERBS[BEGIN])
-
-    def second(self):
-        self.each(VERBS[SECOND])
-
-    def third(self):
-        self.each(VERBS[THIRD])
-
-    def finish(self):
-        self.each(VERBS[FINISH])
-
-    def drain(self):
-        for part in self.parts:
-            part.drain()
+        self.taken(2, self.like.at[:, :, self.grid.core])
 
 
 class Reduce:
-    def __init__(self, grid, part, bufs, out, sems, row):
-        self.grid, self.part, self.out = grid, part, out
+    def __init__(self, grid, part, bufs, out, sems, row, wide):
+        self.grid, self.part, self.out, self.wide = grid, part, out, wide
         send, recv = sems
         g = grid
-        self.from_sibling, self.from_x, self.from_z, self.from_rep = bufs
-        self.chip, self.line, self.own = self.from_sibling, self.from_x.at[0], self.from_z.at[0]
-        self.across = remote(
-            part.at[:, :, 1 - g.core], self.from_sibling, send.at[row, 0], recv.at[row, 0], g.sibling()
-        )
-        self.along_x = [
-            remote(self.chip.at[:, x], self.from_x.at[d - 1], send.at[row, d], recv.at[row, d], g.x_device(x))
-            for d, x in g.x_peers()
+        self.send = send.at[row]
+        self.recv = [recv.at[row, i] for i in range(4)]
+        self.chip, self.last = bufs[0], bufs[-1]
+        self.across = [
+            remote(part.at[:, :, 1 - g.core], self.chip, self.send, self.recv[0], g.sibling())
         ]
-        base = g.xs - 1
-        self.along_z = [
-            remote(self.line.at[z], self.from_z.at[d - 1], send.at[row, base + d], recv.at[row, base + d], g.z_device(z))
-            for d, z in g.z_peers()
-        ]
-        base += g.zs - 1
-        self.along_rep = [
-            remote(self.own, self.from_rep.at[d - 1], send.at[row, base + d], recv.at[row, base + d], g.rep_device(rep))
-            for d, rep in g.rep_peers()
-        ]
+        self.along_x, self.along_z, self.along_rep = [], [], []
+        if wide < 2:
+            self.from_x = bufs[1]
+            self.line = self.from_x.at[0]
+            for d, x in g.x_peers():
+                here = self.from_x.at[d - 1]
+                device = g.x_device(x)
+                self.along_x.append(remote(self.chip.at[:, x], here, self.send, self.recv[1], device))
+        if wide:
+            for dz, dx, dr in self.steps():
+                z, to = lax.rem(g.z + dz, g.zs), lax.rem(g.rep + dr, g.copies)
+                x = lax.rem(g.x + dx, g.xs)
+                source = self.line.at[z] if wide == 1 else self.chip.at[z, x]
+                if dz + dx + dr:
+                    here = self.last.at[self.slot(dz, dx, dr)]
+                    device = g.at(z, x, g.core, to)
+                    self.along_rep.append(remote(source, here, self.send, self.recv[3], device))
+            return
+        self.from_z = bufs[2]
+        self.own = self.from_z.at[0]
+        for d, z in g.z_peers():
+            self.along_z.append(
+                remote(self.line.at[z], self.from_z.at[d - 1], self.send, self.recv[2], g.z_device(z))
+            )
+        for d, to in g.rep_peers():
+            device = g.at(g.z, g.x, g.core, to)
+            self.along_rep.append(remote(self.own, self.last.at[d], self.send, self.recv[3], device))
+
+    def steps(self):
+        g = self.grid
+        zs, xs = (g.zs if self.wide else 1), (g.xs if self.wide == 2 else 1)
+        return [(a, b, c) for a in range(zs) for b in range(xs) for c in range(g.copies)]
+
+    def slot(self, dz, dx, dr):
+        g = self.grid
+        return (dz * (g.xs if self.wide == 2 else 1) + dx) * g.copies + dr
+
+    def start(self, copies):
+        for copy in copies:
+            copy.start()
+
+    def taken(self, phase, ref):
+        take_all(ref, self.recv[phase])
+        take_all(ref, self.send)
 
     def begin(self):
-        self.across.start()
+        self.start(self.across)
 
     def second(self):
-        self.across.wait_recv()
+        self.taken(0, self.chip)
         mine = self.part[:, :, self.grid.core].astype(F32)
         self.chip[...] = (mine + self.chip[...].astype(F32)).astype(BF)
-        for copy in self.along_x:
-            copy.start()
+        if self.wide == 2:
+            self.last[0] = self.chip[self.grid.z, self.grid.x]
+            self.start(self.along_rep)
+        else:
+            self.start(self.along_x)
 
     def third(self):
-        for copy in self.along_x:
-            copy.wait_recv()
-        total = self.chip[:, self.grid.x].astype(F32)
-        for d, _ in self.grid.x_peers():
+        g = self.grid
+        self.taken(1, self.from_x)
+        total = self.chip[:, g.x].astype(F32)
+        for d, _ in g.x_peers():
             total = total + self.from_x[d - 1].astype(F32)
         self.line[...] = total.astype(BF)
-        for copy in self.along_z:
-            copy.start()
+        if self.wide:
+            self.last[0] = self.line[g.z]
+            self.start(self.along_rep)
+        else:
+            self.start(self.along_z)
 
     def fourth(self):
-        for copy in self.along_z:
-            copy.wait_recv()
-        total = self.line[self.grid.z].astype(F32)
-        for d, _ in self.grid.z_peers():
+        g = self.grid
+        self.taken(2, self.from_z)
+        total = self.line[g.z].astype(F32)
+        for d, _ in g.z_peers():
             total = total + self.from_z[d - 1].astype(F32)
         self.own[...] = total.astype(BF)
-        for copy in self.along_rep:
-            copy.start()
+        self.last[0] = self.own[...]
+        self.start(self.along_rep)
 
     def finish(self):
-        for copy in self.along_rep:
-            copy.wait_recv()
-        total = self.own[...].astype(F32)
-        for d, _ in self.grid.rep_peers():
-            total = total + self.from_rep[d - 1].astype(F32)
+        g = self.grid
+        slots = self.last.shape[0]
+        self.taken(3, self.last.at[1:slots])
+        total = None
+        for z, x, rep in self.steps():
+            dz = lax.rem(g.z - z + g.zs, g.zs) if self.wide else 0
+            dx = lax.rem(g.x - x + g.xs, g.xs) if self.wide == 2 else 0
+            value = self.last[self.slot(dz, dx, lax.rem(g.rep - rep + g.copies, g.copies))]
+            total = value.astype(F32) if total is None else total + value.astype(F32)
         held, half, self.leave = self.out
         if half is None:
             held[...] = total[:, 0 : held.shape[1]]
@@ -650,14 +669,17 @@
             self.leave.start()
 
     def drain(self):
-        for copy in [self.across] + self.along_x + self.along_z + self.along_rep:
-            copy.wait_send()
         if self.leave is not None:
             self.leave.wait()
 
 
-def reduce_bufs(zs, xs, copies, shape):
-    dims = [(zs, xs), (xs - 1, zs), (zs - 1,), (copies - 1,)]
+def reduce_bufs(zs, xs, copies, shape, wide):
+    dims = [(zs, xs)]
+    if wide < 2:
+        dims.append((xs - 1, zs))
+    if wide == 0:
+        dims.append((zs - 1,))
+    dims.append((copies * (1, zs, zs * xs)[wide],))
     return [pltpu.VMEM(d + tuple(shape), BF) for d in dims]
 
 
@@ -798,11 +820,11 @@
     (BX_, 0, None): [(VEC, 0, BEGIN)],
 }
 LAST_MOVES = [
-    (VEC, 0, SECOND), (FC1, 0, FOURTH), (PROJ, 0, FOURTH), (QKV_C, 0, THIRD),
-    (VEC, 0, THIRD), (QKV_R, 0, FOURTH), (FC2, 0, FINISH), (FC1, 0, FINISH),
-    (PROJ, 0, FINISH), (QKV_R, 0, FINISH), (QKV_C, 0, FOURTH), (VEC, 0, FOURTH),
-    (QKV_C, 0, FINISH), (VEC, 0, FINISH),
+    (VEC, 0, SECOND), (QKV_C, 0, THIRD), (QKV_R, 0, FOURTH), (FC1, 0, FOURTH), (PROJ, 0, FOURTH),
+    (FC2, 0, FINISH), (QKV_R, 0, FINISH), (FC1, 0, FINISH), (PROJ, 0, FINISH),
+    (VEC, 0, FINISH), (QKV_C, 0, FINISH),
 ]
+WIDE = {(QKV_C, 0): 1, (VEC, 0): 2}
 
 
 class Local:
@@ -876,22 +898,20 @@
     for name in MATRICES:
         shapes["full", name] = pltpu.VMEM((layers,) + place + own[name], BF)
     shapes["full", VEC] = pltpu.VMEM(place + (layers, d, held), BF)
-    gathers = len(MATRICES) * layers + 1 + 6
-    hops = zs - 1 + xs - 1 + 1
-    for name in ("gather send", "gather recv"):
-        shapes[name] = pltpu.SemaphoreType.DMA((gathers, hops))
+    gathers = len(MATRICES) * layers + 2
+    shapes["gather send"] = pltpu.SemaphoreType.DMA((gathers,))
+    shapes["gather recv"] = pltpu.SemaphoreType.DMA((gathers, 3))
     shapes["gather local"] = pltpu.SemaphoreType.DMA((gathers,))
     half = (d, 3 * width // 2)
     own.update({QKV_R: half, QKV_C: half, VEC: (d, 128)})
     sums = len(SUMMED) * layers
-    hops += copies - 1
     for l in range(layers):
         for name in SUMMED:
             shapes["part", name, l] = pltpu.VMEM(place + own[name], BF)
-            for i, buf in enumerate(reduce_bufs(zs, xs, copies, own[name])):
+            for i, buf in enumerate(reduce_bufs(zs, xs, copies, own[name], WIDE.get((name, l), 0))):
                 shapes["buf", name, l, i] = buf
-    for name in ("sum send", "sum recv"):
-        shapes[name] = pltpu.SemaphoreType.DMA((sums, hops))
+    shapes["sum send"] = pltpu.SemaphoreType.DMA((sums,))
+    shapes["sum recv"] = pltpu.SemaphoreType.DMA((sums, 4))
     shapes["out"] = pltpu.SemaphoreType.DMA((8 + 6 * layers,))
     for name in MATRICES:
         shapes["sum", name] = pltpu.VMEM((layers,) + own[name], F32)
@@ -917,19 +937,20 @@
 
     sems = [s["gather send"], s["gather recv"], s["gather local"]]
     order = [(name, l) for l in range(layers) for name in MATRICES][1:]
-    gathers = {
-        (name, l): Gather(grid, own[name].at[l], s["full", name].at[l], sems, i)
-        for i, (name, l) in enumerate(order)
-    }
-    gathers[VEC, 0] = Gather(grid, vec_own, s["full", VEC], sems, len(order))
+    gathers = {}
+    for i, (name, l) in enumerate(order):
+        full = s["full", name].at[l]
+        gathers[name, l] = Gather(grid, [(own[name].at[l], full)], full, sems, i)
+    full = s["full", VEC]
+    gathers[VEC, 0] = Gather(grid, [(vec_own, full)], full, sems, len(order))
+    full = s["full", QKV].at[0]
     for half, name in enumerate((QKV_R, QKV_C)):
         parts = []
         for i in range(3):
             lanes = lanes_of(i, half)
-            full = s["full", QKV].at[0, :, :, :, :, lanes]
-            row = len(order) + 1 + 3 * half + i
-            parts.append(Gather(grid, own[QKV].at[0, :, lanes], full, sems, row))
-        gathers[name, 0] = Group(parts)
+            parts.append((own[QKV].at[0, :, lanes], full.at[:, :, :, :, lanes]))
+        like = full.at[:, :, :, :, 0 : full.shape[-1] // 2]
+        gathers[name, 0] = Gather(grid, parts, like, sems, len(order) + 1 + half)
     wt = Weights({name: s["full", name] for name in MATRICES})
 
     def local(src, dst, i):
@@ -980,10 +1001,11 @@
             half = {QKV_R: 0, QKV_C: 1}.get(name)
             leave = None if half == 0 else local(held, outs[whole].at[l], 8 + l * 6 + i)
             out = (held, half, leave)
-            bufs = [s["buf", name, l, j] for j in range(4)]
+            wide = WIDE.get((name, l), 0)
+            bufs = [s["buf", name, l, j] for j in range(4 - wide)]
             row = l * len(SUMMED) + i
             sums[name, l] = Reduce(
-                grid, s["part", name, l], bufs, out, [s["sum send"], s["sum recv"]], row
+                grid, s["part", name, l], bufs, out, [s["sum send"], s["sum recv"]], row, wide
             )
     gradients = Gradients({(name, l): s["part", name, l] for l in range(layers) for name in SUMMED})
 
@@ -1001,7 +1023,7 @@
     y_copy = local(r.x.at[layers, flat], y_ref, 0)
     y_copy.start()
     at.take(LAST_MOVES[1:])
-    for one in list(gathers.values()) + list(sums.values()):
+    for one in sums.values():
         one.drain()
     y_copy.wait()
     g_copy.wait()
@@ -1012,17 +1034,15 @@
 
 def finish_kernel(count, *refs):
     src, dst, held = refs[:count], refs[count : 2 * count], refs[2 * count : 3 * count]
-    sem_in, sem_out = refs[3 * count :]
+    sems = refs[3 * count]
     moves = []
     for i in range(count):
         pieces = PIECES if i < 2 else 1
         size = src[i].shape[0] // pieces
         for j in range(pieces):
-            part = pl.ds(j * size, size)
-            place = (i, j)
-            first = pltpu.make_async_copy(src[i].at[part], held[i].at[part], sem_in.at[place])
-            last = pltpu.make_async_copy(held[i].at[part], dst[i].at[part], sem_out.at[place])
-            moves.append((first, last))
+            part, sem = pl.ds(j * size, size), sems.at[len(moves)]
+            first = pltpu.make_async_copy(src[i].at[part], held[i].at[part], sem)
+            moves.append((first, pltpu.make_async_copy(held[i].at[part], dst[i].at[part], sem)))
     for first, _ in moves:
         first.start()
     for first, last in moves:
@@ -1057,13 +1077,13 @@
     )(heights, widths, tokens, cotangent, *matrices, turned)
     final = [jax.ShapeDtypeStruct((count, width), F32)] * 2
     final += [jax.ShapeDtypeStruct(m.shape, F32) for m in matrices + [turned]]
-    sems = pltpu.SemaphoreType.DMA((len(raw), PIECES))
+    sems = pltpu.SemaphoreType.DMA((2 * PIECES + len(raw) - 2,))
     *arrays, vec = pl.pallas_call(
         functools.partial(finish_kernel, len(raw)),
         out_shape=final,
         in_specs=[hbm] * len(raw),
         out_specs=[hbm] * len(raw),
-        scratch_shapes=[pltpu.VMEM(f.shape, F32) for f in final] + [sems, sems],
+        scratch_shapes=[pltpu.VMEM(f.shape, F32) for f in final] + [sems],
         compiler_params=pltpu.CompilerParams(vmem_limit_bytes=67043328),
     )(*raw)
     return (*arrays, vec.transpose(0, 2, 1))

time: 106 us -> 103 us (0.972)
  Pallas kernels: 104 us -> 100 us
    pallas_call x1, Pallas kernels: 101 us -> 97.8 us  [shards_step(): pl.pallas_call(functools.partial(step_kernel, shards, copies, list(scratc...]
where the time goes in v5:
time: 103 us
  Pallas kernels  100 us (97%)
  between operations  2.11 us (2%)
    pallas_call x1, Pallas kernels, shards_step(): pl.pallas_call(functools.partial(step_kernel, shards, copies, list(scratc...  97.8 us
    pallas_call x1, Pallas kernels, shards_step(): pl.pallas_call(functools.partial(finish_kernel, len(raw)), out_shape=fina...  2.63 us

profile of v5, /device:TPU:0, one launch (start us, length us, event | category | flops | bytes accessed | tf_op | source)
XLA Modules:
  0.0 102.6 jit_solution(14476865408842377121)
XLA Ops:
  1.9 97.8 %shard_map.144 = (f32[1176,256]{1,0:T(8,128)}, f32[1176,256]{1,0:T(8,128)}, f32[2,16,768]{2,1,0:T(8,128)}, f32[2,16,256]{2,1,0:T(8,128)}, f32[2,16,1024]{2,1,0:T...) custom-call(s32[1]{0:T(128)S(6)} %copy.16.refs_0_, ...), custom_call_target="tpu_custom_call" | custom-call | tf_op jit(solution)/shard_map/pallas_call | solution.py:1068
  99.8 2.6 %shard_map.145 = (f32[1176,256]{1,0:T(8,128)}, f32[1176,256]{1,0:T(8,128)}, f32[2,16,768]{2,1,0:T(8,128)}, f32[2,16,256]{2,1,0:T(8,128)}, f32[2,16,1024]{2,1,0:T...) custom-call(f32[1176,256]{1,0:T(8,128)} %get-tuple-element.21.refs_0_, f32[1176,256]{1,0:T(8,128)} %get-tuple-element.22.refs_1_, ...), custom_call_target="tpu_custom_call" | custom-call | tf_op jit(solution)/shard_map/pallas_call | solution.py:1081
